TPU v7x, 256 devices: a whole 4x4x8 slice. The times are simulated.
256 devices in a mesh: row: 16 (over z, core), col: 16 (over x, y).
Axes of the slice: x: 4, y: 4, z: 8, core: 2. Of those that a mesh axis runs over, the one named last changes fastest.
Arguments:
- genotypes: int32 [4096, 16384], P(('row', 'col')), may hold values from 0 to 2, as said below
- snp_index: int32 [4096], P(('row', 'col')), may hold values from 0 to 16383, as said below
- freq_table: float32 [16384], replicated, as said below
- prior: float32 [16384, 16384], P('row', 'col'), as said below
- start_vectors: float32 [16384, 20], P('row'), may hold values from -6 to 6
Outputs:
- grm: float32 [16384, 16384], P('row', 'col')
- pcs: float32 [16384, 20], P('col')
- spectrum: float32 [3, 20], replicated
Inputs may be any that keep to these rules, and one draw needn't show every extreme that they name: `genotypes`: genotype dosages 0, 1 or 2. `snp_index`: strictly increasing; entry j lies in 4 * j to 4 * j + 3. `freq_table`: frequencies are multiples of 1/1024 between 52/1024 and 512/1024. `prior`: exactly symmetric; diagonal between 1 and 2, off-diagonal entries small.
All inputs are finite; a program needn't handle non-finite values.
Results may differ from a plain program's by a relative error of at most 0.0075.
Values may be sent and summed in bfloat16 or wider, within the bound.
No kernel may reach another device: no remote copies, remote signals or barrier semaphores. Data moves between devices by JAX's collectives and lax.ppermute only.
A program may use at most 128 MiB of HBM per device.

v0:
```python
import jax
import jax.numpy as jnp
from jax import lax
from jax.experimental import pallas as pl
from jax.experimental.pallas import tpu as pltpu
from jax.sharding import Mesh
from jax.sharding import PartitionSpec as P


S = 16384
M = 4096
K = 20
ROW = ("z", "core")
COL = ("x", "y")
ALL = ("z", "core", "x", "y")
SIZES = (8, 2, 4, 4)
F32 = jnp.float32
BF16 = jnp.bfloat16
VMEM = pl.BlockSpec(memory_space=pltpu.VMEM)
ANY = pl.BlockSpec(memory_space=pl.ANY)
SMEM = pl.BlockSpec(memory_space=pltpu.SMEM)


def place(z, core, x, y):
    return ((z * 2 + core) * 4 + x) * 4 + y


def send(array, target):
    pairs = []
    for z in range(8):
        for core in range(2):
            for x in range(4):
                for y in range(4):
                    pairs.append((place(z, core, x, y), place(*target(z, core, x, y))))
    return lax.ppermute(array, ALL, pairs)


def swap_core(array):
    return send(array, lambda z, core, x, y: (z, 1 - core, x, y))


def ring_z(array):
    return send(array, lambda z, core, x, y: ((z + 1 - 2 * core) % 8, core, x, y))


def first_axis(array, step):
    def target(z, core, x, y):
        return (z, core, (x + step) % 4, y) if core == 0 else (z, core, x, (y + step) % 4)

    return send(array, target)


def second_axis(array, step):
    def target(z, core, x, y):
        return (z, core, (x + step) % 4, y) if core == 1 else (z, core, x, (y + step) % 4)

    return send(array, target)


def standardize_kernel(index, table, genotypes, out, rows, doubled, spread):
    count = genotypes.shape[0]

    @pl.when(pl.program_id(0) == 0)
    def _():
        lane = lax.broadcasted_iota(jnp.int32, (count, 128), 1)
        sub = lax.broadcasted_iota(jnp.int32, (count, 128), 0)
        want = jnp.zeros((count, 128), jnp.int32)
        for j in range(count):
            rows[pl.ds(j, 1), :] = table[pl.ds(index[j] // 128, 1), :]
            want = jnp.where(sub == j, index[j] % 128, want)
        freq = jnp.sum(jnp.where(lane == want, rows[...], 0.0), axis=1, keepdims=True)
        doubled[...] = jnp.broadcast_to(2.0 * freq, (count, 128))
        spread[...] = jnp.broadcast_to(jnp.sqrt(2.0 * freq * (1.0 - freq)), (count, 128))

    blocks = out.shape[0]
    for i in range(blocks):
        value = genotypes[:, 1024 * i : 1024 * (i + 1)].astype(F32) - doubled[:, :1]
        out[i] = (value / spread[:, :1]).astype(BF16)


def standardize(genotypes, snp_index, freq_table):
    snps, _ = genotypes.shape
    return pl.pallas_call(
        standardize_kernel,
        grid_spec=pltpu.PrefetchScalarGridSpec(
            num_scalar_prefetch=1,
            grid=(4,),
            in_specs=[
                pl.BlockSpec((128, 128), lambda i, s: (0, 0)),
                pl.BlockSpec((snps, 4096), lambda i, s: (0, i)),
            ],
            out_specs=pl.BlockSpec((4, snps, 1024), lambda i, s: (i, 0, 0)),
            scratch_shapes=[pltpu.VMEM((snps, 128), F32)] * 3,
        ),
        out_shape=jax.ShapeDtypeStruct((16, snps, 1024), BF16),
        compiler_params=pltpu.CompilerParams(vmem_limit_bytes=8 * 2**20),
        name="standardize",
    )(snp_index, freq_table.reshape(128, 128), genotypes)


def turn_kernel(order, piece, out, stage):
    for j in range(16):
        stage[16 * j : 16 * (j + 1), :] = piece[order[j]]
    out[...] = stage[...].T


def turn(order, piece):
    return pl.pallas_call(
        turn_kernel,
        in_specs=[SMEM, VMEM],
        out_specs=VMEM,
        out_shape=jax.ShapeDtypeStruct((1024, 256), BF16),
        scratch_shapes=[pltpu.VMEM((256, 1024), BF16)],
        compiler_params=pltpu.CompilerParams(vmem_limit_bytes=8 * 2**20),
        name="turn",
    )(order, piece)


def fetch_columns(index, columns, target, sem, first):
    for t in range(2):
        which = index[first + t]
        for j in range(16):
            pltpu.make_async_copy(
                columns[j].at[which], target.at[pl.ds(256 * t + 16 * j, 16)], sem
            ).start()


def tile_a_kernel(index, *refs):
    columns, rows, prior = refs[:16], refs[16:22], refs[22]
    total, ahead, left, stage, prior_sem, left_sem, stage_sem, ahead_sem = refs[23:]
    for i in range(2):
        pltpu.make_async_copy(rows[i], left.at[i], left_sem.at[i]).start()
        fetch_columns(index, columns, stage.at[i], stage_sem.at[i], 2 * i)
    from_prior = pltpu.make_async_copy(prior, total, prior_sem)
    from_prior.start()
    for i in range(2, 6):
        pltpu.make_async_copy(rows[i], left.at[i], left_sem.at[i]).start()
        fetch_columns(index, columns, stage.at[i], stage_sem.at[i], 2 * i)
    for i in range(2):
        fetch_columns(index, columns, ahead.at[pl.ds(512 * i, 512)], ahead_sem.at[i], 12 + 2 * i)
    for group in range(3):
        for i in (2 * group, 2 * group + 1):
            pltpu.make_async_copy(rows[i], left.at[i], left_sem.at[i]).wait()
            pltpu.make_async_copy(stage.at[i], stage.at[i], stage_sem.at[i]).wait()
        if group == 0:
            from_prior.wait()

        def step(n, carry, group=group):
            at = pl.ds(pl.multiple_of(n * 256, 256), 256)
            product = jnp.zeros((1024, 256), F32)
            for i in (2 * group, 2 * group + 1):
                product += jnp.dot(left[i], stage[i, :, at], preferred_element_type=F32)
            total[:, at] += product * (1.0 / M)
            return carry

        lax.fori_loop(0, 4, step, 0)
    for i in range(2):
        part = ahead.at[pl.ds(512 * i, 512)]
        pltpu.make_async_copy(part, part, ahead_sem.at[i]).wait()


def tile_a(index, columns, rows, prior):
    return pl.pallas_call(
        tile_a_kernel,
        in_specs=[SMEM] + [ANY] * 23,
        out_specs=[VMEM] * 2,
        out_shape=[jax.ShapeDtypeStruct((1024, 1024), F32), jax.ShapeDtypeStruct((1024, 1024), BF16)],
        scratch_shapes=[
            pltpu.VMEM((6, 1024, 512), BF16),
            pltpu.VMEM((6, 512, 1024), BF16),
            pltpu.SemaphoreType.DMA,
            pltpu.SemaphoreType.DMA((6,)),
            pltpu.SemaphoreType.DMA((6,)),
            pltpu.SemaphoreType.DMA((2,)),
        ],
        compiler_params=pltpu.CompilerParams(vmem_limit_bytes=32 * 2**20),
        cost_estimate=pl.CostEstimate(flops=6 * 2**30, bytes_accessed=18 * 2**20, transcendentals=0),
        name="tile_a",
    )(index, *columns, *rows, prior)


def tile_b_kernel(partial, ahead, row, start, out, rounded, image, total, out_sem):
    def step(n, carry):
        at = pl.ds(pl.multiple_of(n * 256, 256), 256)
        product = jnp.dot(row[...], ahead[:, at], preferred_element_type=F32)
        value = partial[:, at] + product * (1.0 / M)
        total[:, at] = value
        pltpu.make_async_copy(total.at[:, at], out.at[:, at], out_sem.at[n]).start()
        rounded[:, at] = value.astype(BF16)
        image[:, at] = jnp.dot(start[...], value.astype(BF16), preferred_element_type=F32)
        return carry

    lax.fori_loop(0, 4, step, 0)
    for n in range(4):
        at = pl.ds(n * 256, 256)
        pltpu.make_async_copy(total.at[:, at], out.at[:, at], out_sem.at[n]).wait()


def tile_b(partial, ahead, row, start):
    return pl.pallas_call(
        tile_b_kernel,
        in_specs=[VMEM] * 4,
        out_specs=[ANY, VMEM, VMEM],
        out_shape=[
            jax.ShapeDtypeStruct((1024, 1024), F32),
            jax.ShapeDtypeStruct((1024, 1024), BF16),
            jax.ShapeDtypeStruct((K, 1024), F32),
        ],
        scratch_shapes=[pltpu.VMEM((1024, 1024), F32), pltpu.SemaphoreType.DMA((4,))],
        compiler_params=pltpu.CompilerParams(vmem_limit_bytes=20 * 2**20),
        cost_estimate=pl.CostEstimate(flops=2 * 2**30, bytes_accessed=14 * 2**20, transcendentals=0),
        name="tile_b",
    )(partial, ahead, row, start)


def bcast_sum(array, axis):
    length = lax.axis_size(axis)
    copies = jnp.broadcast_to(array[None], (length, *array.shape))
    return lax.all_to_all(copies, axis, 0, 0, tiled=True).astype(F32).sum(axis=0)


def with_gram(wide, gram):
    width, quarter = wide.shape[1], K * K // 4
    high = lax.reduce_precision(gram, 8, 7)
    flat = jnp.concatenate([high.reshape(4, quarter), (gram - high).reshape(4, quarter)], axis=1)
    flat = jnp.pad(flat, ((0, 0), (0, width - 2 * quarter)))
    return jnp.concatenate([wide, flat], axis=0).astype(BF16)


def split_gram(packed):
    quarter = K * K // 4
    flat = packed[K:, :quarter] + packed[K:, quarter : 2 * quarter]
    return packed[:K], flat.reshape(K, K)


def row_sum(wide, gram=None):
    half = wide.shape[1] // 2
    first = lax.axis_index("core") == 0
    lo, hi = wide[:, :half], wide[:, half:]
    keep, give = jnp.where(first, lo, hi), jnp.where(first, hi, lo)
    mine = keep + swap_core(give)
    if gram is None:
        mine = bcast_sum(mine.astype(BF16), "z")
    else:
        mine, gram = split_gram(bcast_sum(with_gram(mine, gram), "z"))
        gram = gram + swap_core(gram)
    other = swap_core(mine)
    full = jnp.where(
        first,
        jnp.concatenate([mine, other], axis=1),
        jnp.concatenate([other, mine], axis=1),
    )
    return full if gram is None else (full, gram)


def dot_t(a, b, dims):
    return lax.dot_general(a, b, (dims, ((), ())), preferred_element_type=F32)


def eliminate(gram, wide=None):
    row = lax.broadcasted_iota(jnp.int32, (K, 1), 0)
    for j in range(K - 1):
        factor = jnp.where(row > j, gram[:, j : j + 1] / gram[j : j + 1, j : j + 1], 0.0)
        if wide is not None:
            wide = wide - factor * wide[j : j + 1, :]
        gram = gram - factor * gram[j : j + 1, :]
    eye = row == lax.broadcasted_iota(jnp.int32, (K, K), 1)
    pivots = jnp.where(eye, gram, 0.0)
    if wide is not None:
        wide = wide / jnp.sqrt(jnp.sum(pivots, axis=1, keepdims=True))
    return jnp.sqrt(jnp.sum(pivots, axis=0, keepdims=True)), wide


def solve_kernel(gram, wide, out, diagonal):
    diagonal[...], out[...] = eliminate(gram[...], wide[...])


def solve(gram, wide):
    return pl.pallas_call(
        solve_kernel,
        in_specs=[VMEM] * 2,
        out_specs=[VMEM] * 2,
        out_shape=[jax.ShapeDtypeStruct(wide.shape, F32), jax.ShapeDtypeStruct((1, K), F32)],
        compiler_params=pltpu.CompilerParams(vmem_limit_bytes=4 * 2**20),
        name="solve",
    )(gram, wide)


def last_kernel(first, gram2, gram3, wide, out, spectrum):
    second, _ = eliminate(gram2[...])
    third, vectors = eliminate(gram3[...], wide[...])
    out[...] = vectors * jnp.sqrt(F32(S))
    spectrum[0:1, :] = first[...]
    spectrum[1:2, :] = second
    spectrum[2:3, :] = third / second


def last(first, gram2, gram3, wide):
    return pl.pallas_call(
        last_kernel,
        in_specs=[VMEM] * 4,
        out_specs=[VMEM] * 2,
        out_shape=[jax.ShapeDtypeStruct(wide.shape, F32), jax.ShapeDtypeStruct((3, K), F32)],
        compiler_params=pltpu.CompilerParams(vmem_limit_bytes=4 * 2**20),
        name="last",
    )(first, gram2, gram3, wide)


def body(genotypes, snp_index, freq_table, prior, start_vectors):
    z, core, x, y = (lax.axis_index(a) for a in ALL)
    sign = 1 - 2 * core
    steps = jnp.array([0, 0, -1, -1, -2, -2, -3, -3, -4, 1, 1, 2, 2, 3, 3, 4], jnp.int32)
    flips = jnp.array([0, 1, 0, 1, 0, 1, 0, 1, 0, 1, 0, 1, 0, 1, 0, 1], jnp.int32)
    order = ((z + sign * steps) % 8) * 2 + (core + flips) % 2
    along = jnp.array([0, -1, 1, 2] * 4, jnp.int32)
    across = jnp.array([0] * 4 + [-1] * 4 + [1] * 4 + [2] * 4, jnp.int32)
    index = ((x + jnp.where(core == 0, along, across)) % 4) * 4 + (
        y + jnp.where(core == 0, across, along)
    ) % 4

    standard = standardize(genotypes, snp_index, freq_table)
    piece = lax.all_to_all(standard, ROW, 0, 0, tiled=True)
    standard, piece = lax.optimization_barrier((standard, piece))
    own = lax.all_to_all(standard, COL, 0, 0, tiled=True)
    a, b = own, swap_core(own)
    down, up = [a, b], []
    for j in range(1, 5):
        a = ring_z(a)
        down.append(a)
        up.append(swap_core(a))
        if j < 4:
            b = ring_z(b)
            down.append(b)
            up.append(swap_core(b))
    columns = down + up

    piece = turn(order, piece)
    f = first_axis(piece, 1)
    g = first_axis(piece, -1)
    h = first_axis(f[:512], 1)
    i = first_axis(g[512:], -1)
    h0 = jnp.concatenate([piece, f], axis=1)
    h1 = jnp.concatenate([g, jnp.concatenate([h, i], axis=0)], axis=1)
    f0 = second_axis(h0, 1)
    g0 = second_axis(h0, -1)
    f1 = second_axis(h1, 1)
    g1 = second_axis(h1, -1)
    last0 = second_axis(f0, 1)
    last1 = second_axis(g1, -1)
    partial, ahead = tile_a(index, columns, [h0, h1, f0, f1, g0, g1], prior)
    start = (start_vectors.T / jnp.sqrt(F32(S))).astype(BF16)
    ahead, last0, last1 = lax.optimization_barrier((ahead, last0, last1))
    grm, rounded, image = tile_b(partial, ahead, jnp.concatenate([last0, last1], axis=1), start)
    image = row_sum(image)
    gram1 = dot_t(image, image, ((1,), (1,)))
    packed = with_gram(dot_t(image.astype(BF16), rounded, ((1,), (1,))), gram1)
    second, gram1 = split_gram(bcast_sum(packed, COL))
    second, diagonal = solve(gram1, second)
    third, gram2 = row_sum(
        dot_t(second.astype(BF16), rounded, ((1,), (0,))), dot_t(second, second, ((1,), (1,)))
    )
    gram3 = bcast_sum(dot_t(third, third, ((1,), (1,))), COL)
    vectors, spectrum = last(diagonal, gram2, gram3, third)
    return (grm, vectors.T, spectrum)


def solution(mesh):
    finer = Mesh(mesh.devices.reshape(SIZES), ALL)
    in_specs = (P(ALL, None), P(ALL), P(), P(ROW, COL), P(ROW, None))
    out_specs = (P(ROW, COL), P(COL, None), P())
    return jax.shard_map(body, mesh=finer, in_specs=in_specs, out_specs=out_specs, check_vma=False)
```

profile of v0, /device:TPU:32, one launch (start us, length us, event | category | flops | bytes accessed | tf_op | source)
XLA Modules:
  0.0 206.5 jit_solution(16789867353314052559)
XLA Ops:
  0.7 1.2 copy-done
  3.4 2.5 %standardize.1 = bf16[16,16,1024]{2,1,0:T(8,128)(2,1)} custom-call(s32[16]{0:T(128)S(1)} %copy-done.2, f32[128,128]{1,0:T(8,128)S(1)} %bitcast.13, s32[16,16384]{1,0:T(8,128)S(1)} %copy-done), custom_call_target="tpu_custom_call" | custom-call | tf_op jit(solution)/shard_map/standardize/pallas_call | solution.py:83
  5.9 22.8 %all_to_all.30.piece = bf16[16,16,1024]{2,1,0:T(8,128)(2,1)S(1)} all-to-all(bf16[16,16,1024]{2,1,0:T(8,128)(2,1)} %standardize.1), channel_id=1, replica_groups=mesh['z'=8,'core'=2,'x'=4,'y'=4] {'z','core'}, dimensions={0} | all-to-all | bytes 1048576 | tf_op jit(solution)/shard_map/all_to_all | solution.py:322
  28.7 7.0 %all-to-all-start.1 = ((bf16[16,16,1024]{2,1,0:T(8,128)(2,1)}), bf16[16,16,1024]{2,1,0:T(8,128)(2,1)S(1)}, u32[]{:S(2)}, u32[]{:S(2)}) async-start(bf16[16,16,1024]{2,1,0:T(8,128)(2,1)} %standardize.1), calls=%async_computation.1 | async-start | bytes 1048576 | tf_op jit(solution)/shard_map/all_to_all | solution.py:324
  36.5 2.0 collective-permute-start.15
  38.5 9.3 %all-to-all-done.1.refs_0_ = bf16[16,16,1024]{2,1,0:T(8,128)(2,1)S(1)} async-done(((bf16[16,16,1024]{2,1,0:T(8,128)(2,1)}), bf16[16,16,1024]{2,1,0:T(8,128)(2,1)S(1)}, u32[]{:S(2)}, u32[]{:S(2)}) %all-to-all-start.1) | async-done | bytes 524320 | tf_op jit(solution)/shard_map/all_to_all | solution.py:324
  47.8 1.8 collective-permute-start.1
  51.4 1.3 collective-permute-start.19
  52.7 4.3 %collective-permute-done.1.refs_2_ = bf16[16,16,1024]{2,1,0:T(8,128)(2,1)S(1)} collective-permute-done((bf16[16,16,1024]{2,1,0:T(8,128)(2,1)S(1)}, bf16[16,16,1024]{2,1,0:T(8,128)(2,1)S(1)}, u32[]{:S(2)}, u32[]{:S(2)}) %collective-permute-start.1) | collective-permute-done | bytes 524320 | tf_op jit(solution)/shard_map/ppermute | solution.py:35
  57.0 1.8 collective-permute-start.3
  58.8 1.5 collective-permute-start.2
  60.5 3.3 %collective-permute-start.18 = (bf16[512,256]{1,0:T(8,128)(2,1)S(1)}, bf16[512,256]{1,0:T(8,128)(2,1)S(1)}, u32[]{:S(2)}, u32[]{:S(2)}) collective-permute-start(bf16[512,256]{1,0:T(8,128)(2,1)S(1)} %slice.49), channel_id=1, source_target_pairs={{0,12},{1,13},{2,14},{3,15},{4,0},{5,1},{6,2},{7,3},{8,4},{9,5},{1... | collective-permute-start | bytes 786440 | tf_op jit(solution)/shard_map/ppermute | solution.py:35
  63.8 5.4 %collective-permute-done.17 = bf16[512,256]{1,0:T(8,128)(2,1)S(1)} collective-permute-done((bf16[512,256]{1,0:T(8,128)(2,1)S(1)}, bf16[512,256]{1,0:T(8,128)(2,1)S(1)}, u32[]{:S(2)}, u32[]{:S(2)}) %collective-permute-start.17) | collective-permute-done | bytes 262176 | tf_op jit(solution)/shard_map/ppermute | solution.py:35
  69.2 1.0 collective-permute-start.21
  70.3 1.3 collective-permute-start.22
  73.7 1.6 collective-permute-start.5
  75.3 1.3 collective-permute-start.4
  76.6 7.4 %collective-permute-done.21.refs_20_ = bf16[1024,512]{1,0:T(8,128)(2,1)S(1)} collective-permute-done((bf16[1024,512]{1,0:T(8,128)(2,1)S(1)}, bf16[1024,512]{1,0:T(8,128)(2,1)S(1)}, u32[]{:S(2)}, u32[]{:S(2)}) %collective-permute-start.21) | collective-permute-done | bytes 1048608 | tf_op jit(solution)/shard_map/ppermute | solution.py:35
  84.0 1.0 copy-done.5
  85.8 1.8 collective-permute-start.7
  87.6 2.2 %collective-permute-done.4.refs_5_ = bf16[16,16,1024]{2,1,0:T(8,128)(2,1)} collective-permute-done((bf16[16,16,1024]{2,1,0:T(8,128)(2,1)}, bf16[16,16,1024]{2,1,0:T(8,128)(2,1)}, u32[]{:S(2)}, u32[]{:S(2)}) %collective-permute-start.4) | collective-permute-done | bytes 524320 | tf_op jit(solution)/shard_map/ppermute | solution.py:35
  90.2 5.0 %collective-permute-done.22.refs_21_ = bf16[1024,512]{1,0:T(8,128)(2,1)S(1)} collective-permute-done((bf16[1024,512]{1,0:T(8,128)(2,1)S(1)}, bf16[1024,512]{1,0:T(8,128)(2,1)S(1)}, u32[]{:S(2)}, u32[]{:S(2)}) %collective-permute-start.22) | collective-permute-done | bytes 1048608 | tf_op jit(solution)/shard_map/ppermute | solution.py:35
  95.3 1.0 copy-done.9
  98.0 3.0 %collective-permute-done.6.refs_7_ = bf16[16,16,1024]{2,1,0:T(8,128)(2,1)} collective-permute-done((bf16[16,16,1024]{2,1,0:T(8,128)(2,1)}, bf16[16,16,1024]{2,1,0:T(8,128)(2,1)}, u32[]{:S(2)}, u32[]{:S(2)}) %collective-permute-start.6) | collective-permute-done | bytes 524320 | tf_op jit(solution)/shard_map/ppermute | solution.py:35
  101.1 1.2 collective-permute-start.23
  102.3 2.1 collective-permute-start.24
  104.4 1.2 copy-done.4
  105.6 1.2 copy-done.6
  106.8 1.2 copy-done.8
  108.1 1.2 copy-done.10
  109.3 1.0 copy-done.12
  110.3 1.0 copy-done.14
  111.4 1.0 copy-done.16
  112.4 1.0 copy-done.18
  113.5 14.5 %tile_a.1 = (f32[1024,1024]{1,0:T(8,128)S(1)}, bf16[1024,1024]{1,0:T(8,128)(2,1)S(1)}) custom-call(s32[16]{0:T(128)S(1)} %fusion.16.index, bf16[16,16,1024]{2,1,0:T(8,128)(2,1)S(1)} %all-to-all-done.1.refs_0_, bf16[16,16,1024]{2,1,0:T(8,128)(2,1)S(1)} %copy-done.12, bf16[16,16,1024]{2,1,0:T(8,128)(2,1)S(1)} %collective-permute-done.1.refs_2_, ...), custom_call_target="tpu_custom_call" | custom-call | flops 6442450944 | bytes 18874368 | tf_op jit(solution)/shard_map/tile_a/pallas_call | solution.py:163
  128.3 4.5 %tile_b.1 = (f32[1024,1024]{1,0:T(8,128)}, bf16[1024,1024]{1,0:T(8,128)(2,1)S(1)}, f32[20,1024]{1,0:T(8,128)S(1)}) custom-call(f32[1024,1024]{1,0:T(8,128)S(1)} %get-tuple-element.19.partial, bf16[1024,1024]{1,0:T(8,128)(2,1)S(1)} %get-tuple-element.21.ahead, bf16[1024,1024]{1,0:T(8,128)(2,1)S(1)} %pad_maximum_fusion.row, bf16[20,1024]{1,0:T(8,128)(2,1)S(1)} %fusion.3.start), custom_call_target="tpu_custom_call" | custom-call | flops 2147483648 | bytes 14680064 | tf_op jit(solution)/shard_map/tile_b/pallas_call | solution.py:200
  132.9 1.2 collective-permute-done.25
  134.2 16.7 %all_to_all.31 = bf16[8,20,512]{2,1,0:T(8,128)(2,1)S(1)} all-to-all(bf16[8,20,512]{2,1,0:T(8,128)(2,1)S(1)} %broadcast_in_dim.8), channel_id=1, replica_groups=mesh['z'=8,'core'=2,'x'=4,'y'=4] {'z'}, dimensions={0} | all-to-all | bytes 327680 | tf_op jit(solution)/shard_map/all_to_all | solution.py:219
  151.4 1.2 collective-permute-done.26
  153.7 18.1 %all_to_all.32 = bf16[16,24,1024]{2,1,0:T(8,128)(2,1)S(1)} all-to-all(bf16[16,24,1024]{2,1,0:T(8,128)(2,1)S(1)} %broadcast_in_dim.9), channel_id=1, replica_groups=mesh['z'=8,'core'=2,'x'=4,'y'=4] {'x','y'}, dimensions={0} | all-to-all | bytes 1572864 | tf_op jit(solution)/shard_map/all_to_all | solution.py:219
  172.1 1.6 solve.1
  174.7 1.0 collective-permute-done.27
  175.7 13.5 %all_to_all.33 = bf16[8,24,512]{2,1,0:T(8,128)(2,1)S(1)} all-to-all(bf16[8,24,512]{2,1,0:T(8,128)(2,1)S(1)} %broadcast_in_dim.10), channel_id=1, replica_groups=mesh['z'=8,'core'=2,'x'=4,'y'=4] {'z'}, dimensions={0} | all-to-all | bytes 393216 | tf_op jit(solution)/shard_map/all_to_all | solution.py:219
  189.3 1.2 collective-permute-done.29
  191.5 3.6 %all-to-all-start.5 = ((f32[16,1,400]{2,1,0:T(1,128)}), f32[16,1,400]{2,1,0:T(1,128)S(1)}, u32[]{:S(2)}, u32[]{:S(2)}) async-start(f32[16,1,400]{2,1,0:T(1,128)} %reshape.70), calls=%async_computation.5 | async-start | bytes 65536 | tf_op jit(solution)/shard_map/all_to_all | solution.py:219
  195.3 1.1 collective-permute-done.28
  196.5 6.3 %all-to-all-done.5 = f32[16,1,400]{2,1,0:T(1,128)S(1)} async-done(((f32[16,1,400]{2,1,0:T(1,128)}), f32[16,1,400]{2,1,0:T(1,128)S(1)}, u32[]{:S(2)}, u32[]{:S(2)}) %all-to-all-start.5) | async-done | bytes 25632 | tf_op jit(solution)/shard_map/all_to_all | solution.py:219
  204.2 2.3 %last.1 = (f32[20,1024]{1,0:T(8,128)}, f32[3,20]{1,0:T(4,128)}) custom-call(f32[1,20]{1,0:T(1,128)S(1)} %get-tuple-element.27.first, f32[20,20]{1,0:T(8,128)S(1)} %add.85.gram2, f32[20,20]{1,0:T(8,128)S(1)} %reduce_sum.39.gram3, f32[20,1024]{1,0:T(8,128)S(1)} %maximum_select_fusion.1.wide), custom_call_target="tpu_custom_call" | custom-call | tf_op jit(solution)/shard_map/last/pallas_call | solution.py:299
  (117 shorter events, 15.4 us)
Async XLA Ops:
  0.6 35.1 %copy-start.22 = (s32[16]{0:T(128)S(1)}, s32[16]{0:T(128)}, u32[]{:S(2)}) copy-start(s32[16]{0:T(128)} %constant.81.clone) | copy-start | bytes 196
  0.6 35.1 %copy-start.23 = (s32[16]{0:T(128)S(1)}, s32[16]{0:T(128)}, u32[]{:S(2)}) copy-start(s32[16]{0:T(128)} %constant.82.clone) | copy-start | bytes 196
  0.7 1.2 copy-start
  28.7 19.1 %all-to-all-start.1 = ((bf16[16,16,1024]{2,1,0:T(8,128)(2,1)}), bf16[16,16,1024]{2,1,0:T(8,128)(2,1)S(1)}, u32[]{:S(2)}, u32[]{:S(2)}) async-start(bf16[16,16,1024]{2,1,0:T(8,128)(2,1)} %standardize.1), calls=%async_computation.1 | async-start | bytes 1048576 | tf_op jit(solution)/shard_map/all_to_all | solution.py:324
  36.5 14.7 %collective-permute-start.15 = (bf16[1024,256]{1,0:T(8,128)(2,1)S(1)}, bf16[1024,256]{1,0:T(8,128)(2,1)S(1)}, u32[]{:S(2)}, u32[]{:S(2)}) collective-permute-start(bf16[1024,256]{1,0:T(8,128)(2,1)S(1)} %turn.1), channel_id=1, source_target_pairs={{0,4},{1,5},{2,6},{3,7},{4,8},{5,9},{6,10},{7,11},{8,12},{9,13},{1... | collective-permute-start | bytes 1572872 | tf_op jit(solution)/shard_map/ppermute | solution.py:35
  47.8 9.2 %collective-permute-start.1 = (bf16[16,16,1024]{2,1,0:T(8,128)(2,1)S(1)}, bf16[16,16,1024]{2,1,0:T(8,128)(2,1)S(1)}, u32[]{:S(2)}, u32[]{:S(2)}) collective-permute-start(bf16[16,16,1024]{2,1,0:T(8,128)(2,1)S(1)} %all-to-all-done.1.refs_0_), channel_id=1, source_target_pairs={{0,32},{1,33},{2,34},{3,35},{4,36},{5,37},{6,38},{7,39},{8,40},{9,... | collective-permute-start | bytes 1572872 | tf_op jit(solution)/shard_map/ppermute | solution.py:35
  49.6 9.2 %collective-permute-start = (bf16[16,16,1024]{2,1,0:T(8,128)(2,1)S(1)}, bf16[16,16,1024]{2,1,0:T(8,128)(2,1)S(1)}, u32[]{:S(2)}, u32[]{:S(2)}) collective-permute-start(bf16[16,16,1024]{2,1,0:T(8,128)(2,1)S(1)} %all-to-all-done.1.refs_0_), channel_id=1, source_target_pairs={{0,16},{1,17},{2,18},{3,19},{4,20},{5,21},{6,22},{7,23},{8,24},{9,... | collective-permute-start | bytes 1572872 | tf_op jit(solution)/shard_map/ppermute | solution.py:35
  50.4 10.1 %collective-permute-start.16 = (bf16[1024,256]{1,0:T(8,128)(2,1)S(1)}, bf16[1024,256]{1,0:T(8,128)(2,1)S(1)}, u32[]{:S(2)}, u32[]{:S(2)}) collective-permute-start(bf16[1024,256]{1,0:T(8,128)(2,1)S(1)} %turn.1), channel_id=1, source_target_pairs={{0,12},{1,13},{2,14},{3,15},{4,0},{5,1},{6,2},{7,3},{8,4},{9,5},{1... | collective-permute-start | bytes 1572872 | tf_op jit(solution)/shard_map/ppermute | solution.py:35
  51.3 53.0 %copy-start.20 = (s32[16]{0:T(128)S(1)}, s32[16]{0:T(128)}, u32[]{:S(2)}) copy-start(s32[16]{0:T(128)} %constant.83.clone) | copy-start | bytes 196
  51.4 53.0 %copy-start.21 = (s32[16]{0:T(128)S(1)}, s32[16]{0:T(128)}, u32[]{:S(2)}) copy-start(s32[16]{0:T(128)} %constant.84.clone) | copy-start | bytes 196
  51.4 53.0 %copy-start.19 = (f32[1024,20]{0,1:T(8,128)S(1)}, f32[1024,20]{0,1:T(8,128)}, u32[]{:S(2)}) copy-start(f32[1024,20]{0,1:T(8,128)} %param.13) | copy-start | bytes 245764
  51.4 23.9 %collective-permute-start.19 = (bf16[1024,512]{1,0:T(8,128)(2,1)S(1)}, bf16[1024,512]{1,0:T(8,128)(2,1)S(1)}, u32[]{:S(2)}, u32[]{:S(2)}) collective-permute-start(bf16[1024,512]{1,0:T(8,128)(2,1)S(1)} %pad_maximum_fusion.1.refs_16_), channel_id=1, source_target_pairs={{0,1},{1,2},{2,3},{3,0},{4,5},{5,6},{6,7},{7,4},{8,9},{9,10},{10,1... | collective-permute-start | bytes 3145736 | tf_op jit(solution)/shard_map/ppermute | solution.py:35
  57.0 13.3 %collective-permute-start.3 = (bf16[16,16,1024]{2,1,0:T(8,128)(2,1)S(1)}, bf16[16,16,1024]{2,1,0:T(8,128)(2,1)S(1)}, u32[]{:S(2)}, u32[]{:S(2)}) collective-permute-start(bf16[16,16,1024]{2,1,0:T(8,128)(2,1)S(1)} %collective-permute-done.1.refs_2_), channel_id=1, source_target_pairs={{0,32},{1,33},{2,34},{3,35},{4,36},{5,37},{6,38},{7,39},{8,40},{9,... | collective-permute-start | bytes 1572872 | tf_op jit(solution)/shard_map/ppermute | solution.py:35
  58.8 37.9 %copy-start.11 = (bf16[16,16,1024]{2,1,0:T(8,128)(2,1)}, bf16[16,16,1024]{2,1,0:T(8,128)(2,1)S(1)}, u32[]{:S(2)}) copy-start(bf16[16,16,1024]{2,1,0:T(8,128)(2,1)S(1)} %collective-permute-done.refs_1_) | copy-start | bytes 1572868
  58.8 13.6 %collective-permute-start.2 = (bf16[16,16,1024]{2,1,0:T(8,128)(2,1)S(1)}, bf16[16,16,1024]{2,1,0:T(8,128)(2,1)}, u32[]{:S(2)}, u32[]{:S(2)}) collective-permute-start(bf16[16,16,1024]{2,1,0:T(8,128)(2,1)S(1)} %collective-permute-done.refs_1_), channel_id=1, source_target_pairs={{0,32},{1,33},{2,34},{3,35},{4,36},{5,37},{6,38},{7,39},{8,40},{9,... | collective-permute-start | bytes 1572872 | tf_op jit(solution)/shard_map/ppermute | solution.py:35
  60.4 8.8 %collective-permute-start.17 = (bf16[512,256]{1,0:T(8,128)(2,1)S(1)}, bf16[512,256]{1,0:T(8,128)(2,1)S(1)}, u32[]{:S(2)}, u32[]{:S(2)}) collective-permute-start(bf16[512,256]{1,0:T(8,128)(2,1)S(1)} %slice.48), channel_id=1, source_target_pairs={{0,4},{1,5},{2,6},{3,7},{4,8},{5,9},{6,10},{7,11},{8,12},{9,13},{1... | collective-permute-start | bytes 786440 | tf_op jit(solution)/shard_map/ppermute | solution.py:35
  60.5 9.7 %collective-permute-start.18 = (bf16[512,256]{1,0:T(8,128)(2,1)S(1)}, bf16[512,256]{1,0:T(8,128)(2,1)S(1)}, u32[]{:S(2)}, u32[]{:S(2)}) collective-permute-start(bf16[512,256]{1,0:T(8,128)(2,1)S(1)} %slice.49), channel_id=1, source_target_pairs={{0,12},{1,13},{2,14},{3,15},{4,0},{5,1},{6,2},{7,3},{8,4},{9,5},{1... | collective-permute-start | bytes 786440 | tf_op jit(solution)/shard_map/ppermute | solution.py:35
  69.2 14.8 %collective-permute-start.21 = (bf16[1024,512]{1,0:T(8,128)(2,1)S(1)}, bf16[1024,512]{1,0:T(8,128)(2,1)S(1)}, u32[]{:S(2)}, u32[]{:S(2)}) collective-permute-start(bf16[1024,512]{1,0:T(8,128)(2,1)S(1)} %pad_maximum_fusion.1.refs_16_), channel_id=1, source_target_pairs={{0,3},{1,0},{2,1},{3,2},{4,7},{5,4},{6,5},{7,6},{8,11},{9,8},{10,9... | collective-permute-start | bytes 3145736 | tf_op jit(solution)/shard_map/ppermute | solution.py:35
  70.2 2.7 %collective-permute-start.8 = (bf16[16,16,1024]{2,1,0:T(8,128)(2,1)S(1)}, bf16[16,16,1024]{2,1,0:T(8,128)(2,1)S(1)}, u32[]{:S(2)}, u32[]{:S(2)}) collective-permute-start(bf16[16,16,1024]{2,1,0:T(8,128)(2,1)S(1)} %collective-permute-done.1.refs_2_), channel_id=1, source_target_pairs={{0,16},{1,17},{2,18},{3,19},{4,20},{5,21},{6,22},{7,23},{8,24},{9,... | collective-permute-start | bytes 1572872 | tf_op jit(solution)/shard_map/ppermute | solution.py:35
  70.3 24.9 %collective-permute-start.22 = (bf16[1024,512]{1,0:T(8,128)(2,1)S(1)}, bf16[1024,512]{1,0:T(8,128)(2,1)S(1)}, u32[]{:S(2)}, u32[]{:S(2)}) collective-permute-start(bf16[1024,512]{1,0:T(8,128)(2,1)S(1)} %maximum_maximum_fusion.refs_17_), channel_id=1, source_target_pairs={{0,3},{1,0},{2,1},{3,2},{4,7},{5,4},{6,5},{7,6},{8,11},{9,8},{10,9... | collective-permute-start | bytes 3145736 | tf_op jit(solution)/shard_map/ppermute | solution.py:35
  72.4 22.9 %collective-permute-start.20 = (bf16[1024,512]{1,0:T(8,128)(2,1)S(1)}, bf16[1024,512]{1,0:T(8,128)(2,1)S(1)}, u32[]{:S(2)}, u32[]{:S(2)}) collective-permute-start(bf16[1024,512]{1,0:T(8,128)(2,1)S(1)} %maximum_maximum_fusion.refs_17_), channel_id=1, source_target_pairs={{0,1},{1,2},{2,3},{3,0},{4,5},{5,6},{6,7},{7,4},{8,9},{9,10},{10,1... | collective-permute-start | bytes 3145736 | tf_op jit(solution)/shard_map/ppermute | solution.py:35
  73.7 12.1 %collective-permute-start.5 = (bf16[16,16,1024]{2,1,0:T(8,128)(2,1)S(1)}, bf16[16,16,1024]{2,1,0:T(8,128)(2,1)}, u32[]{:S(2)}, u32[]{:S(2)}) collective-permute-start(bf16[16,16,1024]{2,1,0:T(8,128)(2,1)S(1)} %collective-permute-done.3.refs_4_), channel_id=1, source_target_pairs={{0,32},{1,33},{2,34},{3,35},{4,36},{5,37},{6,38},{7,39},{8,40},{9,... | collective-permute-start | bytes 1572872 | tf_op jit(solution)/shard_map/ppermute | solution.py:35
  75.3 20.0 %copy-start.3 = (bf16[1024,512]{1,0:T(8,128)(2,1)}, bf16[1024,512]{1,0:T(8,128)(2,1)S(1)}, u32[]{:S(2)}) copy-start(bf16[1024,512]{1,0:T(8,128)(2,1)S(1)} %collective-permute-done.19.refs_18_) | copy-start | bytes 3145732
  75.3 14.5 %collective-permute-start.4 = (bf16[16,16,1024]{2,1,0:T(8,128)(2,1)}, bf16[16,16,1024]{2,1,0:T(8,128)(2,1)}, u32[]{:S(2)}, u32[]{:S(2)}) collective-permute-start(bf16[16,16,1024]{2,1,0:T(8,128)(2,1)} %collective-permute-done.2.refs_3_), channel_id=1, source_target_pairs={{0,32},{1,33},{2,34},{3,35},{4,36},{5,37},{6,38},{7,39},{8,40},{9,... | collective-permute-start | bytes 1572872 | tf_op jit(solution)/shard_map/ppermute | solution.py:35
  85.0 11.7 %collective-permute-start.10 = (bf16[16,16,1024]{2,1,0:T(8,128)(2,1)S(1)}, bf16[16,16,1024]{2,1,0:T(8,128)(2,1)S(1)}, u32[]{:S(2)}, u32[]{:S(2)}) collective-permute-start(bf16[16,16,1024]{2,1,0:T(8,128)(2,1)S(1)} %collective-permute-done.3.refs_4_), channel_id=1, source_target_pairs={{0,16},{1,17},{2,18},{3,19},{4,20},{5,21},{6,22},{7,23},{8,24},{9,... | collective-permute-start | bytes 1572872 | tf_op jit(solution)/shard_map/ppermute | solution.py:35
  85.8 11.8 %collective-permute-start.7 = (bf16[16,16,1024]{2,1,0:T(8,128)(2,1)}, bf16[16,16,1024]{2,1,0:T(8,128)(2,1)}, u32[]{:S(2)}, u32[]{:S(2)}) collective-permute-start(bf16[16,16,1024]{2,1,0:T(8,128)(2,1)} %collective-permute-done.5.refs_6_), channel_id=1, source_target_pairs={{0,32},{1,33},{2,34},{3,35},{4,36},{5,37},{6,38},{7,39},{8,40},{9,... | collective-permute-start | bytes 1572872 | tf_op jit(solution)/shard_map/ppermute | solution.py:35
  89.8 11.2 %collective-permute-start.6 = (bf16[16,16,1024]{2,1,0:T(8,128)(2,1)}, bf16[16,16,1024]{2,1,0:T(8,128)(2,1)}, u32[]{:S(2)}, u32[]{:S(2)}) collective-permute-start(bf16[16,16,1024]{2,1,0:T(8,128)(2,1)} %collective-permute-done.4.refs_5_), channel_id=1, source_target_pairs={{0,32},{1,33},{2,34},{3,35},{4,36},{5,37},{6,38},{7,39},{8,40},{9,... | collective-permute-start | bytes 1572872 | tf_op jit(solution)/shard_map/ppermute | solution.py:35
  95.2 1.5 copy-start.7
  95.2 5.8 %collective-permute-start.9 = (bf16[16,16,1024]{2,1,0:T(8,128)(2,1)}, bf16[16,16,1024]{2,1,0:T(8,128)(2,1)}, u32[]{:S(2)}, u32[]{:S(2)}) collective-permute-start(bf16[16,16,1024]{2,1,0:T(8,128)(2,1)} %collective-permute-done.2.refs_3_), channel_id=1, source_target_pairs={{0,16},{1,17},{2,18},{3,19},{4,20},{5,21},{6,22},{7,23},{8,24},{9,... | collective-permute-start | bytes 1572872 | tf_op jit(solution)/shard_map/ppermute | solution.py:35
  96.2 6.0 %collective-permute-start.12 = (bf16[16,16,1024]{2,1,0:T(8,128)(2,1)}, bf16[16,16,1024]{2,1,0:T(8,128)(2,1)}, u32[]{:S(2)}, u32[]{:S(2)}) collective-permute-start(bf16[16,16,1024]{2,1,0:T(8,128)(2,1)} %collective-permute-done.5.refs_6_), channel_id=1, source_target_pairs={{0,16},{1,17},{2,18},{3,19},{4,20},{5,21},{6,22},{7,23},{8,24},{9,... | collective-permute-start | bytes 1572872 | tf_op jit(solution)/shard_map/ppermute | solution.py:35
  97.5 6.8 %collective-permute-start.11 = (bf16[16,16,1024]{2,1,0:T(8,128)(2,1)}, bf16[16,16,1024]{2,1,0:T(8,128)(2,1)}, u32[]{:S(2)}, u32[]{:S(2)}) collective-permute-start(bf16[16,16,1024]{2,1,0:T(8,128)(2,1)} %collective-permute-done.4.refs_5_), channel_id=1, source_target_pairs={{0,16},{1,17},{2,18},{3,19},{4,20},{5,21},{6,22},{7,23},{8,24},{9,... | collective-permute-start | bytes 1572872 | tf_op jit(solution)/shard_map/ppermute | solution.py:35
  97.6 6.8 %collective-permute-start.14 = (bf16[16,16,1024]{2,1,0:T(8,128)(2,1)}, bf16[16,16,1024]{2,1,0:T(8,128)(2,1)}, u32[]{:S(2)}, u32[]{:S(2)}) collective-permute-start(bf16[16,16,1024]{2,1,0:T(8,128)(2,1)} %collective-permute-done.7.refs_8_), channel_id=1, source_target_pairs={{0,16},{1,17},{2,18},{3,19},{4,20},{5,21},{6,22},{7,23},{8,24},{9,... | collective-permute-start | bytes 1572872 | tf_op jit(solution)/shard_map/ppermute | solution.py:35
  101.1 3.3 %collective-permute-start.13 = (bf16[16,16,1024]{2,1,0:T(8,128)(2,1)}, bf16[16,16,1024]{2,1,0:T(8,128)(2,1)}, u32[]{:S(2)}, u32[]{:S(2)}) collective-permute-start(bf16[16,16,1024]{2,1,0:T(8,128)(2,1)} %collective-permute-done.6.refs_7_), channel_id=1, source_target_pairs={{0,16},{1,17},{2,18},{3,19},{4,20},{5,21},{6,22},{7,23},{8,24},{9,... | collective-permute-start | bytes 1572872 | tf_op jit(solution)/shard_map/ppermute | solution.py:35
  101.1 26.9 %collective-permute-start.23 = (bf16[1024,512]{1,0:T(8,128)(2,1)}, bf16[1024,512]{1,0:T(8,128)(2,1)S(1)}, u32[]{:S(2)}, u32[]{:S(2)}) collective-permute-start(bf16[1024,512]{1,0:T(8,128)(2,1)} %copy-done.3), channel_id=1, source_target_pairs={{0,1},{1,2},{2,3},{3,0},{4,5},{5,6},{6,7},{7,4},{8,9},{9,10},{10,1... | collective-permute-start | bytes 3145736 | tf_op jit(solution)/shard_map/ppermute | solution.py:35
  102.3 25.7 %collective-permute-start.24 = (bf16[1024,512]{1,0:T(8,128)(2,1)}, bf16[1024,512]{1,0:T(8,128)(2,1)S(1)}, u32[]{:S(2)}, u32[]{:S(2)}) collective-permute-start(bf16[1024,512]{1,0:T(8,128)(2,1)} %copy-done.7), channel_id=1, source_target_pairs={{0,3},{1,0},{2,1},{3,2},{4,7},{5,4},{6,5},{7,6},{8,11},{9,8},{10,9... | collective-permute-start | bytes 3145736 | tf_op jit(solution)/shard_map/ppermute | solution.py:35
  104.4 1.2 copy-start.4
  105.6 1.2 copy-start.6
  106.8 1.2 copy-start.8
  108.1 1.2 copy-start.10
  109.3 1.0 copy-start.12
  110.3 1.0 copy-start.14
  111.4 1.0 copy-start.16
  132.8 1.3 collective-permute-start.25
  151.0 1.5 collective-permute-start.26
  174.3 1.3 collective-permute-start.27
  189.2 1.3 collective-permute-start.29
  191.5 11.3 %all-to-all-start.5 = ((f32[16,1,400]{2,1,0:T(1,128)}), f32[16,1,400]{2,1,0:T(1,128)S(1)}, u32[]{:S(2)}, u32[]{:S(2)}) async-start(f32[16,1,400]{2,1,0:T(1,128)} %reshape.70), calls=%async_computation.5 | async-start | bytes 65536 | tf_op jit(solution)/shard_map/all_to_all | solution.py:219
  195.3 1.2 collective-permute-start.28
  (8 other events, 6.9 us)
where the time goes:
time: 209 us; the launch traced here: 206 us
  blocking collectives  71.1 us (34%)
  waiting for transfers between devices  49.6 us (24%)
  starting transfers between devices  36.8 us (18%)
  Pallas kernels  26.1 us (12%)
  local copies, waits for them, and re-layouts  18.3 us (9%)
    all_to_all x3, blocking collectives, bcast_sum(): lax.all_to_all(copies, axis, 0, 0, tiled=True).astype(F32).sum(axis=0)  48.3 us
    ppermute x30, waiting for transfers between devices, send(): return lax.ppermute(array, ALL, pairs)  34 us
    ppermute x30, starting transfers between devices, send(): return lax.ppermute(array, ALL, pairs)  26.2 us
    all_to_all x1, blocking collectives, body(): piece = lax.all_to_all(standard, ROW, 0, 0, tiled=True)  22.8 us
    unnamed x50, local copies, waits for them, and re-layouts  17.2 us
    pallas_call x1, Pallas kernels, tile_a(): pl.pallas_call(tile_a_kernel, in_specs=[SMEM] + [ANY] * 23, out_specs=[VM...  14.5 us
    all_to_all x1, waiting for transfers between devices, body(): own = lax.all_to_all(standard, COL, 0, 0, tiled=True)  9.32 us
    all_to_all x1, starting transfers between devices, body(): own = lax.all_to_all(standard, COL, 0, 0, tiled=True)  7.04 us
  transfers between devices with their start and end apart: 32, of which 14 were waited for; matrix products, arithmetic and copies ran while one was open for 0% of the time, Pallas kernels for 7%

commit v1 on v0

--- a/solution.py
+++ b/solution.py
@@ -93,7 +93,7 @@
             scratch_shapes=[pltpu.VMEM((snps, 128), F32)] * 3,
         ),
         out_shape=jax.ShapeDtypeStruct((16, snps, 1024), BF16),
-        compiler_params=pltpu.CompilerParams(vmem_limit_bytes=8 * 2**20),
+        compiler_params=pltpu.CompilerParams(vmem_limit_bytes=60 * 2**20),
         name="standardize",
     )(snp_index, freq_table.reshape(128, 128), genotypes)
 
@@ -179,10 +179,11 @@
     )(index, *columns, *rows, prior)
 
 
-def tile_b_kernel(partial, ahead, row, start, out, rounded, image, total, out_sem):
+def tile_b_kernel(partial, ahead, row0, row1, start, out, rounded, image, total, out_sem):
     def step(n, carry):
         at = pl.ds(pl.multiple_of(n * 256, 256), 256)
-        product = jnp.dot(row[...], ahead[:, at], preferred_element_type=F32)
+        product = jnp.dot(row0[...], ahead[:512, at], preferred_element_type=F32)
+        product += jnp.dot(row1[...], ahead[512:, at], preferred_element_type=F32)
         value = partial[:, at] + product * (1.0 / M)
         total[:, at] = value
         pltpu.make_async_copy(total.at[:, at], out.at[:, at], out_sem.at[n]).start()
@@ -196,10 +197,10 @@
         pltpu.make_async_copy(total.at[:, at], out.at[:, at], out_sem.at[n]).wait()
 
 
-def tile_b(partial, ahead, row, start):
+def tile_b(partial, ahead, row0, row1, start):
     return pl.pallas_call(
         tile_b_kernel,
-        in_specs=[VMEM] * 4,
+        in_specs=[VMEM] * 5,
         out_specs=[ANY, VMEM, VMEM],
         out_shape=[
             jax.ShapeDtypeStruct((1024, 1024), F32),
@@ -210,7 +211,7 @@
         compiler_params=pltpu.CompilerParams(vmem_limit_bytes=20 * 2**20),
         cost_estimate=pl.CostEstimate(flops=2 * 2**30, bytes_accessed=14 * 2**20, transcendentals=0),
         name="tile_b",
-    )(partial, ahead, row, start)
+    )(partial, ahead, row0, row1, start)
 
 
 def bcast_sum(array, axis):
@@ -350,16 +351,18 @@
     partial, ahead = tile_a(index, columns, [h0, h1, f0, f1, g0, g1], prior)
     start = (start_vectors.T / jnp.sqrt(F32(S))).astype(BF16)
     ahead, last0, last1 = lax.optimization_barrier((ahead, last0, last1))
-    grm, rounded, image = tile_b(partial, ahead, jnp.concatenate([last0, last1], axis=1), start)
+    grm, rounded, image = tile_b(partial, ahead, last0, last1, start)
     image = row_sum(image)
     gram1 = dot_t(image, image, ((1,), (1,)))
     packed = with_gram(dot_t(image.astype(BF16), rounded, ((1,), (1,))), gram1)
-    second, gram1 = split_gram(bcast_sum(packed, COL))
+    packed = bcast_sum(packed, "x").astype(BF16)
+    second, gram1 = split_gram(bcast_sum(packed, "y"))
     second, diagonal = solve(gram1, second)
     third, gram2 = row_sum(
         dot_t(second.astype(BF16), rounded, ((1,), (0,))), dot_t(second, second, ((1,), (1,)))
     )
-    gram3 = bcast_sum(dot_t(third, third, ((1,), (1,))), COL)
+    gram3 = jnp.pad(dot_t(third, third, ((1,), (1,))), ((0, 4), (0, 108)))
+    gram3 = bcast_sum(gram3, COL)[:K, :K]
     vectors, spectrum = last(diagonal, gram2, gram3, third)
     return (grm, vectors.T, spectrum)
 

time: 209 us -> 207 us (level)
  local copies, waits for them, and re-layouts: 18.3 us -> 14.8 us
    unnamed x50 -> x42, local copies, waits for them, and re-layouts: 17.2 us -> 13.5 us
    all_to_all x3 -> x4, blocking collectives: 48.3 us -> 49 us  [bcast_sum(): lax.all_to_all(copies, axis, 0, 0, tiled=True).astype(F32).sum(axis=0)]
where the time goes in v1:
time: 207 us; the launch traced here: 205 us
  blocking collectives  71.8 us (35%)
  waiting for transfers between devices  50.2 us (24%)
  starting transfers between devices  36.6 us (18%)
  Pallas kernels  28.1 us (14%)
  local copies, waits for them, and re-layouts  14.8 us (7%)
    all_to_all x4, blocking collectives, bcast_sum(): lax.all_to_all(copies, axis, 0, 0, tiled=True).astype(F32).sum(axis=0)  49 us
    ppermute x30, waiting for transfers between devices, send(): return lax.ppermute(array, ALL, pairs)  33.9 us
    ppermute x30, starting transfers between devices, send(): return lax.ppermute(array, ALL, pairs)  26 us
    all_to_all x1, blocking collectives, body(): piece = lax.all_to_all(standard, ROW, 0, 0, tiled=True)  22.8 us
    pallas_call x1, Pallas kernels, tile_a(): pl.pallas_call(tile_a_kernel, in_specs=[SMEM] + [ANY] * 23, out_specs=[VM...  14.5 us
    unnamed x42, local copies, waits for them, and re-layouts  13.5 us
    all_to_all x1, waiting for transfers between devices, body(): own = lax.all_to_all(standard, COL, 0, 0, tiled=True)  9.32 us
    all_to_all x1, waiting for transfers between devices, bcast_sum(): lax.all_to_all(copies, axis, 0, 0, tiled=True).astype(F32).sum(axis=0)  7.05 us
  transfers between devices with their start and end apart: 32, of which 14 were waited for; matrix products, arithmetic and copies ran while one was open for 0% of the time, Pallas kernels for 7%

profile of v1, /device:TPU:32, one launch (start us, length us, event | category | flops | bytes accessed | tf_op | source)
XLA Modules:
  0.0 204.9 jit_solution(1122910504809898697)
XLA Ops:
  0.7 4.4 %standardize.1 = bf16[16,16,1024]{2,1,0:T(8,128)(2,1)} custom-call(s32[16]{0:T(128)} %index.1, f32[128,128]{1,0:T(8,128)} %bitcast.17, s32[16,16384]{1,0:T(8,128)} %genotypes.1), custom_call_target="tpu_custom_call" | custom-call | tf_op jit(solution)/shard_map/standardize/pallas_call | solution.py:83
  5.1 22.8 %all_to_all.35.piece = bf16[16,16,1024]{2,1,0:T(8,128)(2,1)S(1)} all-to-all(bf16[16,16,1024]{2,1,0:T(8,128)(2,1)} %standardize.1), channel_id=1, replica_groups=mesh['z'=8,'core'=2,'x'=4,'y'=4] {'z','core'}, dimensions={0} | all-to-all | bytes 1048576 | tf_op jit(solution)/shard_map/all_to_all | solution.py:323
  27.9 7.0 %all-to-all-start.1 = ((bf16[16,16,1024]{2,1,0:T(8,128)(2,1)}), bf16[16,16,1024]{2,1,0:T(8,128)(2,1)S(1)}, u32[]{:S(2)}, u32[]{:S(2)}) async-start(bf16[16,16,1024]{2,1,0:T(8,128)(2,1)} %standardize.1), calls=%async_computation.1 | async-start | bytes 1048576 | tf_op jit(solution)/shard_map/all_to_all | solution.py:325
  35.7 2.0 collective-permute-start.15
  37.7 9.3 %all-to-all-done.1.refs_0_ = bf16[16,16,1024]{2,1,0:T(8,128)(2,1)S(1)} async-done(((bf16[16,16,1024]{2,1,0:T(8,128)(2,1)}), bf16[16,16,1024]{2,1,0:T(8,128)(2,1)S(1)}, u32[]{:S(2)}, u32[]{:S(2)}) %all-to-all-start.1) | async-done | bytes 524320 | tf_op jit(solution)/shard_map/all_to_all | solution.py:325
  47.0 1.8 collective-permute-start.1
  50.6 1.3 collective-permute-start.19
  51.9 4.3 %collective-permute-done.1.refs_2_ = bf16[16,16,1024]{2,1,0:T(8,128)(2,1)S(1)} collective-permute-done((bf16[16,16,1024]{2,1,0:T(8,128)(2,1)S(1)}, bf16[16,16,1024]{2,1,0:T(8,128)(2,1)S(1)}, u32[]{:S(2)}, u32[]{:S(2)}) %collective-permute-start.1) | collective-permute-done | bytes 524320 | tf_op jit(solution)/shard_map/ppermute | solution.py:35
  56.2 1.8 collective-permute-start.3
  58.0 1.5 collective-permute-start.2
  59.7 3.3 %collective-permute-start.18 = (bf16[512,256]{1,0:T(8,128)(2,1)S(1)}, bf16[512,256]{1,0:T(8,128)(2,1)S(1)}, u32[]{:S(2)}, u32[]{:S(2)}) collective-permute-start(bf16[512,256]{1,0:T(8,128)(2,1)S(1)} %slice.53), channel_id=1, source_target_pairs={{0,12},{1,13},{2,14},{3,15},{4,0},{5,1},{6,2},{7,3},{8,4},{9,5},{1... | collective-permute-start | bytes 786440 | tf_op jit(solution)/shard_map/ppermute | solution.py:35
  63.0 5.4 %collective-permute-done.17 = bf16[512,256]{1,0:T(8,128)(2,1)S(1)} collective-permute-done((bf16[512,256]{1,0:T(8,128)(2,1)S(1)}, bf16[512,256]{1,0:T(8,128)(2,1)S(1)}, u32[]{:S(2)}, u32[]{:S(2)}) %collective-permute-start.17) | collective-permute-done | bytes 262176 | tf_op jit(solution)/shard_map/ppermute | solution.py:35
  68.4 1.0 collective-permute-start.21
  69.5 1.3 collective-permute-start.22
  72.9 1.6 collective-permute-start.5
  74.5 1.3 collective-permute-start.4
  75.8 7.4 %collective-permute-done.21.refs_20_ = bf16[1024,512]{1,0:T(8,128)(2,1)S(1)} collective-permute-done((bf16[1024,512]{1,0:T(8,128)(2,1)S(1)}, bf16[1024,512]{1,0:T(8,128)(2,1)S(1)}, u32[]{:S(2)}, u32[]{:S(2)}) %collective-permute-start.21) | collective-permute-done | bytes 1048608 | tf_op jit(solution)/shard_map/ppermute | solution.py:35
  83.2 1.0 copy-done.2
  85.0 1.8 collective-permute-start.7
  86.8 2.3 %collective-permute-done.4.refs_5_ = bf16[16,16,1024]{2,1,0:T(8,128)(2,1)} collective-permute-done((bf16[16,16,1024]{2,1,0:T(8,128)(2,1)}, bf16[16,16,1024]{2,1,0:T(8,128)(2,1)}, u32[]{:S(2)}, u32[]{:S(2)}) %collective-permute-start.4) | collective-permute-done | bytes 524320 | tf_op jit(solution)/shard_map/ppermute | solution.py:35
  89.4 5.0 %collective-permute-done.22.refs_21_ = bf16[1024,512]{1,0:T(8,128)(2,1)S(1)} collective-permute-done((bf16[1024,512]{1,0:T(8,128)(2,1)S(1)}, bf16[1024,512]{1,0:T(8,128)(2,1)S(1)}, u32[]{:S(2)}, u32[]{:S(2)}) %collective-permute-start.22) | collective-permute-done | bytes 1048608 | tf_op jit(solution)/shard_map/ppermute | solution.py:35
  94.5 1.0 copy-done.6
  97.3 3.0 %collective-permute-done.6.refs_7_ = bf16[16,16,1024]{2,1,0:T(8,128)(2,1)} collective-permute-done((bf16[16,16,1024]{2,1,0:T(8,128)(2,1)}, bf16[16,16,1024]{2,1,0:T(8,128)(2,1)}, u32[]{:S(2)}, u32[]{:S(2)}) %collective-permute-start.6) | collective-permute-done | bytes 524320 | tf_op jit(solution)/shard_map/ppermute | solution.py:35
  100.3 1.2 collective-permute-start.23
  101.5 2.1 %collective-permute-start.24 = (bf16[1024,512]{1,0:T(8,128)(2,1)}, bf16[1024,512]{1,0:T(8,128)(2,1)S(1)}, u32[]{:S(2)}, u32[]{:S(2)}) collective-permute-start(bf16[1024,512]{1,0:T(8,128)(2,1)} %copy-done.4), channel_id=1, source_target_pairs={{0,3},{1,0},{2,1},{3,2},{4,7},{5,4},{6,5},{7,6},{8,11},{9,8},{10,9... | collective-permute-start | bytes 3145736 | tf_op jit(solution)/shard_map/ppermute | solution.py:35
  103.6 1.2 copy-done.1
  104.8 1.2 copy-done.3
  106.1 1.2 copy-done.5
  107.3 1.2 copy-done.7
  108.5 1.0 copy-done.9
  109.6 1.0 copy-done.11
  110.6 1.0 copy-done.13
  111.6 1.0 copy-done.15
  112.7 14.5 %tile_a.1 = (f32[1024,1024]{1,0:T(8,128)S(1)}, bf16[1024,1024]{1,0:T(8,128)(2,1)S(1)}) custom-call(s32[16]{0:T(128)S(1)} %fusion.16.index, bf16[16,16,1024]{2,1,0:T(8,128)(2,1)S(1)} %all-to-all-done.1.refs_0_, bf16[16,16,1024]{2,1,0:T(8,128)(2,1)S(1)} %copy-done.9, bf16[16,16,1024]{2,1,0:T(8,128)(2,1)S(1)} %collective-permute-done.1.refs_2_, ...), custom_call_target="tpu_custom_call" | custom-call | flops 6442450944 | bytes 18874368 | tf_op jit(solution)/shard_map/tile_a/pallas_call | solution.py:163
  127.2 4.5 %tile_b.1 = (f32[1024,1024]{1,0:T(8,128)}, bf16[1024,1024]{1,0:T(8,128)(2,1)S(1)}, f32[20,1024]{1,0:T(8,128)S(1)}) custom-call(f32[1024,1024]{1,0:T(8,128)S(1)} %get-tuple-element.19.partial, bf16[1024,1024]{1,0:T(8,128)(2,1)S(1)} %get-tuple-element.21.ahead, bf16[1024,512]{1,0:T(8,128)(2,1)S(1)} %collective-permute-done.23.row0, ...), custom_call_target="tpu_custom_call" | custom-call | flops 2147483648 | bytes 14680064 | tf_op jit(solution)/shard_map/tile_b/pallas_call | solution.py:201
  131.8 1.2 collective-permute-done.25
  133.1 16.7 %all_to_all.36 = bf16[8,20,512]{2,1,0:T(8,128)(2,1)S(1)} all-to-all(bf16[8,20,512]{2,1,0:T(8,128)(2,1)S(1)} %broadcast_in_dim.10), channel_id=1, replica_groups=mesh['z'=8,'core'=2,'x'=4,'y'=4] {'z'}, dimensions={0} | all-to-all | bytes 327680 | tf_op jit(solution)/shard_map/all_to_all | solution.py:220
  150.0 1.2 collective-permute-done.26
  152.3 8.9 %all_to_all.37 = bf16[4,24,1024]{2,1,0:T(8,128)(2,1)S(1)} all-to-all(bf16[4,24,1024]{2,1,0:T(8,128)(2,1)S(1)} %broadcast_in_dim.11), channel_id=1, replica_groups=mesh['z'=8,'core'=2,'x'=4,'y'=4] {'x'}, dimensions={0} | all-to-all | bytes 393216 | tf_op jit(solution)/shard_map/all_to_all | solution.py:220
  161.3 9.9 %all_to_all.38 = bf16[4,24,1024]{2,1,0:T(8,128)(2,1)S(1)} all-to-all(bf16[4,24,1024]{2,1,0:T(8,128)(2,1)S(1)} %broadcast_in_dim.12), channel_id=1, replica_groups=mesh['z'=8,'core'=2,'x'=4,'y'=4] {'y'}, dimensions={0} | all-to-all | bytes 393216 | tf_op jit(solution)/shard_map/all_to_all | solution.py:220
  171.4 1.6 solve.1
  173.9 1.0 collective-permute-done.27
  175.0 13.5 %all_to_all.39 = bf16[8,24,512]{2,1,0:T(8,128)(2,1)S(1)} all-to-all(bf16[8,24,512]{2,1,0:T(8,128)(2,1)S(1)} %broadcast_in_dim.13), channel_id=1, replica_groups=mesh['z'=8,'core'=2,'x'=4,'y'=4] {'z'}, dimensions={0} | all-to-all | bytes 393216 | tf_op jit(solution)/shard_map/all_to_all | solution.py:220
  188.6 1.2 collective-permute-done.29
  190.6 3.5 %all-to-all-start.6 = ((f32[16,24,128]{2,1,0:T(8,128)}), f32[16,24,128]{2,1,0:T(8,128)S(1)}, u32[]{:S(2)}, u32[]{:S(2)}) async-start(f32[16,24,128]{2,1,0:T(8,128)} %broadcast_in_dim.14), calls=%async_computation.6 | async-start | bytes 393216 | tf_op jit(solution)/shard_map/all_to_all | solution.py:220
  194.5 1.0 collective-permute-done.28
  195.5 7.1 %all-to-all-done.6 = f32[16,24,128]{2,1,0:T(8,128)S(1)} async-done(((f32[16,24,128]{2,1,0:T(8,128)}), f32[16,24,128]{2,1,0:T(8,128)S(1)}, u32[]{:S(2)}, u32[]{:S(2)}) %all-to-all-start.6) | async-done | bytes 196640 | tf_op jit(solution)/shard_map/all_to_all | solution.py:220
  202.6 2.3 %last.1 = (f32[20,1024]{1,0:T(8,128)}, f32[3,20]{1,0:T(4,128)}) custom-call(f32[1,20]{1,0:T(1,128)S(1)} %get-tuple-element.27.first, f32[20,20]{1,0:T(8,128)S(1)} %add.87.gram2, f32[20,20]{1,0:T(8,128)S(1)} %bitcast.14, f32[20,1024]{1,0:T(8,128)S(1)} %maximum_select_fusion.1.wide), custom_call_target="tpu_custom_call" | custom-call | tf_op jit(solution)/shard_map/last/pallas_call | solution.py:300
  (110 shorter events, 11.8 us)
Async XLA Ops:
  0.6 34.3 %copy-start.19 = (s32[16]{0:T(128)S(1)}, s32[16]{0:T(128)}, u32[]{:S(2)}) copy-start(s32[16]{0:T(128)} %constant.82.clone) | copy-start | bytes 196
  0.6 34.3 %copy-start.20 = (s32[16]{0:T(128)S(1)}, s32[16]{0:T(128)}, u32[]{:S(2)}) copy-start(s32[16]{0:T(128)} %constant.83.clone) | copy-start | bytes 196
  27.9 19.1 %all-to-all-start.1 = ((bf16[16,16,1024]{2,1,0:T(8,128)(2,1)}), bf16[16,16,1024]{2,1,0:T(8,128)(2,1)S(1)}, u32[]{:S(2)}, u32[]{:S(2)}) async-start(bf16[16,16,1024]{2,1,0:T(8,128)(2,1)} %standardize.1), calls=%async_computation.1 | async-start | bytes 1048576 | tf_op jit(solution)/shard_map/all_to_all | solution.py:325
  35.7 14.7 %collective-permute-start.15 = (bf16[1024,256]{1,0:T(8,128)(2,1)S(1)}, bf16[1024,256]{1,0:T(8,128)(2,1)S(1)}, u32[]{:S(2)}, u32[]{:S(2)}) collective-permute-start(bf16[1024,256]{1,0:T(8,128)(2,1)S(1)} %turn.1), channel_id=1, source_target_pairs={{0,4},{1,5},{2,6},{3,7},{4,8},{5,9},{6,10},{7,11},{8,12},{9,13},{1... | collective-permute-start | bytes 1572872 | tf_op jit(solution)/shard_map/ppermute | solution.py:35
  47.0 9.2 %collective-permute-start.1 = (bf16[16,16,1024]{2,1,0:T(8,128)(2,1)S(1)}, bf16[16,16,1024]{2,1,0:T(8,128)(2,1)S(1)}, u32[]{:S(2)}, u32[]{:S(2)}) collective-permute-start(bf16[16,16,1024]{2,1,0:T(8,128)(2,1)S(1)} %all-to-all-done.1.refs_0_), channel_id=1, source_target_pairs={{0,32},{1,33},{2,34},{3,35},{4,36},{5,37},{6,38},{7,39},{8,40},{9,... | collective-permute-start | bytes 1572872 | tf_op jit(solution)/shard_map/ppermute | solution.py:35
  48.8 9.2 %collective-permute-start = (bf16[16,16,1024]{2,1,0:T(8,128)(2,1)S(1)}, bf16[16,16,1024]{2,1,0:T(8,128)(2,1)S(1)}, u32[]{:S(2)}, u32[]{:S(2)}) collective-permute-start(bf16[16,16,1024]{2,1,0:T(8,128)(2,1)S(1)} %all-to-all-done.1.refs_0_), channel_id=1, source_target_pairs={{0,16},{1,17},{2,18},{3,19},{4,20},{5,21},{6,22},{7,23},{8,24},{9,... | collective-permute-start | bytes 1572872 | tf_op jit(solution)/shard_map/ppermute | solution.py:35
  49.6 10.1 %collective-permute-start.16 = (bf16[1024,256]{1,0:T(8,128)(2,1)S(1)}, bf16[1024,256]{1,0:T(8,128)(2,1)S(1)}, u32[]{:S(2)}, u32[]{:S(2)}) collective-permute-start(bf16[1024,256]{1,0:T(8,128)(2,1)S(1)} %turn.1), channel_id=1, source_target_pairs={{0,12},{1,13},{2,14},{3,15},{4,0},{5,1},{6,2},{7,3},{8,4},{9,5},{1... | collective-permute-start | bytes 1572872 | tf_op jit(solution)/shard_map/ppermute | solution.py:35
  50.6 53.0 %copy-start.17 = (s32[16]{0:T(128)S(1)}, s32[16]{0:T(128)}, u32[]{:S(2)}) copy-start(s32[16]{0:T(128)} %constant.84.clone) | copy-start | bytes 196
  50.6 53.0 %copy-start.18 = (s32[16]{0:T(128)S(1)}, s32[16]{0:T(128)}, u32[]{:S(2)}) copy-start(s32[16]{0:T(128)} %constant.85.clone) | copy-start | bytes 196
  50.6 53.0 %copy-start.16 = (f32[1024,20]{0,1:T(8,128)S(1)}, f32[1024,20]{0,1:T(8,128)}, u32[]{:S(2)}) copy-start(f32[1024,20]{0,1:T(8,128)} %param.13) | copy-start | bytes 245764
  50.6 23.9 %collective-permute-start.19 = (bf16[1024,512]{1,0:T(8,128)(2,1)S(1)}, bf16[1024,512]{1,0:T(8,128)(2,1)S(1)}, u32[]{:S(2)}, u32[]{:S(2)}) collective-permute-start(bf16[1024,512]{1,0:T(8,128)(2,1)S(1)} %pad_maximum_fusion.refs_16_), channel_id=1, source_target_pairs={{0,1},{1,2},{2,3},{3,0},{4,5},{5,6},{6,7},{7,4},{8,9},{9,10},{10,1... | collective-permute-start | bytes 3145736 | tf_op jit(solution)/shard_map/ppermute | solution.py:35
  56.2 13.3 %collective-permute-start.3 = (bf16[16,16,1024]{2,1,0:T(8,128)(2,1)S(1)}, bf16[16,16,1024]{2,1,0:T(8,128)(2,1)S(1)}, u32[]{:S(2)}, u32[]{:S(2)}) collective-permute-start(bf16[16,16,1024]{2,1,0:T(8,128)(2,1)S(1)} %collective-permute-done.1.refs_2_), channel_id=1, source_target_pairs={{0,32},{1,33},{2,34},{3,35},{4,36},{5,37},{6,38},{7,39},{8,40},{9,... | collective-permute-start | bytes 1572872 | tf_op jit(solution)/shard_map/ppermute | solution.py:35
  58.0 37.9 %copy-start.8 = (bf16[16,16,1024]{2,1,0:T(8,128)(2,1)}, bf16[16,16,1024]{2,1,0:T(8,128)(2,1)S(1)}, u32[]{:S(2)}) copy-start(bf16[16,16,1024]{2,1,0:T(8,128)(2,1)S(1)} %collective-permute-done.refs_1_) | copy-start | bytes 1572868
  58.0 13.6 %collective-permute-start.2 = (bf16[16,16,1024]{2,1,0:T(8,128)(2,1)S(1)}, bf16[16,16,1024]{2,1,0:T(8,128)(2,1)}, u32[]{:S(2)}, u32[]{:S(2)}) collective-permute-start(bf16[16,16,1024]{2,1,0:T(8,128)(2,1)S(1)} %collective-permute-done.refs_1_), channel_id=1, source_target_pairs={{0,32},{1,33},{2,34},{3,35},{4,36},{5,37},{6,38},{7,39},{8,40},{9,... | collective-permute-start | bytes 1572872 | tf_op jit(solution)/shard_map/ppermute | solution.py:35
  59.6 8.8 %collective-permute-start.17 = (bf16[512,256]{1,0:T(8,128)(2,1)S(1)}, bf16[512,256]{1,0:T(8,128)(2,1)S(1)}, u32[]{:S(2)}, u32[]{:S(2)}) collective-permute-start(bf16[512,256]{1,0:T(8,128)(2,1)S(1)} %slice.52), channel_id=1, source_target_pairs={{0,4},{1,5},{2,6},{3,7},{4,8},{5,9},{6,10},{7,11},{8,12},{9,13},{1... | collective-permute-start | bytes 786440 | tf_op jit(solution)/shard_map/ppermute | solution.py:35
  59.7 9.7 %collective-permute-start.18 = (bf16[512,256]{1,0:T(8,128)(2,1)S(1)}, bf16[512,256]{1,0:T(8,128)(2,1)S(1)}, u32[]{:S(2)}, u32[]{:S(2)}) collective-permute-start(bf16[512,256]{1,0:T(8,128)(2,1)S(1)} %slice.53), channel_id=1, source_target_pairs={{0,12},{1,13},{2,14},{3,15},{4,0},{5,1},{6,2},{7,3},{8,4},{9,5},{1... | collective-permute-start | bytes 786440 | tf_op jit(solution)/shard_map/ppermute | solution.py:35
  68.4 14.8 %collective-permute-start.21 = (bf16[1024,512]{1,0:T(8,128)(2,1)S(1)}, bf16[1024,512]{1,0:T(8,128)(2,1)S(1)}, u32[]{:S(2)}, u32[]{:S(2)}) collective-permute-start(bf16[1024,512]{1,0:T(8,128)(2,1)S(1)} %pad_maximum_fusion.refs_16_), channel_id=1, source_target_pairs={{0,3},{1,0},{2,1},{3,2},{4,7},{5,4},{6,5},{7,6},{8,11},{9,8},{10,9... | collective-permute-start | bytes 3145736 | tf_op jit(solution)/shard_map/ppermute | solution.py:35
  69.4 2.7 %collective-permute-start.8 = (bf16[16,16,1024]{2,1,0:T(8,128)(2,1)S(1)}, bf16[16,16,1024]{2,1,0:T(8,128)(2,1)S(1)}, u32[]{:S(2)}, u32[]{:S(2)}) collective-permute-start(bf16[16,16,1024]{2,1,0:T(8,128)(2,1)S(1)} %collective-permute-done.1.refs_2_), channel_id=1, source_target_pairs={{0,16},{1,17},{2,18},{3,19},{4,20},{5,21},{6,22},{7,23},{8,24},{9,... | collective-permute-start | bytes 1572872 | tf_op jit(solution)/shard_map/ppermute | solution.py:35
  69.5 24.9 %collective-permute-start.22 = (bf16[1024,512]{1,0:T(8,128)(2,1)S(1)}, bf16[1024,512]{1,0:T(8,128)(2,1)S(1)}, u32[]{:S(2)}, u32[]{:S(2)}) collective-permute-start(bf16[1024,512]{1,0:T(8,128)(2,1)S(1)} %maximum_maximum_fusion.refs_17_), channel_id=1, source_target_pairs={{0,3},{1,0},{2,1},{3,2},{4,7},{5,4},{6,5},{7,6},{8,11},{9,8},{10,9... | collective-permute-start | bytes 3145736 | tf_op jit(solution)/shard_map/ppermute | solution.py:35
  71.6 22.9 %collective-permute-start.20 = (bf16[1024,512]{1,0:T(8,128)(2,1)S(1)}, bf16[1024,512]{1,0:T(8,128)(2,1)S(1)}, u32[]{:S(2)}, u32[]{:S(2)}) collective-permute-start(bf16[1024,512]{1,0:T(8,128)(2,1)S(1)} %maximum_maximum_fusion.refs_17_), channel_id=1, source_target_pairs={{0,1},{1,2},{2,3},{3,0},{4,5},{5,6},{6,7},{7,4},{8,9},{9,10},{10,1... | collective-permute-start | bytes 3145736 | tf_op jit(solution)/shard_map/ppermute | solution.py:35
  72.9 12.0 %collective-permute-start.5 = (bf16[16,16,1024]{2,1,0:T(8,128)(2,1)S(1)}, bf16[16,16,1024]{2,1,0:T(8,128)(2,1)}, u32[]{:S(2)}, u32[]{:S(2)}) collective-permute-start(bf16[16,16,1024]{2,1,0:T(8,128)(2,1)S(1)} %collective-permute-done.3.refs_4_), channel_id=1, source_target_pairs={{0,32},{1,33},{2,34},{3,35},{4,36},{5,37},{6,38},{7,39},{8,40},{9,... | collective-permute-start | bytes 1572872 | tf_op jit(solution)/shard_map/ppermute | solution.py:35
  74.5 19.9 %copy-start = (bf16[1024,512]{1,0:T(8,128)(2,1)}, bf16[1024,512]{1,0:T(8,128)(2,1)S(1)}, u32[]{:S(2)}) copy-start(bf16[1024,512]{1,0:T(8,128)(2,1)S(1)} %collective-permute-done.19.refs_18_) | copy-start | bytes 3145732
  74.5 14.5 %collective-permute-start.4 = (bf16[16,16,1024]{2,1,0:T(8,128)(2,1)}, bf16[16,16,1024]{2,1,0:T(8,128)(2,1)}, u32[]{:S(2)}, u32[]{:S(2)}) collective-permute-start(bf16[16,16,1024]{2,1,0:T(8,128)(2,1)} %collective-permute-done.2.refs_3_), channel_id=1, source_target_pairs={{0,32},{1,33},{2,34},{3,35},{4,36},{5,37},{6,38},{7,39},{8,40},{9,... | collective-permute-start | bytes 1572872 | tf_op jit(solution)/shard_map/ppermute | solution.py:35
  84.2 11.8 %collective-permute-start.10 = (bf16[16,16,1024]{2,1,0:T(8,128)(2,1)S(1)}, bf16[16,16,1024]{2,1,0:T(8,128)(2,1)S(1)}, u32[]{:S(2)}, u32[]{:S(2)}) collective-permute-start(bf16[16,16,1024]{2,1,0:T(8,128)(2,1)S(1)} %collective-permute-done.3.refs_4_), channel_id=1, source_target_pairs={{0,16},{1,17},{2,18},{3,19},{4,20},{5,21},{6,22},{7,23},{8,24},{9,... | collective-permute-start | bytes 1572872 | tf_op jit(solution)/shard_map/ppermute | solution.py:35
  85.0 11.8 %collective-permute-start.7 = (bf16[16,16,1024]{2,1,0:T(8,128)(2,1)}, bf16[16,16,1024]{2,1,0:T(8,128)(2,1)}, u32[]{:S(2)}, u32[]{:S(2)}) collective-permute-start(bf16[16,16,1024]{2,1,0:T(8,128)(2,1)} %collective-permute-done.5.refs_6_), channel_id=1, source_target_pairs={{0,32},{1,33},{2,34},{3,35},{4,36},{5,37},{6,38},{7,39},{8,40},{9,... | collective-permute-start | bytes 1572872 | tf_op jit(solution)/shard_map/ppermute | solution.py:35
  89.0 11.2 %collective-permute-start.6 = (bf16[16,16,1024]{2,1,0:T(8,128)(2,1)}, bf16[16,16,1024]{2,1,0:T(8,128)(2,1)}, u32[]{:S(2)}, u32[]{:S(2)}) collective-permute-start(bf16[16,16,1024]{2,1,0:T(8,128)(2,1)} %collective-permute-done.4.refs_5_), channel_id=1, source_target_pairs={{0,32},{1,33},{2,34},{3,35},{4,36},{5,37},{6,38},{7,39},{8,40},{9,... | collective-permute-start | bytes 1572872 | tf_op jit(solution)/shard_map/ppermute | solution.py:35
  94.4 1.5 copy-start.4
  94.4 5.9 %collective-permute-start.9 = (bf16[16,16,1024]{2,1,0:T(8,128)(2,1)}, bf16[16,16,1024]{2,1,0:T(8,128)(2,1)}, u32[]{:S(2)}, u32[]{:S(2)}) collective-permute-start(bf16[16,16,1024]{2,1,0:T(8,128)(2,1)} %collective-permute-done.2.refs_3_), channel_id=1, source_target_pairs={{0,16},{1,17},{2,18},{3,19},{4,20},{5,21},{6,22},{7,23},{8,24},{9,... | collective-permute-start | bytes 1572872 | tf_op jit(solution)/shard_map/ppermute | solution.py:35
  95.5 6.0 %collective-permute-start.12 = (bf16[16,16,1024]{2,1,0:T(8,128)(2,1)}, bf16[16,16,1024]{2,1,0:T(8,128)(2,1)}, u32[]{:S(2)}, u32[]{:S(2)}) collective-permute-start(bf16[16,16,1024]{2,1,0:T(8,128)(2,1)} %collective-permute-done.5.refs_6_), channel_id=1, source_target_pairs={{0,16},{1,17},{2,18},{3,19},{4,20},{5,21},{6,22},{7,23},{8,24},{9,... | collective-permute-start | bytes 1572872 | tf_op jit(solution)/shard_map/ppermute | solution.py:35
  96.7 6.8 %collective-permute-start.11 = (bf16[16,16,1024]{2,1,0:T(8,128)(2,1)}, bf16[16,16,1024]{2,1,0:T(8,128)(2,1)}, u32[]{:S(2)}, u32[]{:S(2)}) collective-permute-start(bf16[16,16,1024]{2,1,0:T(8,128)(2,1)} %collective-permute-done.4.refs_5_), channel_id=1, source_target_pairs={{0,16},{1,17},{2,18},{3,19},{4,20},{5,21},{6,22},{7,23},{8,24},{9,... | collective-permute-start | bytes 1572872 | tf_op jit(solution)/shard_map/ppermute | solution.py:35
  96.8 6.8 %collective-permute-start.14 = (bf16[16,16,1024]{2,1,0:T(8,128)(2,1)}, bf16[16,16,1024]{2,1,0:T(8,128)(2,1)}, u32[]{:S(2)}, u32[]{:S(2)}) collective-permute-start(bf16[16,16,1024]{2,1,0:T(8,128)(2,1)} %collective-permute-done.7.refs_8_), channel_id=1, source_target_pairs={{0,16},{1,17},{2,18},{3,19},{4,20},{5,21},{6,22},{7,23},{8,24},{9,... | collective-permute-start | bytes 1572872 | tf_op jit(solution)/shard_map/ppermute | solution.py:35
  100.3 3.3 %collective-permute-start.13 = (bf16[16,16,1024]{2,1,0:T(8,128)(2,1)}, bf16[16,16,1024]{2,1,0:T(8,128)(2,1)}, u32[]{:S(2)}, u32[]{:S(2)}) collective-permute-start(bf16[16,16,1024]{2,1,0:T(8,128)(2,1)} %collective-permute-done.6.refs_7_), channel_id=1, source_target_pairs={{0,16},{1,17},{2,18},{3,19},{4,20},{5,21},{6,22},{7,23},{8,24},{9,... | collective-permute-start | bytes 1572872 | tf_op jit(solution)/shard_map/ppermute | solution.py:35
  100.3 26.9 %collective-permute-start.23 = (bf16[1024,512]{1,0:T(8,128)(2,1)}, bf16[1024,512]{1,0:T(8,128)(2,1)S(1)}, u32[]{:S(2)}, u32[]{:S(2)}) collective-permute-start(bf16[1024,512]{1,0:T(8,128)(2,1)} %copy-done), channel_id=1, source_target_pairs={{0,1},{1,2},{2,3},{3,0},{4,5},{5,6},{6,7},{7,4},{8,9},{9,10},{10,1... | collective-permute-start | bytes 3145736 | tf_op jit(solution)/shard_map/ppermute | solution.py:35
  101.5 25.7 %collective-permute-start.24 = (bf16[1024,512]{1,0:T(8,128)(2,1)}, bf16[1024,512]{1,0:T(8,128)(2,1)S(1)}, u32[]{:S(2)}, u32[]{:S(2)}) collective-permute-start(bf16[1024,512]{1,0:T(8,128)(2,1)} %copy-done.4), channel_id=1, source_target_pairs={{0,3},{1,0},{2,1},{3,2},{4,7},{5,4},{6,5},{7,6},{8,11},{9,8},{10,9... | collective-permute-start | bytes 3145736 | tf_op jit(solution)/shard_map/ppermute | solution.py:35
  103.6 1.2 copy-start.1
  104.8 1.2 copy-start.3
  106.1 1.2 copy-start.5
  107.3 1.2 copy-start.7
  108.5 1.0 copy-start.9
  109.6 1.0 copy-start.11
  110.6 1.0 copy-start.13
  111.6 1.0 copy-start.15
  131.7 1.3 collective-permute-start.25
  149.9 1.3 collective-permute-start.26
  173.6 1.3 collective-permute-start.27
  188.5 1.3 collective-permute-start.29
  190.6 11.9 %all-to-all-start.6 = ((f32[16,24,128]{2,1,0:T(8,128)}), f32[16,24,128]{2,1,0:T(8,128)S(1)}, u32[]{:S(2)}, u32[]{:S(2)}) async-start(f32[16,24,128]{2,1,0:T(8,128)} %broadcast_in_dim.14), calls=%async_computation.6 | async-start | bytes 393216 | tf_op jit(solution)/shard_map/all_to_all | solution.py:220
  194.3 1.2 collective-permute-start.28
  (5 other events, 4.4 us)

commit v2 on v1

--- a/solution.py
+++ b/solution.py
@@ -126,31 +126,42 @@
 
 
 def tile_a_kernel(index, *refs):
-    columns, rows, prior = refs[:16], refs[16:22], refs[22]
-    total, ahead, left, stage, prior_sem, left_sem, stage_sem, ahead_sem = refs[23:]
+    columns, rows, prior, spread = refs[:16], refs[16:22], refs[22], refs[23]
+    total, ahead, image, left, stage, prior_sem, left_sem, stage_sem, ahead_sem = refs[24:]
+
+    def fetch_row(i):
+        return pltpu.make_async_copy(rows[i], left.at[i, pl.ds(0, 1024)], left_sem.at[i])
+
     for i in range(2):
-        pltpu.make_async_copy(rows[i], left.at[i], left_sem.at[i]).start()
+        fetch_row(i).start()
         fetch_columns(index, columns, stage.at[i], stage_sem.at[i], 2 * i)
     from_prior = pltpu.make_async_copy(prior, total, prior_sem)
     from_prior.start()
     for i in range(2, 6):
-        pltpu.make_async_copy(rows[i], left.at[i], left_sem.at[i]).start()
+        fetch_row(i).start()
         fetch_columns(index, columns, stage.at[i], stage_sem.at[i], 2 * i)
     for i in range(2):
         fetch_columns(index, columns, ahead.at[pl.ds(512 * i, 512)], ahead_sem.at[i], 12 + 2 * i)
+    for i in range(6):
+        for t in range(2):
+            left[i, 1024:1056, 256 * t : 256 * (t + 1)] = spread[index[2 * i + t]]
     for group in range(3):
         for i in (2 * group, 2 * group + 1):
-            pltpu.make_async_copy(rows[i], left.at[i], left_sem.at[i]).wait()
+            fetch_row(i).wait()
             pltpu.make_async_copy(stage.at[i], stage.at[i], stage_sem.at[i]).wait()
         if group == 0:
             from_prior.wait()
 
         def step(n, carry, group=group):
             at = pl.ds(pl.multiple_of(n * 256, 256), 256)
-            product = jnp.zeros((1024, 256), F32)
+            product = jnp.zeros((1056, 256), F32)
             for i in (2 * group, 2 * group + 1):
                 product += jnp.dot(left[i], stage[i, :, at], preferred_element_type=F32)
-            total[:, at] += product * (1.0 / M)
+            total[:, at] += product[:1024] * (1.0 / M)
+            if group == 0:
+                image[:, at] = product[1024:]
+            else:
+                image[:, at] += product[1024:]
             return carry
 
         lax.fori_loop(0, 4, step, 0)
@@ -159,14 +170,18 @@
         pltpu.make_async_copy(part, part, ahead_sem.at[i]).wait()
 
 
-def tile_a(index, columns, rows, prior):
+def tile_a(index, columns, rows, prior, spread):
     return pl.pallas_call(
         tile_a_kernel,
-        in_specs=[SMEM] + [ANY] * 23,
-        out_specs=[VMEM] * 2,
-        out_shape=[jax.ShapeDtypeStruct((1024, 1024), F32), jax.ShapeDtypeStruct((1024, 1024), BF16)],
+        in_specs=[SMEM] + [ANY] * 23 + [VMEM],
+        out_specs=[VMEM] * 3,
+        out_shape=[
+            jax.ShapeDtypeStruct((1024, 1024), F32),
+            jax.ShapeDtypeStruct((1024, 1024), BF16),
+            jax.ShapeDtypeStruct((32, 1024), F32),
+        ],
         scratch_shapes=[
-            pltpu.VMEM((6, 1024, 512), BF16),
+            pltpu.VMEM((6, 1056, 512), BF16),
             pltpu.VMEM((6, 512, 1024), BF16),
             pltpu.SemaphoreType.DMA,
             pltpu.SemaphoreType.DMA((6,)),
@@ -176,10 +191,15 @@
         compiler_params=pltpu.CompilerParams(vmem_limit_bytes=32 * 2**20),
         cost_estimate=pl.CostEstimate(flops=6 * 2**30, bytes_accessed=18 * 2**20, transcendentals=0),
         name="tile_a",
-    )(index, *columns, *rows, prior)
-
-
-def tile_b_kernel(partial, ahead, row0, row1, start, out, rounded, image, total, out_sem):
+    )(index, *columns, *rows, prior, spread)
+
+
+def tile_b_kernel(
+    index, partial, ahead, row0, row1, spread, so_far, first, out, rounded, image, total, left, out_sem
+):
+    for t in range(4):
+        left[:, 256 * t : 256 * (t + 1)] = spread[index[12 + t]]
+
     def step(n, carry):
         at = pl.ds(pl.multiple_of(n * 256, 256), 256)
         product = jnp.dot(row0[...], ahead[:512, at], preferred_element_type=F32)
@@ -188,7 +208,8 @@
         total[:, at] = value
         pltpu.make_async_copy(total.at[:, at], out.at[:, at], out_sem.at[n]).start()
         rounded[:, at] = value.astype(BF16)
-        image[:, at] = jnp.dot(start[...], value.astype(BF16), preferred_element_type=F32)
+        rest = so_far[:, at] + jnp.dot(left[...], ahead[:, at], preferred_element_type=F32)
+        image[:, at] = first[:, at] + rest[:K] * (1.0 / M)
         return carry
 
     lax.fori_loop(0, 4, step, 0)
@@ -197,21 +218,25 @@
         pltpu.make_async_copy(total.at[:, at], out.at[:, at], out_sem.at[n]).wait()
 
 
-def tile_b(partial, ahead, row0, row1, start):
+def tile_b(index, partial, ahead, row0, row1, spread, so_far, first):
     return pl.pallas_call(
         tile_b_kernel,
-        in_specs=[VMEM] * 5,
+        in_specs=[SMEM] + [VMEM] * 7,
         out_specs=[ANY, VMEM, VMEM],
         out_shape=[
             jax.ShapeDtypeStruct((1024, 1024), F32),
             jax.ShapeDtypeStruct((1024, 1024), BF16),
             jax.ShapeDtypeStruct((K, 1024), F32),
         ],
-        scratch_shapes=[pltpu.VMEM((1024, 1024), F32), pltpu.SemaphoreType.DMA((4,))],
+        scratch_shapes=[
+            pltpu.VMEM((1024, 1024), F32),
+            pltpu.VMEM((32, 1024), BF16),
+            pltpu.SemaphoreType.DMA((4,)),
+        ],
         compiler_params=pltpu.CompilerParams(vmem_limit_bytes=20 * 2**20),
         cost_estimate=pl.CostEstimate(flops=2 * 2**30, bytes_accessed=14 * 2**20, transcendentals=0),
         name="tile_b",
-    )(partial, ahead, row0, row1, start)
+    )(index, partial, ahead, row0, row1, spread, so_far, first)
 
 
 def bcast_sum(array, axis):
@@ -335,6 +360,19 @@
             up.append(swap_core(b))
     columns = down + up
 
+    start = (start_vectors.T / jnp.sqrt(F32(S))).astype(BF16)
+    parts = [
+        dot_t(start, prior.astype(BF16), ((1,), (0,))),
+        dot_t(start, piece.reshape(256, 1024), ((1,), (1,))),
+    ]
+    early = row_sum(jnp.concatenate(parts, axis=1))
+    spread = jnp.pad(early[:, 1024:], ((0, 32 - K), (0, 0))).astype(BF16)
+    spread = lax.all_to_all(jnp.broadcast_to(spread[None], (16, 32, 256)), COL, 0, 0, tiled=True)
+    at = jnp.arange(256, dtype=jnp.int32)
+    moved = jnp.broadcast_to(order[:, None], (16, 16)).reshape(1, 256) * 16 + at[None] % 16
+    moved = (at[:, None] == moved).astype(BF16)
+    spread = dot_t(spread.reshape(512, 256), moved, ((1,), (0,))).astype(BF16)
+    spread = spread.reshape(16, 32, 256)
     piece = turn(order, piece)
     f = first_axis(piece, 1)
     g = first_axis(piece, -1)
@@ -348,11 +386,11 @@
     g1 = second_axis(h1, -1)
     last0 = second_axis(f0, 1)
     last1 = second_axis(g1, -1)
-    partial, ahead = tile_a(index, columns, [h0, h1, f0, f1, g0, g1], prior)
-    start = (start_vectors.T / jnp.sqrt(F32(S))).astype(BF16)
+    partial, ahead, so_far = tile_a(index, columns, [h0, h1, f0, f1, g0, g1], prior, spread)
     ahead, last0, last1 = lax.optimization_barrier((ahead, last0, last1))
-    grm, rounded, image = tile_b(partial, ahead, last0, last1, start)
-    image = row_sum(image)
+    grm, rounded, image = tile_b(
+        index, partial, ahead, last0, last1, spread, so_far, early[:, :1024]
+    )
     gram1 = dot_t(image, image, ((1,), (1,)))
     packed = with_gram(dot_t(image.astype(BF16), rounded, ((1,), (1,))), gram1)
     packed = bcast_sum(packed, "x").astype(BF16)

time: 207 us -> 212 us (1.024)
  blocking collectives: 71.8 us -> 32.8 us
  waiting for transfers between devices: 50.2 us -> 65.2 us
  local copies, waits for them, and re-layouts: 14.8 us -> 26.2 us
  starting transfers between devices: 36.6 us -> 47.1 us
  matrix products: 1.47 us -> 4.53 us
  other arithmetic: 0.87 us -> 3.6 us
    all_to_all x1 -> x0, blocking collectives: 22.8 us -> none  [body(): piece = lax.all_to_all(standard, ROW, 0, 0, tiled=True)]
    all_to_all x4 -> x3, blocking collectives: 49 us -> 32.8 us  [bcast_sum(): lax.all_to_all(copies, axis, 0, 0, tiled=True).astype(F32).sum(axis=0)]
    all_to_all x0 -> x2, waiting for transfers between devices: none -> 15.5 us  [the longest x1 11.6 us: body(): piece = lax.all_to_all(standard, ROW, 0, 0, tiled=True)]
    all_to_all x0 -> x2, starting transfers between devices: none -> 12.1 us  [the longest x1 8.59 us: body(): piece = lax.all_to_all(standard, ROW, 0, 0, tiled=True)]
    ppermute x30, waiting for transfers between devices: 33.9 us -> 23.5 us  [send(): return lax.ppermute(array, ALL, pairs)]
    all_to_all x1 -> x2, waiting for transfers between devices: 7.05 us -> 14.7 us  [bcast_sum(): lax.all_to_all(copies, axis, 0, 0, tiled=True).astype(F32).sum(axis=0)]
    unnamed x42 -> x54, local copies, waits for them, and re-layouts: 13.5 us -> 19.7 us
    ppermute x30, starting transfers between devices: 26 us -> 20.1 us  [send(): return lax.ppermute(array, ALL, pairs)]
  transfers between devices with their start and end apart: 32 -> 35, of which waited for: 14 -> 14; matrix products, arithmetic and copies ran while one was open for 0% -> 6% of each run, Pallas kernels for 7% -> 7%
where the time goes in v2:
time: 212 us; the launch traced here: 209 us
  waiting for transfers between devices  65.2 us (31%)
  starting transfers between devices  47.1 us (22%)
  blocking collectives  32.8 us (15%)
  Pallas kernels  28.6 us (13%)
  local copies, waits for them, and re-layouts  26.2 us (12%)
  matrix products  4.53 us (2%)
  other arithmetic  3.6 us (2%)
    all_to_all x3, blocking collectives, bcast_sum(): lax.all_to_all(copies, axis, 0, 0, tiled=True).astype(F32).sum(axis=0)  32.8 us
    ppermute x30, waiting for transfers between devices, send(): return lax.ppermute(array, ALL, pairs)  23.5 us
    ppermute x30, starting transfers between devices, send(): return lax.ppermute(array, ALL, pairs)  20.1 us
    unnamed x54, local copies, waits for them, and re-layouts  19.7 us
    all_to_all x2, waiting for transfers between devices, bcast_sum(): lax.all_to_all(copies, axis, 0, 0, tiled=True).astype(F32).sum(axis=0)  14.7 us
    pallas_call x1, Pallas kernels, tile_a(): pl.pallas_call(tile_a_kernel, in_specs=[SMEM] + [ANY] * 23 + [VMEM], out_...  14.7 us
    all_to_all x1, waiting for transfers between devices, body(): piece = lax.all_to_all(standard, ROW, 0, 0, tiled=True)  11.6 us
    all_to_all x1, waiting for transfers between devices, body(): own = lax.all_to_all(standard, COL, 0, 0, tiled=True)  11.5 us
  transfers between devices with their start and end apart: 35, of which 14 were waited for; matrix products, arithmetic and copies ran while one was open for 6% of the time, Pallas kernels for 7%

profile of v2, /device:TPU:32, one launch (start us, length us, event | category | flops | bytes accessed | tf_op | source)
XLA Modules:
  0.0 209.1 jit_solution(7052528745846351673)
XLA Ops:
  0.7 4.4 %standardize.1 = bf16[16,16,1024]{2,1,0:T(8,128)(2,1)} custom-call(s32[16]{0:T(128)} %index.1, f32[128,128]{1,0:T(8,128)} %bitcast.26, s32[16,16384]{1,0:T(8,128)} %genotypes.1), custom_call_target="tpu_custom_call" | custom-call | tf_op jit(solution)/shard_map/standardize/pallas_call | solution.py:83
  5.1 8.6 %all-to-all-start = ((bf16[16,16,1024]{2,1,0:T(8,128)(2,1)}), bf16[16,16,1024]{2,1,0:T(8,128)(2,1)S(1)}, u32[]{:S(2)}, u32[]{:S(2)}) async-start(bf16[16,16,1024]{2,1,0:T(8,128)(2,1)} %standardize.1), calls=%async_computation | async-start | bytes 1048576 | tf_op jit(solution)/shard_map/all_to_all | solution.py:348
  13.7 2.6 %fusion = f32[20,1024]{1,0:T(8,128)S(1)} fusion(f32[1024,1024]{1,0:T(8,128)} %refs_22_.1, f32[1024,20]{0,1:T(8,128)S(1)} %copy-done.22), kind=kOutput, calls=%fused_computation | convolution fusion | flops 43032576 | bytes 4358144 | tf_op jit(solution)/shard_map/dot_general | solution.py:283
  16.3 11.6 %all-to-all-done.piece = bf16[16,16,1024]{2,1,0:T(8,128)(2,1)S(1)} async-done(((bf16[16,16,1024]{2,1,0:T(8,128)(2,1)}), bf16[16,16,1024]{2,1,0:T(8,128)(2,1)S(1)}, u32[]{:S(2)}, u32[]{:S(2)}) %all-to-all-start) | async-done | bytes 524320 | tf_op jit(solution)/shard_map/all_to_all | solution.py:348
  28.6 1.6 collective-permute-start.15
  30.2 6.7 %all-to-all-start.1 = ((bf16[16,16,1024]{2,1,0:T(8,128)(2,1)}), bf16[16,16,1024]{2,1,0:T(8,128)(2,1)S(1)}, u32[]{:S(2)}, u32[]{:S(2)}) async-start(bf16[16,16,1024]{2,1,0:T(8,128)(2,1)} %standardize.1), calls=%async_computation.1 | async-start | bytes 1048576 | tf_op jit(solution)/shard_map/all_to_all | solution.py:350
  37.3 11.5 %all-to-all-done.1.refs_0_ = bf16[16,16,1024]{2,1,0:T(8,128)(2,1)S(1)} async-done(((bf16[16,16,1024]{2,1,0:T(8,128)(2,1)}), bf16[16,16,1024]{2,1,0:T(8,128)(2,1)S(1)}, u32[]{:S(2)}, u32[]{:S(2)}) %all-to-all-start.1) | async-done | bytes 524320 | tf_op jit(solution)/shard_map/all_to_all | solution.py:350
  48.9 1.8 collective-permute-start.1
  52.0 4.7 %all-to-all-start.2 = ((bf16[8,20,640]{2,1,0:T(8,128)(2,1)}), bf16[8,20,640]{2,1,0:T(8,128)(2,1)S(1)}, u32[]{:S(2)}, u32[]{:S(2)}) async-start(bf16[8,20,640]{2,1,0:T(8,128)(2,1)} %broadcast_in_dim.14), calls=%async_computation.2 | async-start | bytes 491520 | tf_op jit(solution)/shard_map/all_to_all | solution.py:245
  56.6 1.3 collective-permute-start.16
  58.0 1.1 pad_maximum_fusion.refs_16_
  59.7 7.6 %all-to-all-done.2 = bf16[8,20,640]{2,1,0:T(8,128)(2,1)S(1)} async-done(((bf16[8,20,640]{2,1,0:T(8,128)(2,1)}), bf16[8,20,640]{2,1,0:T(8,128)(2,1)S(1)}, u32[]{:S(2)}, u32[]{:S(2)}) %all-to-all-start.2) | async-done | bytes 204832 | tf_op jit(solution)/shard_map/all_to_all | solution.py:245
  70.6 3.3 %collective-permute-start.18 = (bf16[512,256]{1,0:T(8,128)(2,1)S(1)}, bf16[512,256]{1,0:T(8,128)(2,1)S(1)}, u32[]{:S(2)}, u32[]{:S(2)}) collective-permute-start(bf16[512,256]{1,0:T(8,128)(2,1)S(1)} %slice.62), channel_id=1, source_target_pairs={{0,12},{1,13},{2,14},{3,15},{4,0},{5,1},{6,2},{7,3},{8,4},{9,5},{1... | collective-permute-start | bytes 786440 | tf_op jit(solution)/shard_map/ppermute | solution.py:35
  73.9 3.3 %collective-permute-done.17 = bf16[512,256]{1,0:T(8,128)(2,1)S(1)} collective-permute-done((bf16[512,256]{1,0:T(8,128)(2,1)S(1)}, bf16[512,256]{1,0:T(8,128)(2,1)S(1)}, u32[]{:S(2)}, u32[]{:S(2)}) %collective-permute-start.17) | collective-permute-done | bytes 262176 | tf_op jit(solution)/shard_map/ppermute | solution.py:35
  78.0 1.1 maximum_maximum_fusion.refs_17_
  79.1 2.6 %collective-permute-start.22 = (bf16[1024,512]{1,0:T(8,128)(2,1)S(1)}, bf16[1024,512]{1,0:T(8,128)(2,1)S(1)}, u32[]{:S(2)}, u32[]{:S(2)}) collective-permute-start(bf16[1024,512]{1,0:T(8,128)(2,1)S(1)} %maximum_maximum_fusion.refs_17_), channel_id=1, source_target_pairs={{0,3},{1,0},{2,1},{3,2},{4,7},{5,4},{6,5},{7,6},{8,11},{9,8},{10,9... | collective-permute-start | bytes 3145736 | tf_op jit(solution)/shard_map/ppermute | solution.py:35
  85.1 1.1 collective-permute-start.4
  86.1 5.8 %collective-permute-done.21.refs_20_ = bf16[1024,512]{1,0:T(8,128)(2,1)S(1)} collective-permute-done((bf16[1024,512]{1,0:T(8,128)(2,1)S(1)}, bf16[1024,512]{1,0:T(8,128)(2,1)S(1)}, u32[]{:S(2)}, u32[]{:S(2)}) %collective-permute-start.21) | collective-permute-done | bytes 1048608 | tf_op jit(solution)/shard_map/ppermute | solution.py:35
  92.9 1.6 collective-permute-done.5.refs_6_
  94.5 5.7 %collective-permute-done.4.refs_5_ = bf16[16,16,1024]{2,1,0:T(8,128)(2,1)} collective-permute-done((bf16[16,16,1024]{2,1,0:T(8,128)(2,1)}, bf16[16,16,1024]{2,1,0:T(8,128)(2,1)}, u32[]{:S(2)}, u32[]{:S(2)}) %collective-permute-start.4) | collective-permute-done | bytes 524320 | tf_op jit(solution)/shard_map/ppermute | solution.py:35
  100.2 3.0 %collective-permute-done.22.refs_21_ = bf16[1024,512]{1,0:T(8,128)(2,1)S(1)} collective-permute-done((bf16[1024,512]{1,0:T(8,128)(2,1)S(1)}, bf16[1024,512]{1,0:T(8,128)(2,1)S(1)}, u32[]{:S(2)}, u32[]{:S(2)}) %collective-permute-start.22) | collective-permute-done | bytes 1048608 | tf_op jit(solution)/shard_map/ppermute | solution.py:35
  103.2 1.0 copy-done.8
  108.3 3.5 %all-to-all-start.3 = ((bf16[16,32,256]{2,1,0:T(8,128)(2,1)}), bf16[16,32,256]{2,1,0:T(8,128)(2,1)S(1)}, u32[]{:S(2)}, u32[]{:S(2)}) async-start(bf16[16,32,256]{2,1,0:T(8,128)(2,1)} %broadcast_in_dim.15), calls=%async_computation.3 | async-start | bytes 524288 | tf_op jit(solution)/shard_map/all_to_all | solution.py:370
  113.7 1.5 collective-permute-start.25
  115.2 1.7 collective-permute-start.26
  117.9 3.9 %all-to-all-done.3 = bf16[16,32,256]{2,1,0:T(8,128)(2,1)S(1)} async-done(((bf16[16,32,256]{2,1,0:T(8,128)(2,1)}), bf16[16,32,256]{2,1,0:T(8,128)(2,1)S(1)}, u32[]{:S(2)}, u32[]{:S(2)}) %all-to-all-start.3) | async-done | bytes 262176 | tf_op jit(solution)/shard_map/all_to_all | solution.py:370
  122.1 1.2 copy-done.3
  123.3 1.0 copy-done.5
  124.3 1.2 copy-done.7
  125.6 1.2 copy-done.9
  126.8 1.2 copy-done.11
  128.0 1.0 copy-done.13
  129.1 1.0 copy-done.15
  130.1 1.0 copy-done.17
  131.1 1.0 copy-done.19
  132.2 1.0 copy-done.21
  133.2 14.7 %tile_a.1 = (f32[1024,1024]{1,0:T(8,128)S(1)}, bf16[1024,1024]{1,0:T(8,128)(2,1)S(1)}, f32[32,1024]{1,0:T(8,128)S(1)}) custom-call(s32[16]{0:T(128)S(1)} %fusion.16.index, bf16[16,16,1024]{2,1,0:T(8,128)(2,1)S(1)} %copy-done.5, bf16[16,16,1024]{2,1,0:T(8,128)(2,1)S(1)} %copy-done.15, bf16[16,16,1024]{2,1,0:T(8,128)(2,1)S(1)} %copy-done.13, ...), custom_call_target="tpu_custom_call" | custom-call | flops 6442450944 | bytes 18874368 | tf_op jit(solution)/shard_map/tile_a/pallas_call | solution.py:174
  148.9 1.2 copy-done.1
  150.1 4.8 %tile_b.1 = (f32[1024,1024]{1,0:T(8,128)}, bf16[1024,1024]{1,0:T(8,128)(2,1)S(1)}, f32[20,1024]{1,0:T(8,128)S(1)}) custom-call(s32[16]{0:T(128)S(1)} %fusion.16.index, f32[1024,1024]{1,0:T(8,128)S(1)} %get-tuple-element.20.partial, bf16[1024,1024]{1,0:T(8,128)(2,1)S(1)} %get-tuple-element.22.ahead, bf16[1024,512]{1,0:T(8,128)(2,1)S(1)} %collective-permute-done.25.row0, ...), custom_call_target="tpu_custom_call" | custom-call | flops 2147483648 | bytes 14680064 | tf_op jit(solution)/shard_map/tile_b/pallas_call | solution.py:222
  156.0 8.7 %all_to_all.40 = bf16[4,24,1024]{2,1,0:T(8,128)(2,1)S(1)} all-to-all(bf16[4,24,1024]{2,1,0:T(8,128)(2,1)S(1)} %broadcast_in_dim.17), channel_id=1, replica_groups=mesh['z'=8,'core'=2,'x'=4,'y'=4] {'x'}, dimensions={0} | all-to-all | bytes 393216 | tf_op jit(solution)/shard_map/all_to_all | solution.py:245
  164.8 8.7 %all_to_all.41 = bf16[4,24,1024]{2,1,0:T(8,128)(2,1)S(1)} all-to-all(bf16[4,24,1024]{2,1,0:T(8,128)(2,1)S(1)} %broadcast_in_dim.18), channel_id=1, replica_groups=mesh['z'=8,'core'=2,'x'=4,'y'=4] {'y'}, dimensions={0} | all-to-all | bytes 393216 | tf_op jit(solution)/shard_map/all_to_all | solution.py:245
  173.7 1.6 solve.1
  177.2 15.4 %all_to_all.42 = bf16[8,24,512]{2,1,0:T(8,128)(2,1)S(1)} all-to-all(bf16[8,24,512]{2,1,0:T(8,128)(2,1)S(1)} %broadcast_in_dim.19), channel_id=1, replica_groups=mesh['z'=8,'core'=2,'x'=4,'y'=4] {'z'}, dimensions={0} | all-to-all | bytes 393216 | tf_op jit(solution)/shard_map/all_to_all | solution.py:245
  192.8 1.2 collective-permute-done.29
  194.8 3.5 %all-to-all-start.7 = ((f32[16,24,128]{2,1,0:T(8,128)}), f32[16,24,128]{2,1,0:T(8,128)S(1)}, u32[]{:S(2)}, u32[]{:S(2)}) async-start(f32[16,24,128]{2,1,0:T(8,128)} %broadcast_in_dim.20), calls=%async_computation.7 | async-start | bytes 393216 | tf_op jit(solution)/shard_map/all_to_all | solution.py:245
  198.7 1.0 collective-permute-done.28
  199.7 7.1 %all-to-all-done.7 = f32[16,24,128]{2,1,0:T(8,128)S(1)} async-done(((f32[16,24,128]{2,1,0:T(8,128)}), f32[16,24,128]{2,1,0:T(8,128)S(1)}, u32[]{:S(2)}, u32[]{:S(2)}) %all-to-all-start.7) | async-done | bytes 196640 | tf_op jit(solution)/shard_map/all_to_all | solution.py:245
  206.8 2.3 %last.1 = (f32[20,1024]{1,0:T(8,128)}, f32[3,20]{1,0:T(4,128)}) custom-call(f32[1,20]{1,0:T(1,128)S(1)} %get-tuple-element.29.first, f32[20,20]{1,0:T(8,128)S(1)} %add.110.gram2, f32[20,20]{1,0:T(8,128)S(1)} %bitcast.22, f32[20,1024]{1,0:T(8,128)S(1)} %maximum_select_fusion.1.wide), custom_call_target="tpu_custom_call" | custom-call | tf_op jit(solution)/shard_map/last/pallas_call | solution.py:325
  (136 shorter events, 24.0 us)
Async XLA Ops:
  0.6 13.1 %copy-start.23 = (s32[16]{0:T(128)S(1)}, s32[16]{0:T(128)}, u32[]{:S(2)}) copy-start(s32[16]{0:T(128)} %constant.98.clone) | copy-start | bytes 196
  0.6 13.0 %copy-start.24 = (s32[16]{0:T(128)S(1)}, s32[16]{0:T(128)}, u32[]{:S(2)}) copy-start(s32[16]{0:T(128)} %constant.99.clone) | copy-start | bytes 196
  0.7 13.1 %copy-start.22 = (f32[1024,20]{0,1:T(8,128)S(1)}, f32[1024,20]{0,1:T(8,128)}, u32[]{:S(2)}) copy-start(f32[1024,20]{0,1:T(8,128)} %param.13) | copy-start | bytes 245764
  5.1 22.8 %all-to-all-start = ((bf16[16,16,1024]{2,1,0:T(8,128)(2,1)}), bf16[16,16,1024]{2,1,0:T(8,128)(2,1)S(1)}, u32[]{:S(2)}, u32[]{:S(2)}) async-start(bf16[16,16,1024]{2,1,0:T(8,128)(2,1)} %standardize.1), calls=%async_computation | async-start | bytes 1048576 | tf_op jit(solution)/shard_map/all_to_all | solution.py:348
  28.6 29.3 %collective-permute-start.15 = (bf16[1024,256]{1,0:T(8,128)(2,1)S(1)}, bf16[1024,256]{1,0:T(8,128)(2,1)}, u32[]{:S(2)}, u32[]{:S(2)}) collective-permute-start(bf16[1024,256]{1,0:T(8,128)(2,1)S(1)} %turn.1), channel_id=1, source_target_pairs={{0,4},{1,5},{2,6},{3,7},{4,8},{5,9},{6,10},{7,11},{8,12},{9,13},{1... | collective-permute-start | bytes 1572872 | tf_op jit(solution)/shard_map/ppermute | solution.py:35
  30.2 18.6 %all-to-all-start.1 = ((bf16[16,16,1024]{2,1,0:T(8,128)(2,1)}), bf16[16,16,1024]{2,1,0:T(8,128)(2,1)S(1)}, u32[]{:S(2)}, u32[]{:S(2)}) async-start(bf16[16,16,1024]{2,1,0:T(8,128)(2,1)} %standardize.1), calls=%async_computation.1 | async-start | bytes 1048576 | tf_op jit(solution)/shard_map/all_to_all | solution.py:350
  37.2 14.0 %collective-permute-start.23 = (f32[20,640]{1,0:T(8,128)S(1)}, f32[20,640]{1,0:T(8,128)S(1)}, u32[]{:S(2)}, u32[]{:S(2)}) collective-permute-start(f32[20,640]{1,0:T(8,128)S(1)} %slice_select_fusion), channel_id=1, source_target_pairs={{0,16},{1,17},{2,18},{3,19},{4,20},{5,21},{6,22},{7,23},{8,24},{9,... | collective-permute-start | bytes 153608 | tf_op jit(solution)/shard_map/ppermute | solution.py:35
  48.9 21.7 %copy-start.4 = (bf16[16,16,1024]{2,1,0:T(8,128)(2,1)}, bf16[16,16,1024]{2,1,0:T(8,128)(2,1)S(1)}, u32[]{:S(2)}) copy-start(bf16[16,16,1024]{2,1,0:T(8,128)(2,1)S(1)} %all-to-all-done.1.refs_0_) | copy-start | bytes 1572868
  48.9 18.7 %collective-permute-start.1 = (bf16[16,16,1024]{2,1,0:T(8,128)(2,1)S(1)}, bf16[16,16,1024]{2,1,0:T(8,128)(2,1)S(1)}, u32[]{:S(2)}, u32[]{:S(2)}) collective-permute-start(bf16[16,16,1024]{2,1,0:T(8,128)(2,1)S(1)} %all-to-all-done.1.refs_0_), channel_id=1, source_target_pairs={{0,32},{1,33},{2,34},{3,35},{4,36},{5,37},{6,38},{7,39},{8,40},{9,... | collective-permute-start | bytes 1572872 | tf_op jit(solution)/shard_map/ppermute | solution.py:35
  50.7 17.1 %collective-permute-start = (bf16[16,16,1024]{2,1,0:T(8,128)(2,1)S(1)}, bf16[16,16,1024]{2,1,0:T(8,128)(2,1)S(1)}, u32[]{:S(2)}, u32[]{:S(2)}) collective-permute-start(bf16[16,16,1024]{2,1,0:T(8,128)(2,1)S(1)} %all-to-all-done.1.refs_0_), channel_id=1, source_target_pairs={{0,16},{1,17},{2,18},{3,19},{4,20},{5,21},{6,22},{7,23},{8,24},{9,... | collective-permute-start | bytes 1572872 | tf_op jit(solution)/shard_map/ppermute | solution.py:35
  52.0 15.4 %all-to-all-start.2 = ((bf16[8,20,640]{2,1,0:T(8,128)(2,1)}), bf16[8,20,640]{2,1,0:T(8,128)(2,1)S(1)}, u32[]{:S(2)}, u32[]{:S(2)}) async-start(bf16[8,20,640]{2,1,0:T(8,128)(2,1)} %broadcast_in_dim.14), calls=%async_computation.2 | async-start | bytes 491520 | tf_op jit(solution)/shard_map/all_to_all | solution.py:245
  56.6 12.9 %collective-permute-start.16 = (bf16[1024,256]{1,0:T(8,128)(2,1)S(1)}, bf16[1024,256]{1,0:T(8,128)(2,1)}, u32[]{:S(2)}, u32[]{:S(2)}) collective-permute-start(bf16[1024,256]{1,0:T(8,128)(2,1)S(1)} %turn.1), channel_id=1, source_target_pairs={{0,12},{1,13},{2,14},{3,15},{4,0},{5,1},{6,2},{7,3},{8,4},{9,5},{1... | collective-permute-start | bytes 1572872 | tf_op jit(solution)/shard_map/ppermute | solution.py:35
  59.1 26.0 %collective-permute-start.19 = (bf16[1024,512]{1,0:T(8,128)(2,1)S(1)}, bf16[1024,512]{1,0:T(8,128)(2,1)}, u32[]{:S(2)}, u32[]{:S(2)}) collective-permute-start(bf16[1024,512]{1,0:T(8,128)(2,1)S(1)} %pad_maximum_fusion.refs_16_), channel_id=1, source_target_pairs={{0,1},{1,2},{2,3},{3,0},{4,5},{5,6},{6,7},{7,4},{8,9},{9,10},{10,1... | collective-permute-start | bytes 3145736 | tf_op jit(solution)/shard_map/ppermute | solution.py:35
  67.5 49.5 %copy-start.25 = (s32[16]{0:T(128)S(1)}, s32[16]{0:T(128)}, u32[]{:S(2)}) copy-start(s32[16]{0:T(128)} %constant.100.clone) | copy-start | bytes 196
  67.5 49.4 %copy-start.26 = (s32[16]{0:T(128)S(1)}, s32[16]{0:T(128)}, u32[]{:S(2)}) copy-start(s32[16]{0:T(128)} %constant.101.clone) | copy-start | bytes 196
  67.5 3.1 %collective-permute-start.24 = (f32[20,640]{1,0:T(8,128)S(1)}, f32[20,640]{1,0:T(8,128)S(1)}, u32[]{:S(2)}, u32[]{:S(2)}) collective-permute-start(f32[20,640]{1,0:T(8,128)S(1)} %convert_reduce_fusion), channel_id=1, source_target_pairs={{0,16},{1,17},{2,18},{3,19},{4,20},{5,21},{6,22},{7,23},{8,24},{9,... | collective-permute-start | bytes 153608 | tf_op jit(solution)/shard_map/ppermute | solution.py:35
  67.6 40.6 %copy-start.12 = (bf16[16,16,1024]{2,1,0:T(8,128)(2,1)}, bf16[16,16,1024]{2,1,0:T(8,128)(2,1)S(1)}, u32[]{:S(2)}) copy-start(bf16[16,16,1024]{2,1,0:T(8,128)(2,1)S(1)} %collective-permute-done.1.refs_2_) | copy-start | bytes 1572868
  67.6 11.5 %collective-permute-start.3 = (bf16[16,16,1024]{2,1,0:T(8,128)(2,1)S(1)}, bf16[16,16,1024]{2,1,0:T(8,128)(2,1)}, u32[]{:S(2)}, u32[]{:S(2)}) collective-permute-start(bf16[16,16,1024]{2,1,0:T(8,128)(2,1)S(1)} %collective-permute-done.1.refs_2_), channel_id=1, source_target_pairs={{0,32},{1,33},{2,34},{3,35},{4,36},{5,37},{6,38},{7,39},{8,40},{9,... | collective-permute-start | bytes 1572872 | tf_op jit(solution)/shard_map/ppermute | solution.py:35
  67.7 40.5 %copy-start.14 = (bf16[16,16,1024]{2,1,0:T(8,128)(2,1)}, bf16[16,16,1024]{2,1,0:T(8,128)(2,1)S(1)}, u32[]{:S(2)}) copy-start(bf16[16,16,1024]{2,1,0:T(8,128)(2,1)S(1)} %collective-permute-done.refs_1_) | copy-start | bytes 1572868
  67.7 14.9 %collective-permute-start.2 = (bf16[16,16,1024]{2,1,0:T(8,128)(2,1)S(1)}, bf16[16,16,1024]{2,1,0:T(8,128)(2,1)}, u32[]{:S(2)}, u32[]{:S(2)}) collective-permute-start(bf16[16,16,1024]{2,1,0:T(8,128)(2,1)S(1)} %collective-permute-done.refs_1_), channel_id=1, source_target_pairs={{0,32},{1,33},{2,34},{3,35},{4,36},{5,37},{6,38},{7,39},{8,40},{9,... | collective-permute-start | bytes 1572872 | tf_op jit(solution)/shard_map/ppermute | solution.py:35
  69.5 7.7 %collective-permute-start.17 = (bf16[512,256]{1,0:T(8,128)(2,1)S(1)}, bf16[512,256]{1,0:T(8,128)(2,1)S(1)}, u32[]{:S(2)}, u32[]{:S(2)}) collective-permute-start(bf16[512,256]{1,0:T(8,128)(2,1)S(1)} %slice.61), channel_id=1, source_target_pairs={{0,4},{1,5},{2,6},{3,7},{4,8},{5,9},{6,10},{7,11},{8,12},{9,13},{1... | collective-permute-start | bytes 786440 | tf_op jit(solution)/shard_map/ppermute | solution.py:35
  70.6 7.4 %collective-permute-start.18 = (bf16[512,256]{1,0:T(8,128)(2,1)S(1)}, bf16[512,256]{1,0:T(8,128)(2,1)S(1)}, u32[]{:S(2)}, u32[]{:S(2)}) collective-permute-start(bf16[512,256]{1,0:T(8,128)(2,1)S(1)} %slice.62), channel_id=1, source_target_pairs={{0,12},{1,13},{2,14},{3,15},{4,0},{5,1},{6,2},{7,3},{8,4},{9,5},{1... | collective-permute-start | bytes 786440 | tf_op jit(solution)/shard_map/ppermute | solution.py:35
  77.2 14.8 %collective-permute-start.21 = (bf16[1024,512]{1,0:T(8,128)(2,1)S(1)}, bf16[1024,512]{1,0:T(8,128)(2,1)S(1)}, u32[]{:S(2)}, u32[]{:S(2)}) collective-permute-start(bf16[1024,512]{1,0:T(8,128)(2,1)S(1)} %pad_maximum_fusion.refs_16_), channel_id=1, source_target_pairs={{0,3},{1,0},{2,1},{3,2},{4,7},{5,4},{6,5},{7,6},{8,11},{9,8},{10,9... | collective-permute-start | bytes 3145736 | tf_op jit(solution)/shard_map/ppermute | solution.py:35
  78.0 6.2 %collective-permute-start.8 = (bf16[16,16,1024]{2,1,0:T(8,128)(2,1)S(1)}, bf16[16,16,1024]{2,1,0:T(8,128)(2,1)S(1)}, u32[]{:S(2)}, u32[]{:S(2)}) collective-permute-start(bf16[16,16,1024]{2,1,0:T(8,128)(2,1)S(1)} %collective-permute-done.1.refs_2_), channel_id=1, source_target_pairs={{0,16},{1,17},{2,18},{3,19},{4,20},{5,21},{6,22},{7,23},{8,24},{9,... | collective-permute-start | bytes 1572872 | tf_op jit(solution)/shard_map/ppermute | solution.py:35
  79.1 24.1 %collective-permute-start.22 = (bf16[1024,512]{1,0:T(8,128)(2,1)S(1)}, bf16[1024,512]{1,0:T(8,128)(2,1)S(1)}, u32[]{:S(2)}, u32[]{:S(2)}) collective-permute-start(bf16[1024,512]{1,0:T(8,128)(2,1)S(1)} %maximum_maximum_fusion.refs_17_), channel_id=1, source_target_pairs={{0,3},{1,0},{2,1},{3,2},{4,7},{5,4},{6,5},{7,6},{8,11},{9,8},{10,9... | collective-permute-start | bytes 3145736 | tf_op jit(solution)/shard_map/ppermute | solution.py:35
  82.6 20.6 %collective-permute-start.20 = (bf16[1024,512]{1,0:T(8,128)(2,1)S(1)}, bf16[1024,512]{1,0:T(8,128)(2,1)S(1)}, u32[]{:S(2)}, u32[]{:S(2)}) collective-permute-start(bf16[1024,512]{1,0:T(8,128)(2,1)S(1)} %maximum_maximum_fusion.refs_17_), channel_id=1, source_target_pairs={{0,1},{1,2},{2,3},{3,0},{4,5},{5,6},{6,7},{7,4},{8,9},{9,10},{10,1... | collective-permute-start | bytes 3145736 | tf_op jit(solution)/shard_map/ppermute | solution.py:35
  85.0 9.5 %collective-permute-start.5 = (bf16[16,16,1024]{2,1,0:T(8,128)(2,1)}, bf16[16,16,1024]{2,1,0:T(8,128)(2,1)S(1)}, u32[]{:S(2)}, u32[]{:S(2)}) collective-permute-start(bf16[16,16,1024]{2,1,0:T(8,128)(2,1)} %collective-permute-done.3.refs_4_), channel_id=1, source_target_pairs={{0,32},{1,33},{2,34},{3,35},{4,36},{5,37},{6,38},{7,39},{8,40},{9,... | collective-permute-start | bytes 1572872 | tf_op jit(solution)/shard_map/ppermute | solution.py:35
  85.1 15.2 %collective-permute-start.4 = (bf16[16,16,1024]{2,1,0:T(8,128)(2,1)}, bf16[16,16,1024]{2,1,0:T(8,128)(2,1)}, u32[]{:S(2)}, u32[]{:S(2)}) collective-permute-start(bf16[16,16,1024]{2,1,0:T(8,128)(2,1)} %collective-permute-done.2.refs_3_), channel_id=1, source_target_pairs={{0,32},{1,33},{2,34},{3,35},{4,36},{5,37},{6,38},{7,39},{8,40},{9,... | collective-permute-start | bytes 1572872 | tf_op jit(solution)/shard_map/ppermute | solution.py:35
  92.9 18.9 %collective-permute-start.10 = (bf16[16,16,1024]{2,1,0:T(8,128)(2,1)}, bf16[16,16,1024]{2,1,0:T(8,128)(2,1)S(1)}, u32[]{:S(2)}, u32[]{:S(2)}) collective-permute-start(bf16[16,16,1024]{2,1,0:T(8,128)(2,1)} %collective-permute-done.3.refs_4_), channel_id=1, source_target_pairs={{0,16},{1,17},{2,18},{3,19},{4,20},{5,21},{6,22},{7,23},{8,24},{9,... | collective-permute-start | bytes 1572872 | tf_op jit(solution)/shard_map/ppermute | solution.py:35
  94.5 18.7 %collective-permute-start.7 = (bf16[16,16,1024]{2,1,0:T(8,128)(2,1)S(1)}, bf16[16,16,1024]{2,1,0:T(8,128)(2,1)}, u32[]{:S(2)}, u32[]{:S(2)}) collective-permute-start(bf16[16,16,1024]{2,1,0:T(8,128)(2,1)S(1)} %collective-permute-done.5.refs_6_), channel_id=1, source_target_pairs={{0,32},{1,33},{2,34},{3,35},{4,36},{5,37},{6,38},{7,39},{8,40},{9,... | collective-permute-start | bytes 1572872 | tf_op jit(solution)/shard_map/ppermute | solution.py:35
  100.2 13.0 %collective-permute-start.6 = (bf16[16,16,1024]{2,1,0:T(8,128)(2,1)}, bf16[16,16,1024]{2,1,0:T(8,128)(2,1)}, u32[]{:S(2)}, u32[]{:S(2)}) collective-permute-start(bf16[16,16,1024]{2,1,0:T(8,128)(2,1)} %collective-permute-done.4.refs_5_), channel_id=1, source_target_pairs={{0,32},{1,33},{2,34},{3,35},{4,36},{5,37},{6,38},{7,39},{8,40},{9,... | collective-permute-start | bytes 1572872 | tf_op jit(solution)/shard_map/ppermute | solution.py:35
  103.2 10.5 %collective-permute-start.9 = (bf16[16,16,1024]{2,1,0:T(8,128)(2,1)}, bf16[16,16,1024]{2,1,0:T(8,128)(2,1)}, u32[]{:S(2)}, u32[]{:S(2)}) collective-permute-start(bf16[16,16,1024]{2,1,0:T(8,128)(2,1)} %collective-permute-done.2.refs_3_), channel_id=1, source_target_pairs={{0,16},{1,17},{2,18},{3,19},{4,20},{5,21},{6,22},{7,23},{8,24},{9,... | collective-permute-start | bytes 1572872 | tf_op jit(solution)/shard_map/ppermute | solution.py:35
  105.1 10.1 %collective-permute-start.12 = (bf16[16,16,1024]{2,1,0:T(8,128)(2,1)S(1)}, bf16[16,16,1024]{2,1,0:T(8,128)(2,1)}, u32[]{:S(2)}, u32[]{:S(2)}) collective-permute-start(bf16[16,16,1024]{2,1,0:T(8,128)(2,1)S(1)} %collective-permute-done.5.refs_6_), channel_id=1, source_target_pairs={{0,16},{1,17},{2,18},{3,19},{4,20},{5,21},{6,22},{7,23},{8,24},{9,... | collective-permute-start | bytes 1572872 | tf_op jit(solution)/shard_map/ppermute | solution.py:35
  108.3 13.5 %all-to-all-start.3 = ((bf16[16,32,256]{2,1,0:T(8,128)(2,1)}), bf16[16,32,256]{2,1,0:T(8,128)(2,1)S(1)}, u32[]{:S(2)}, u32[]{:S(2)}) async-start(bf16[16,32,256]{2,1,0:T(8,128)(2,1)} %broadcast_in_dim.15), calls=%async_computation.3 | async-start | bytes 524288 | tf_op jit(solution)/shard_map/all_to_all | solution.py:370
  112.7 9.4 %collective-permute-start.11 = (bf16[16,16,1024]{2,1,0:T(8,128)(2,1)}, bf16[16,16,1024]{2,1,0:T(8,128)(2,1)}, u32[]{:S(2)}, u32[]{:S(2)}) collective-permute-start(bf16[16,16,1024]{2,1,0:T(8,128)(2,1)} %collective-permute-done.4.refs_5_), channel_id=1, source_target_pairs={{0,16},{1,17},{2,18},{3,19},{4,20},{5,21},{6,22},{7,23},{8,24},{9,... | collective-permute-start | bytes 1572872 | tf_op jit(solution)/shard_map/ppermute | solution.py:35
  113.2 8.9 %collective-permute-start.14 = (bf16[16,16,1024]{2,1,0:T(8,128)(2,1)}, bf16[16,16,1024]{2,1,0:T(8,128)(2,1)}, u32[]{:S(2)}, u32[]{:S(2)}) collective-permute-start(bf16[16,16,1024]{2,1,0:T(8,128)(2,1)} %collective-permute-done.7.refs_8_), channel_id=1, source_target_pairs={{0,16},{1,17},{2,18},{3,19},{4,20},{5,21},{6,22},{7,23},{8,24},{9,... | collective-permute-start | bytes 1572872 | tf_op jit(solution)/shard_map/ppermute | solution.py:35
  113.2 8.9 %collective-permute-start.13 = (bf16[16,16,1024]{2,1,0:T(8,128)(2,1)}, bf16[16,16,1024]{2,1,0:T(8,128)(2,1)}, u32[]{:S(2)}, u32[]{:S(2)}) collective-permute-start(bf16[16,16,1024]{2,1,0:T(8,128)(2,1)} %collective-permute-done.6.refs_7_), channel_id=1, source_target_pairs={{0,16},{1,17},{2,18},{3,19},{4,20},{5,21},{6,22},{7,23},{8,24},{9,... | collective-permute-start | bytes 1572872 | tf_op jit(solution)/shard_map/ppermute | solution.py:35
  113.7 34.2 %collective-permute-start.25 = (bf16[1024,512]{1,0:T(8,128)(2,1)}, bf16[1024,512]{1,0:T(8,128)(2,1)S(1)}, u32[]{:S(2)}, u32[]{:S(2)}) collective-permute-start(bf16[1024,512]{1,0:T(8,128)(2,1)} %collective-permute-done.19.refs_18_), channel_id=1, source_target_pairs={{0,1},{1,2},{2,3},{3,0},{4,5},{5,6},{6,7},{7,4},{8,9},{9,10},{10,1... | collective-permute-start | bytes 3145736 | tf_op jit(solution)/shard_map/ppermute | solution.py:35
  115.2 32.7 %collective-permute-start.26 = (bf16[1024,512]{1,0:T(8,128)(2,1)}, bf16[1024,512]{1,0:T(8,128)(2,1)S(1)}, u32[]{:S(2)}, u32[]{:S(2)}) collective-permute-start(bf16[1024,512]{1,0:T(8,128)(2,1)} %copy-done.8), channel_id=1, source_target_pairs={{0,3},{1,0},{2,1},{3,2},{4,7},{5,4},{6,5},{7,6},{8,11},{9,8},{10,9... | collective-permute-start | bytes 3145736 | tf_op jit(solution)/shard_map/ppermute | solution.py:35
  122.1 1.2 copy-start.3
  124.3 1.2 copy-start.7
  125.6 1.2 copy-start.9
  126.8 1.2 copy-start.11
  148.9 1.2 copy-start.1
  175.9 1.3 collective-permute-start.27
  192.7 1.3 collective-permute-start.29
  194.8 11.9 %all-to-all-start.7 = ((f32[16,24,128]{2,1,0:T(8,128)}), f32[16,24,128]{2,1,0:T(8,128)S(1)}, u32[]{:S(2)}, u32[]{:S(2)}) async-start(f32[16,24,128]{2,1,0:T(8,128)} %broadcast_in_dim.20), calls=%async_computation.7 | async-start | bytes 393216 | tf_op jit(solution)/shard_map/all_to_all | solution.py:245
  198.5 1.2 collective-permute-start.28
  (14 other events, 13.6 us)

commit v3 on v2

--- a/solution.py
+++ b/solution.py
@@ -125,103 +125,59 @@
             ).start()
 
 
-def tile_a_kernel(index, *refs):
-    columns, rows, prior, spread = refs[:16], refs[16:22], refs[22], refs[23]
-    total, ahead, image, left, stage, prior_sem, left_sem, stage_sem, ahead_sem = refs[24:]
+def tile_kernel(index, *refs):
+    columns, rows = refs[:16], refs[16:24]
+    prior, spread, first = refs[24:27]
+    out, rounded, image = refs[27:30]
+    total, old, left, stage, old_sem, left_sem, stage_sem, out_sem = refs[30:]
 
     def fetch_row(i):
         return pltpu.make_async_copy(rows[i], left.at[i, pl.ds(0, 1024)], left_sem.at[i])
 
-    for i in range(2):
+    fetch_old = pltpu.make_async_copy(prior, old, old_sem)
+    for i in range(8):
         fetch_row(i).start()
         fetch_columns(index, columns, stage.at[i], stage_sem.at[i], 2 * i)
-    from_prior = pltpu.make_async_copy(prior, total, prior_sem)
-    from_prior.start()
-    for i in range(2, 6):
-        fetch_row(i).start()
-        fetch_columns(index, columns, stage.at[i], stage_sem.at[i], 2 * i)
-    for i in range(2):
-        fetch_columns(index, columns, ahead.at[pl.ds(512 * i, 512)], ahead_sem.at[i], 12 + 2 * i)
-    for i in range(6):
+        if i == 5:
+            fetch_old.start()
+    for i in range(8):
         for t in range(2):
             left[i, 1024:1056, 256 * t : 256 * (t + 1)] = spread[index[2 * i + t]]
-    for group in range(3):
+    for group in range(4):
         for i in (2 * group, 2 * group + 1):
             fetch_row(i).wait()
             pltpu.make_async_copy(stage.at[i], stage.at[i], stage_sem.at[i]).wait()
-        if group == 0:
-            from_prior.wait()
+        if group == 3:
+            fetch_old.wait()
 
         def step(n, carry, group=group):
             at = pl.ds(pl.multiple_of(n * 256, 256), 256)
             product = jnp.zeros((1056, 256), F32)
             for i in (2 * group, 2 * group + 1):
                 product += jnp.dot(left[i], stage[i, :, at], preferred_element_type=F32)
-            total[:, at] += product[:1024] * (1.0 / M)
             if group == 0:
-                image[:, at] = product[1024:]
+                total[:, at] = product
+            elif group < 3:
+                total[:, at] += product
             else:
-                image[:, at] += product[1024:]
+                product += total[:, at]
+                value = old[:, at] + product[:1024] * (1.0 / M)
+                old[:, at] = value
+                pltpu.make_async_copy(old.at[:, at], out.at[:, at], out_sem.at[n]).start()
+                rounded[:, at] = value.astype(BF16)
+                image[:, at] = first[:, at] + product[1024 : 1024 + K] * (1.0 / M)
             return carry
 
         lax.fori_loop(0, 4, step, 0)
-    for i in range(2):
-        part = ahead.at[pl.ds(512 * i, 512)]
-        pltpu.make_async_copy(part, part, ahead_sem.at[i]).wait()
-
-
-def tile_a(index, columns, rows, prior, spread):
-    return pl.pallas_call(
-        tile_a_kernel,
-        in_specs=[SMEM] + [ANY] * 23 + [VMEM],
-        out_specs=[VMEM] * 3,
-        out_shape=[
-            jax.ShapeDtypeStruct((1024, 1024), F32),
-            jax.ShapeDtypeStruct((1024, 1024), BF16),
-            jax.ShapeDtypeStruct((32, 1024), F32),
-        ],
-        scratch_shapes=[
-            pltpu.VMEM((6, 1056, 512), BF16),
-            pltpu.VMEM((6, 512, 1024), BF16),
-            pltpu.SemaphoreType.DMA,
-            pltpu.SemaphoreType.DMA((6,)),
-            pltpu.SemaphoreType.DMA((6,)),
-            pltpu.SemaphoreType.DMA((2,)),
-        ],
-        compiler_params=pltpu.CompilerParams(vmem_limit_bytes=32 * 2**20),
-        cost_estimate=pl.CostEstimate(flops=6 * 2**30, bytes_accessed=18 * 2**20, transcendentals=0),
-        name="tile_a",
-    )(index, *columns, *rows, prior, spread)
-
-
-def tile_b_kernel(
-    index, partial, ahead, row0, row1, spread, so_far, first, out, rounded, image, total, left, out_sem
-):
-    for t in range(4):
-        left[:, 256 * t : 256 * (t + 1)] = spread[index[12 + t]]
-
-    def step(n, carry):
-        at = pl.ds(pl.multiple_of(n * 256, 256), 256)
-        product = jnp.dot(row0[...], ahead[:512, at], preferred_element_type=F32)
-        product += jnp.dot(row1[...], ahead[512:, at], preferred_element_type=F32)
-        value = partial[:, at] + product * (1.0 / M)
-        total[:, at] = value
-        pltpu.make_async_copy(total.at[:, at], out.at[:, at], out_sem.at[n]).start()
-        rounded[:, at] = value.astype(BF16)
-        rest = so_far[:, at] + jnp.dot(left[...], ahead[:, at], preferred_element_type=F32)
-        image[:, at] = first[:, at] + rest[:K] * (1.0 / M)
-        return carry
-
-    lax.fori_loop(0, 4, step, 0)
     for n in range(4):
         at = pl.ds(n * 256, 256)
-        pltpu.make_async_copy(total.at[:, at], out.at[:, at], out_sem.at[n]).wait()
-
-
-def tile_b(index, partial, ahead, row0, row1, spread, so_far, first):
-    return pl.pallas_call(
-        tile_b_kernel,
-        in_specs=[SMEM] + [VMEM] * 7,
+        pltpu.make_async_copy(old.at[:, at], out.at[:, at], out_sem.at[n]).wait()
+
+
+def tile(index, columns, rows, prior, spread, first):
+    return pl.pallas_call(
+        tile_kernel,
+        in_specs=[SMEM] + [ANY] * 25 + [VMEM] * 2,
         out_specs=[ANY, VMEM, VMEM],
         out_shape=[
             jax.ShapeDtypeStruct((1024, 1024), F32),
@@ -229,14 +185,19 @@
             jax.ShapeDtypeStruct((K, 1024), F32),
         ],
         scratch_shapes=[
+            pltpu.VMEM((1056, 1024), F32),
             pltpu.VMEM((1024, 1024), F32),
-            pltpu.VMEM((32, 1024), BF16),
+            pltpu.VMEM((8, 1056, 512), BF16),
+            pltpu.VMEM((8, 512, 1024), BF16),
+            pltpu.SemaphoreType.DMA,
+            pltpu.SemaphoreType.DMA((8,)),
+            pltpu.SemaphoreType.DMA((8,)),
             pltpu.SemaphoreType.DMA((4,)),
         ],
-        compiler_params=pltpu.CompilerParams(vmem_limit_bytes=20 * 2**20),
-        cost_estimate=pl.CostEstimate(flops=2 * 2**30, bytes_accessed=14 * 2**20, transcendentals=0),
-        name="tile_b",
-    )(index, partial, ahead, row0, row1, spread, so_far, first)
+        compiler_params=pltpu.CompilerParams(vmem_limit_bytes=40 * 2**20),
+        cost_estimate=pl.CostEstimate(flops=8 * 2**30, bytes_accessed=26 * 2**20, transcendentals=0),
+        name="tile",
+    )(index, *columns, *rows, prior, spread, first)
 
 
 def bcast_sum(array, axis):
@@ -361,11 +322,9 @@
     columns = down + up
 
     start = (start_vectors.T / jnp.sqrt(F32(S))).astype(BF16)
-    parts = [
-        dot_t(start, prior.astype(BF16), ((1,), (0,))),
-        dot_t(start, piece.reshape(256, 1024), ((1,), (1,))),
-    ]
-    early = row_sum(jnp.concatenate(parts, axis=1))
+    of_prior = dot_t(start, prior.astype(BF16), ((1,), (0,)))
+    of_piece = dot_t(start, piece.reshape(256, 1024), ((1,), (1,)))
+    early = row_sum(jnp.concatenate([of_prior, of_piece], axis=1))
     spread = jnp.pad(early[:, 1024:], ((0, 32 - K), (0, 0))).astype(BF16)
     spread = lax.all_to_all(jnp.broadcast_to(spread[None], (16, 32, 256)), COL, 0, 0, tiled=True)
     at = jnp.arange(256, dtype=jnp.int32)
@@ -386,11 +345,8 @@
     g1 = second_axis(h1, -1)
     last0 = second_axis(f0, 1)
     last1 = second_axis(g1, -1)
-    partial, ahead, so_far = tile_a(index, columns, [h0, h1, f0, f1, g0, g1], prior, spread)
-    ahead, last0, last1 = lax.optimization_barrier((ahead, last0, last1))
-    grm, rounded, image = tile_b(
-        index, partial, ahead, last0, last1, spread, so_far, early[:, :1024]
-    )
+    rows = [h0, h1, f0, f1, g0, g1, last0, last1]
+    grm, rounded, image = tile(index, columns, rows, prior, spread, early[:, :1024])
     gram1 = dot_t(image, image, ((1,), (1,)))
     packed = with_gram(dot_t(image.astype(BF16), rounded, ((1,), (1,))), gram1)
     packed = bcast_sum(packed, "x").astype(BF16)

time: 212 us -> 207 us (0.976)
  local copies, waits for them, and re-layouts: 26.2 us -> 13.7 us
  starting transfers between devices: 47.1 us -> 56.4 us
  waiting for transfers between devices: 65.2 us -> 61.7 us
  blocking collectives: 32.8 us -> 35.8 us
    unnamed x54 -> x34, local copies, waits for them, and re-layouts: 19.7 us -> 9.17 us
    all_to_all x2, waiting for transfers between devices: 14.7 us -> 7.09 us  [bcast_sum(): lax.all_to_all(copies, axis, 0, 0, tiled=True).astype(F32).sum(axis=0)]
    ppermute x30, starting transfers between devices: 20.1 us -> 26.6 us  [send(): return lax.ppermute(array, ALL, pairs)]
    all_to_all x1, waiting for transfers between devices: 3.94 us -> 7.07 us  [body(): lax.all_to_all(jnp.broadcast_to(spread[None], (16, 32, 256)), COL, 0, 0,...]
    all_to_all x3, blocking collectives: 32.8 us -> 35.8 us  [bcast_sum(): lax.all_to_all(copies, axis, 0, 0, tiled=True).astype(F32).sum(axis=0)]
    pallas_call x2 -> x1, Pallas kernels: 19.5 us -> 18.8 us  [tile(): pl.pallas_call(tile_kernel, in_specs=[SMEM] + [ANY] * 25 + [VMEM] * 2, ou...]
  transfers between devices with their start and end apart: 35 -> 35, of which waited for: 14 -> 15; matrix products, arithmetic and copies ran while one was open for 6% -> 4% of each run, Pallas kernels for 7% -> 0%
where the time goes in v3:
time: 207 us; the launch traced here: 205 us
  waiting for transfers between devices  61.7 us (30%)
  starting transfers between devices  56.4 us (27%)
  blocking collectives  35.8 us (17%)
  Pallas kernels  27.9 us (13%)
  local copies, waits for them, and re-layouts  13.7 us (7%)
  matrix products  6.23 us (3%)
    all_to_all x3, blocking collectives, bcast_sum(): lax.all_to_all(copies, axis, 0, 0, tiled=True).astype(F32).sum(axis=0)  35.8 us
    ppermute x30, starting transfers between devices, send(): return lax.ppermute(array, ALL, pairs)  26.6 us
    ppermute x30, waiting for transfers between devices, send(): return lax.ppermute(array, ALL, pairs)  24.7 us
    pallas_call x1, Pallas kernels, tile(): pl.pallas_call(tile_kernel, in_specs=[SMEM] + [ANY] * 25 + [VMEM] * 2, ou...  18.8 us
    all_to_all x1, waiting for transfers between devices, body(): piece = lax.all_to_all(standard, ROW, 0, 0, tiled=True)  11.6 us
    all_to_all x1, waiting for transfers between devices, body(): own = lax.all_to_all(standard, COL, 0, 0, tiled=True)  11.2 us
    all_to_all x2, starting transfers between devices, bcast_sum(): lax.all_to_all(copies, axis, 0, 0, tiled=True).astype(F32).sum(axis=0)  9.18 us
    unnamed x34, local copies, waits for them, and re-layouts  9.17 us
  transfers between devices with their start and end apart: 35, of which 15 were waited for; matrix products, arithmetic and copies ran while one was open for 4% of the time, Pallas kernels for 0%

profile of v3, /device:TPU:32, one launch (start us, length us, event | category | flops | bytes accessed | tf_op | source)
XLA Modules:
  0.0 204.9 jit_solution(6000261990125969305)
XLA Ops:
  0.7 4.4 %standardize.1 = bf16[16,16,1024]{2,1,0:T(8,128)(2,1)} custom-call(s32[16]{0:T(128)} %index.1, f32[128,128]{1,0:T(8,128)} %bitcast.25, s32[16,16384]{1,0:T(8,128)} %genotypes.1), custom_call_target="tpu_custom_call" | custom-call | tf_op jit(solution)/shard_map/standardize/pallas_call | solution.py:83
  5.1 8.6 %all-to-all-start = ((bf16[16,16,1024]{2,1,0:T(8,128)(2,1)}), bf16[16,16,1024]{2,1,0:T(8,128)(2,1)S(1)}, u32[]{:S(2)}, u32[]{:S(2)}) async-start(bf16[16,16,1024]{2,1,0:T(8,128)(2,1)} %standardize.1), calls=%async_computation | async-start | bytes 1048576 | tf_op jit(solution)/shard_map/all_to_all | solution.py:309
  13.7 2.6 %fusion = f32[20,1024]{1,0:T(8,128)S(1)} fusion(f32[1024,1024]{1,0:T(8,128)} %refs_24_.1, f32[1024,20]{0,1:T(8,128)S(1)} %copy-done.11), kind=kOutput, calls=%fused_computation | convolution fusion | flops 43032576 | bytes 4358144 | tf_op jit(solution)/shard_map/dot_general | solution.py:244
  16.3 11.6 %all-to-all-done.piece = bf16[16,16,1024]{2,1,0:T(8,128)(2,1)S(1)} async-done(((bf16[16,16,1024]{2,1,0:T(8,128)(2,1)}), bf16[16,16,1024]{2,1,0:T(8,128)(2,1)S(1)}, u32[]{:S(2)}, u32[]{:S(2)}) %all-to-all-start) | async-done | bytes 524320 | tf_op jit(solution)/shard_map/all_to_all | solution.py:309
  28.6 2.8 %collective-permute-start.16 = (bf16[1024,256]{1,0:T(8,128)(2,1)S(1)}, bf16[1024,256]{1,0:T(8,128)(2,1)S(1)}, u32[]{:S(2)}, u32[]{:S(2)}) collective-permute-start(bf16[1024,256]{1,0:T(8,128)(2,1)S(1)} %turn.1), channel_id=1, source_target_pairs={{0,12},{1,13},{2,14},{3,15},{4,0},{5,1},{6,2},{7,3},{8,4},{9,5},{1... | collective-permute-start | bytes 1572872 | tf_op jit(solution)/shard_map/ppermute | solution.py:35
  31.5 7.2 %all-to-all-start.1 = ((bf16[16,16,1024]{2,1,0:T(8,128)(2,1)}), bf16[16,16,1024]{2,1,0:T(8,128)(2,1)S(1)}, u32[]{:S(2)}, u32[]{:S(2)}) async-start(bf16[16,16,1024]{2,1,0:T(8,128)(2,1)} %standardize.1), calls=%async_computation.1 | async-start | bytes 1048576 | tf_op jit(solution)/shard_map/all_to_all | solution.py:311
  39.1 11.2 %all-to-all-done.1.refs_0_ = bf16[16,16,1024]{2,1,0:T(8,128)(2,1)S(1)} async-done(((bf16[16,16,1024]{2,1,0:T(8,128)(2,1)}), bf16[16,16,1024]{2,1,0:T(8,128)(2,1)S(1)}, u32[]{:S(2)}, u32[]{:S(2)}) %all-to-all-start.1) | async-done | bytes 524320 | tf_op jit(solution)/shard_map/all_to_all | solution.py:311
  50.4 1.9 collective-permute-start.1
  53.0 5.7 %all-to-all-start.2 = ((bf16[8,20,640]{2,1,0:T(8,128)(2,1)}), bf16[8,20,640]{2,1,0:T(8,128)(2,1)S(1)}, u32[]{:S(2)}, u32[]{:S(2)}) async-start(bf16[8,20,640]{2,1,0:T(8,128)(2,1)} %broadcast_in_dim.14), calls=%async_computation.2 | async-start | bytes 491520 | tf_op jit(solution)/shard_map/all_to_all | solution.py:206
  58.7 1.3 collective-permute-start.18
  61.6 0.9 collective-permute-start.21
  62.7 3.2 %collective-permute-done.18 = bf16[512,256]{1,0:T(8,128)(2,1)S(1)} collective-permute-done((bf16[512,256]{1,0:T(8,128)(2,1)S(1)}, bf16[512,256]{1,0:T(8,128)(2,1)S(1)}, u32[]{:S(2)}, u32[]{:S(2)}) %collective-permute-start.18) | collective-permute-done | bytes 262176 | tf_op jit(solution)/shard_map/ppermute | solution.py:35
  66.7 1.5 collective-permute-start.3
  68.9 1.3 maximum_maximum_fusion.refs_17_
  70.9 2.7 %collective-permute-start.22 = (bf16[1024,512]{1,0:T(8,128)(2,1)S(1)}, bf16[1024,512]{1,0:T(8,128)(2,1)}, u32[]{:S(2)}, u32[]{:S(2)}) collective-permute-start(bf16[1024,512]{1,0:T(8,128)(2,1)S(1)} %maximum_maximum_fusion.refs_17_), channel_id=1, source_target_pairs={{0,3},{1,0},{2,1},{3,2},{4,7},{5,4},{6,5},{7,6},{8,11},{9,8},{10,9... | collective-permute-start | bytes 3145736 | tf_op jit(solution)/shard_map/ppermute | solution.py:35
  73.6 1.2 collective-permute-start.2
  74.7 1.2 collective-permute-done.3.refs_4_
  75.9 0.8 collective-permute-start.20
  76.8 6.1 %collective-permute-done.2.refs_3_ = bf16[16,16,1024]{2,1,0:T(8,128)(2,1)S(1)} collective-permute-done((bf16[16,16,1024]{2,1,0:T(8,128)(2,1)}, bf16[16,16,1024]{2,1,0:T(8,128)(2,1)S(1)}, u32[]{:S(2)}, u32[]{:S(2)}) %collective-permute-start.2) | collective-permute-done | bytes 524320 | tf_op jit(solution)/shard_map/ppermute | solution.py:35
  82.9 1.2 collective-permute-start.5
  84.1 2.4 %collective-permute-start.4 = (bf16[16,16,1024]{2,1,0:T(8,128)(2,1)S(1)}, bf16[16,16,1024]{2,1,0:T(8,128)(2,1)}, u32[]{:S(2)}, u32[]{:S(2)}) collective-permute-start(bf16[16,16,1024]{2,1,0:T(8,128)(2,1)S(1)} %collective-permute-done.2.refs_3_), channel_id=1, source_target_pairs={{0,32},{1,33},{2,34},{3,35},{4,36},{5,37},{6,38},{7,39},{8,40},{9,... | collective-permute-start | bytes 1572872 | tf_op jit(solution)/shard_map/ppermute | solution.py:35
  86.5 1.3 collective-permute-done.22.refs_21_
  88.7 3.8 %collective-permute-done.5.refs_6_ = bf16[16,16,1024]{2,1,0:T(8,128)(2,1)} collective-permute-done((bf16[16,16,1024]{2,1,0:T(8,128)(2,1)}, bf16[16,16,1024]{2,1,0:T(8,128)(2,1)}, u32[]{:S(2)}, u32[]{:S(2)}) %collective-permute-start.5) | collective-permute-done | bytes 524320 | tf_op jit(solution)/shard_map/ppermute | solution.py:35
  92.4 5.1 %collective-permute-done.20.refs_19_ = bf16[1024,512]{1,0:T(8,128)(2,1)S(1)} collective-permute-done((bf16[1024,512]{1,0:T(8,128)(2,1)S(1)}, bf16[1024,512]{1,0:T(8,128)(2,1)S(1)}, u32[]{:S(2)}, u32[]{:S(2)}) %collective-permute-start.20) | collective-permute-done | bytes 1048608 | tf_op jit(solution)/shard_map/ppermute | solution.py:35
  97.6 1.0 copy-done
  98.5 1.2 collective-permute-start.7
  99.7 2.4 %collective-permute-start.6 = (bf16[16,16,1024]{2,1,0:T(8,128)(2,1)}, bf16[16,16,1024]{2,1,0:T(8,128)(2,1)}, u32[]{:S(2)}, u32[]{:S(2)}) collective-permute-start(bf16[16,16,1024]{2,1,0:T(8,128)(2,1)} %collective-permute-done.4.refs_5_), channel_id=1, source_target_pairs={{0,32},{1,33},{2,34},{3,35},{4,36},{5,37},{6,38},{7,39},{8,40},{9,... | collective-permute-start | bytes 1572872 | tf_op jit(solution)/shard_map/ppermute | solution.py:35
  102.1 0.8 copy-done.4
  103.8 3.2 %collective-permute-start.24 = (bf16[1024,512]{1,0:T(8,128)(2,1)}, bf16[1024,512]{1,0:T(8,128)(2,1)}, u32[]{:S(2)}, u32[]{:S(2)}) collective-permute-start(bf16[1024,512]{1,0:T(8,128)(2,1)} %collective-permute-done.22.refs_21_), channel_id=1, source_target_pairs={{0,3},{1,0},{2,1},{3,2},{4,7},{5,4},{6,5},{7,6},{8,11},{9,8},{10,9... | collective-permute-start | bytes 3145736 | tf_op jit(solution)/shard_map/ppermute | solution.py:35
  108.4 4.8 %all-to-all-start.3 = ((bf16[16,32,256]{2,1,0:T(8,128)(2,1)}), bf16[16,32,256]{2,1,0:T(8,128)(2,1)S(1)}, u32[]{:S(2)}, u32[]{:S(2)}) async-start(bf16[16,32,256]{2,1,0:T(8,128)(2,1)} %broadcast_in_dim.15), calls=%async_computation.3 | async-start | bytes 524288 | tf_op jit(solution)/shard_map/all_to_all | solution.py:329
  114.4 0.9 slice.65.refs_26_
  115.3 7.1 %all-to-all-done.3 = bf16[16,32,256]{2,1,0:T(8,128)(2,1)S(1)} async-done(((bf16[16,32,256]{2,1,0:T(8,128)(2,1)}), bf16[16,32,256]{2,1,0:T(8,128)(2,1)S(1)}, u32[]{:S(2)}, u32[]{:S(2)}) %all-to-all-start.3) | async-done | bytes 262176 | tf_op jit(solution)/shard_map/all_to_all | solution.py:329
  122.6 1.2 copy-done.1
  123.9 1.0 copy-done.3
  124.9 1.0 copy-done.5
  125.9 1.0 copy-done.7
  127.0 18.8 %tile.1 = (f32[1024,1024]{1,0:T(8,128)}, bf16[1024,1024]{1,0:T(8,128)(2,1)}, f32[20,1024]{1,0:T(8,128)S(1)}) custom-call(s32[16]{0:T(128)S(1)} %fusion.16.index, bf16[16,16,1024]{2,1,0:T(8,128)(2,1)S(1)} %all-to-all-done.1.refs_0_, bf16[16,16,1024]{2,1,0:T(8,128)(2,1)} %collective-permute-done.refs_1_, ...), custom_call_target="tpu_custom_call" | custom-call | flops 8589934592 | bytes 27262976 | tf_op jit(solution)/shard_map/tile/pallas_call | solution.py:178
  146.0 2.4 %convolution_convert_fusion.1 = bf16[20,1024]{1,0:T(8,128)(2,1)S(1)} fusion(bf16[1024,1024]{1,0:T(8,128)(2,1)} %get-tuple-element.16, f32[20,1024]{1,0:T(8,128)S(1)} %get-tuple-element.15), kind=kOutput, calls=%fused_computation.3 | convolution fusion | flops 41984000 | bytes 2220032 | tf_op jit(solution)/shard_map/dot_general | solution.py:244
  148.7 10.8 %all_to_all.40 = bf16[4,24,1024]{2,1,0:T(8,128)(2,1)S(1)} all-to-all(bf16[4,24,1024]{2,1,0:T(8,128)(2,1)S(1)} %broadcast_in_dim.17), channel_id=1, replica_groups=mesh['z'=8,'core'=2,'x'=4,'y'=4] {'x'}, dimensions={0} | all-to-all | bytes 393216 | tf_op jit(solution)/shard_map/all_to_all | solution.py:206
  159.6 11.1 %all_to_all.41 = bf16[4,24,1024]{2,1,0:T(8,128)(2,1)S(1)} all-to-all(bf16[4,24,1024]{2,1,0:T(8,128)(2,1)S(1)} %broadcast_in_dim.18), channel_id=1, replica_groups=mesh['z'=8,'core'=2,'x'=4,'y'=4] {'y'}, dimensions={0} | all-to-all | bytes 393216 | tf_op jit(solution)/shard_map/all_to_all | solution.py:206
  170.9 1.6 solve.1
  173.4 1.1 collective-permute-done.27
  174.6 13.8 %all_to_all.42 = bf16[8,24,512]{2,1,0:T(8,128)(2,1)S(1)} all-to-all(bf16[8,24,512]{2,1,0:T(8,128)(2,1)S(1)} %broadcast_in_dim.19), channel_id=1, replica_groups=mesh['z'=8,'core'=2,'x'=4,'y'=4] {'z'}, dimensions={0} | all-to-all | bytes 393216 | tf_op jit(solution)/shard_map/all_to_all | solution.py:206
  188.6 1.2 collective-permute-done.29
  190.6 3.5 %all-to-all-start.7 = ((f32[16,24,128]{2,1,0:T(8,128)}), f32[16,24,128]{2,1,0:T(8,128)S(1)}, u32[]{:S(2)}, u32[]{:S(2)}) async-start(f32[16,24,128]{2,1,0:T(8,128)} %broadcast_in_dim.20), calls=%async_computation.7 | async-start | bytes 393216 | tf_op jit(solution)/shard_map/all_to_all | solution.py:206
  194.5 1.0 collective-permute-done.28
  195.5 7.1 %all-to-all-done.7 = f32[16,24,128]{2,1,0:T(8,128)S(1)} async-done(((f32[16,24,128]{2,1,0:T(8,128)}), f32[16,24,128]{2,1,0:T(8,128)S(1)}, u32[]{:S(2)}, u32[]{:S(2)}) %all-to-all-start.7) | async-done | bytes 196640 | tf_op jit(solution)/shard_map/all_to_all | solution.py:206
  202.6 2.3 %last.1 = (f32[20,1024]{1,0:T(8,128)}, f32[3,20]{1,0:T(4,128)}) custom-call(f32[1,20]{1,0:T(1,128)S(1)} %get-tuple-element.17.first, f32[20,20]{1,0:T(8,128)S(1)} %add.110.gram2, f32[20,20]{1,0:T(8,128)S(1)} %bitcast.21, f32[20,1024]{1,0:T(8,128)S(1)} %maximum_select_fusion.1.wide), custom_call_target="tpu_custom_call" | custom-call | tf_op jit(solution)/shard_map/last/pallas_call | solution.py:286
  (115 shorter events, 13.1 us)
Async XLA Ops:
  0.6 13.1 %copy-start.13 = (s32[16]{0:T(128)S(1)}, s32[16]{0:T(128)}, u32[]{:S(2)}) copy-start(s32[16]{0:T(128)} %constant.99.clone) | copy-start | bytes 196
  0.6 13.0 %copy-start.14 = (s32[16]{0:T(128)S(1)}, s32[16]{0:T(128)}, u32[]{:S(2)}) copy-start(s32[16]{0:T(128)} %constant.98.clone) | copy-start | bytes 196
  0.7 13.1 %copy-start.11 = (f32[1024,20]{0,1:T(8,128)S(1)}, f32[1024,20]{0,1:T(8,128)}, u32[]{:S(2)}) copy-start(f32[1024,20]{0,1:T(8,128)} %param.13) | copy-start | bytes 245764
  5.1 22.8 %all-to-all-start = ((bf16[16,16,1024]{2,1,0:T(8,128)(2,1)}), bf16[16,16,1024]{2,1,0:T(8,128)(2,1)S(1)}, u32[]{:S(2)}, u32[]{:S(2)}) async-start(bf16[16,16,1024]{2,1,0:T(8,128)(2,1)} %standardize.1), calls=%async_computation | async-start | bytes 1048576 | tf_op jit(solution)/shard_map/all_to_all | solution.py:309
  28.6 30.0 %collective-permute-start.16 = (bf16[1024,256]{1,0:T(8,128)(2,1)S(1)}, bf16[1024,256]{1,0:T(8,128)(2,1)S(1)}, u32[]{:S(2)}, u32[]{:S(2)}) collective-permute-start(bf16[1024,256]{1,0:T(8,128)(2,1)S(1)} %turn.1), channel_id=1, source_target_pairs={{0,12},{1,13},{2,14},{3,15},{4,0},{5,1},{6,2},{7,3},{8,4},{9,5},{1... | collective-permute-start | bytes 1572872 | tf_op jit(solution)/shard_map/ppermute | solution.py:35
  31.5 28.5 %collective-permute-start.15 = (bf16[1024,256]{1,0:T(8,128)(2,1)S(1)}, bf16[1024,256]{1,0:T(8,128)(2,1)S(1)}, u32[]{:S(2)}, u32[]{:S(2)}) collective-permute-start(bf16[1024,256]{1,0:T(8,128)(2,1)S(1)} %turn.1), channel_id=1, source_target_pairs={{0,4},{1,5},{2,6},{3,7},{4,8},{5,9},{6,10},{7,11},{8,12},{9,13},{1... | collective-permute-start | bytes 1572872 | tf_op jit(solution)/shard_map/ppermute | solution.py:35
  31.5 18.9 %all-to-all-start.1 = ((bf16[16,16,1024]{2,1,0:T(8,128)(2,1)}), bf16[16,16,1024]{2,1,0:T(8,128)(2,1)S(1)}, u32[]{:S(2)}, u32[]{:S(2)}) async-start(bf16[16,16,1024]{2,1,0:T(8,128)(2,1)} %standardize.1), calls=%async_computation.1 | async-start | bytes 1048576 | tf_op jit(solution)/shard_map/all_to_all | solution.py:311
  39.0 13.2 %collective-permute-start.25 = (f32[20,640]{1,0:T(8,128)S(1)}, f32[20,640]{1,0:T(8,128)S(1)}, u32[]{:S(2)}, u32[]{:S(2)}) collective-permute-start(f32[20,640]{1,0:T(8,128)S(1)} %slice_select_fusion), channel_id=1, source_target_pairs={{0,16},{1,17},{2,18},{3,19},{4,20},{5,21},{6,22},{7,23},{8,24},{9,... | collective-permute-start | bytes 153608 | tf_op jit(solution)/shard_map/ppermute | solution.py:35
  50.4 12.4 %collective-permute-start.1 = (bf16[16,16,1024]{2,1,0:T(8,128)(2,1)S(1)}, bf16[16,16,1024]{2,1,0:T(8,128)(2,1)S(1)}, u32[]{:S(2)}, u32[]{:S(2)}) collective-permute-start(bf16[16,16,1024]{2,1,0:T(8,128)(2,1)S(1)} %all-to-all-done.1.refs_0_), channel_id=1, source_target_pairs={{0,32},{1,33},{2,34},{3,35},{4,36},{5,37},{6,38},{7,39},{8,40},{9,... | collective-permute-start | bytes 1572872 | tf_op jit(solution)/shard_map/ppermute | solution.py:35
  53.0 15.2 %all-to-all-start.2 = ((bf16[8,20,640]{2,1,0:T(8,128)(2,1)}), bf16[8,20,640]{2,1,0:T(8,128)(2,1)S(1)}, u32[]{:S(2)}, u32[]{:S(2)}) async-start(bf16[8,20,640]{2,1,0:T(8,128)(2,1)} %broadcast_in_dim.14), calls=%async_computation.2 | async-start | bytes 491520 | tf_op jit(solution)/shard_map/all_to_all | solution.py:206
  58.7 2.1 %copy-start.9 = (bf16[1024,256]{1,0:T(8,128)(2,1)}, bf16[1024,256]{1,0:T(8,128)(2,1)S(1)}, u32[]{:S(2)}) copy-start(bf16[1024,256]{1,0:T(8,128)(2,1)S(1)} %collective-permute-done.16) | copy-start | bytes 1572868
  58.7 7.3 %collective-permute-start.18 = (bf16[512,256]{1,0:T(8,128)(2,1)S(1)}, bf16[512,256]{1,0:T(8,128)(2,1)S(1)}, u32[]{:S(2)}, u32[]{:S(2)}) collective-permute-start(bf16[512,256]{1,0:T(8,128)(2,1)S(1)} %slice.62), channel_id=1, source_target_pairs={{0,12},{1,13},{2,14},{3,15},{4,0},{5,1},{6,2},{7,3},{8,4},{9,5},{1... | collective-permute-start | bytes 786440 | tf_op jit(solution)/shard_map/ppermute | solution.py:35
  60.0 10.9 %collective-permute-start = (bf16[16,16,1024]{2,1,0:T(8,128)(2,1)S(1)}, bf16[16,16,1024]{2,1,0:T(8,128)(2,1)}, u32[]{:S(2)}, u32[]{:S(2)}) collective-permute-start(bf16[16,16,1024]{2,1,0:T(8,128)(2,1)S(1)} %all-to-all-done.1.refs_0_), channel_id=1, source_target_pairs={{0,16},{1,17},{2,18},{3,19},{4,20},{5,21},{6,22},{7,23},{8,24},{9,... | collective-permute-start | bytes 1572872 | tf_op jit(solution)/shard_map/ppermute | solution.py:35
  60.8 7.9 %collective-permute-start.17 = (bf16[512,256]{1,0:T(8,128)(2,1)}, bf16[512,256]{1,0:T(8,128)(2,1)}, u32[]{:S(2)}, u32[]{:S(2)}) collective-permute-start(bf16[512,256]{1,0:T(8,128)(2,1)} %slice.61), channel_id=1, source_target_pairs={{0,4},{1,5},{2,6},{3,7},{4,8},{5,9},{6,10},{7,11},{8,12},{9,13},{1... | collective-permute-start | bytes 786440 | tf_op jit(solution)/shard_map/ppermute | solution.py:35
  61.6 52.6 %copy-start.15 = (s32[16]{0:T(128)S(1)}, s32[16]{0:T(128)}, u32[]{:S(2)}) copy-start(s32[16]{0:T(128)} %constant.101.clone) | copy-start | bytes 196
  61.6 52.6 %copy-start.16 = (s32[16]{0:T(128)S(1)}, s32[16]{0:T(128)}, u32[]{:S(2)}) copy-start(s32[16]{0:T(128)} %constant.100.clone) | copy-start | bytes 196
  61.6 22.5 %collective-permute-start.21 = (bf16[1024,512]{1,0:T(8,128)(2,1)S(1)}, bf16[1024,512]{1,0:T(8,128)(2,1)}, u32[]{:S(2)}, u32[]{:S(2)}) collective-permute-start(bf16[1024,512]{1,0:T(8,128)(2,1)S(1)} %pad_maximum_fusion.refs_16_), channel_id=1, source_target_pairs={{0,3},{1,0},{2,1},{3,2},{4,7},{5,4},{6,5},{7,6},{8,11},{9,8},{10,9... | collective-permute-start | bytes 3145736 | tf_op jit(solution)/shard_map/ppermute | solution.py:35
  62.7 10.8 %collective-permute-start.8 = (bf16[16,16,1024]{2,1,0:T(8,128)(2,1)S(1)}, bf16[16,16,1024]{2,1,0:T(8,128)(2,1)}, u32[]{:S(2)}, u32[]{:S(2)}) collective-permute-start(bf16[16,16,1024]{2,1,0:T(8,128)(2,1)S(1)} %collective-permute-done.1.refs_2_), channel_id=1, source_target_pairs={{0,16},{1,17},{2,18},{3,19},{4,20},{5,21},{6,22},{7,23},{8,24},{9,... | collective-permute-start | bytes 1572872 | tf_op jit(solution)/shard_map/ppermute | solution.py:35
  66.7 9.3 %collective-permute-start.3 = (bf16[16,16,1024]{2,1,0:T(8,128)(2,1)S(1)}, bf16[16,16,1024]{2,1,0:T(8,128)(2,1)}, u32[]{:S(2)}, u32[]{:S(2)}) collective-permute-start(bf16[16,16,1024]{2,1,0:T(8,128)(2,1)S(1)} %collective-permute-done.1.refs_2_), channel_id=1, source_target_pairs={{0,32},{1,33},{2,34},{3,35},{4,36},{5,37},{6,38},{7,39},{8,40},{9,... | collective-permute-start | bytes 1572872 | tf_op jit(solution)/shard_map/ppermute | solution.py:35
  68.7 1.6 collective-permute-start.26
  70.2 16.3 %collective-permute-start.19 = (bf16[1024,512]{1,0:T(8,128)(2,1)S(1)}, bf16[1024,512]{1,0:T(8,128)(2,1)}, u32[]{:S(2)}, u32[]{:S(2)}) collective-permute-start(bf16[1024,512]{1,0:T(8,128)(2,1)S(1)} %pad_maximum_fusion.refs_16_), channel_id=1, source_target_pairs={{0,1},{1,2},{2,3},{3,0},{4,5},{5,6},{6,7},{7,4},{8,9},{9,10},{10,1... | collective-permute-start | bytes 3145736 | tf_op jit(solution)/shard_map/ppermute | solution.py:35
  70.9 17.0 %collective-permute-start.22 = (bf16[1024,512]{1,0:T(8,128)(2,1)S(1)}, bf16[1024,512]{1,0:T(8,128)(2,1)}, u32[]{:S(2)}, u32[]{:S(2)}) collective-permute-start(bf16[1024,512]{1,0:T(8,128)(2,1)S(1)} %maximum_maximum_fusion.refs_17_), channel_id=1, source_target_pairs={{0,3},{1,0},{2,1},{3,2},{4,7},{5,4},{6,5},{7,6},{8,11},{9,8},{10,9... | collective-permute-start | bytes 3145736 | tf_op jit(solution)/shard_map/ppermute | solution.py:35
  73.6 9.4 %collective-permute-start.2 = (bf16[16,16,1024]{2,1,0:T(8,128)(2,1)}, bf16[16,16,1024]{2,1,0:T(8,128)(2,1)S(1)}, u32[]{:S(2)}, u32[]{:S(2)}) collective-permute-start(bf16[16,16,1024]{2,1,0:T(8,128)(2,1)} %collective-permute-done.refs_1_), channel_id=1, source_target_pairs={{0,32},{1,33},{2,34},{3,35},{4,36},{5,37},{6,38},{7,39},{8,40},{9,... | collective-permute-start | bytes 1572872 | tf_op jit(solution)/shard_map/ppermute | solution.py:35
  75.9 21.6 %collective-permute-start.20 = (bf16[1024,512]{1,0:T(8,128)(2,1)S(1)}, bf16[1024,512]{1,0:T(8,128)(2,1)S(1)}, u32[]{:S(2)}, u32[]{:S(2)}) collective-permute-start(bf16[1024,512]{1,0:T(8,128)(2,1)S(1)} %maximum_maximum_fusion.refs_17_), channel_id=1, source_target_pairs={{0,1},{1,2},{2,3},{3,0},{4,5},{5,6},{6,7},{7,4},{8,9},{9,10},{10,1... | collective-permute-start | bytes 3145736 | tf_op jit(solution)/shard_map/ppermute | solution.py:35
  82.9 9.5 %collective-permute-start.5 = (bf16[16,16,1024]{2,1,0:T(8,128)(2,1)}, bf16[16,16,1024]{2,1,0:T(8,128)(2,1)}, u32[]{:S(2)}, u32[]{:S(2)}) collective-permute-start(bf16[16,16,1024]{2,1,0:T(8,128)(2,1)} %collective-permute-done.3.refs_4_), channel_id=1, source_target_pairs={{0,32},{1,33},{2,34},{3,35},{4,36},{5,37},{6,38},{7,39},{8,40},{9,... | collective-permute-start | bytes 1572872 | tf_op jit(solution)/shard_map/ppermute | solution.py:35
  84.1 15.6 %collective-permute-start.4 = (bf16[16,16,1024]{2,1,0:T(8,128)(2,1)S(1)}, bf16[16,16,1024]{2,1,0:T(8,128)(2,1)}, u32[]{:S(2)}, u32[]{:S(2)}) collective-permute-start(bf16[16,16,1024]{2,1,0:T(8,128)(2,1)S(1)} %collective-permute-done.2.refs_3_), channel_id=1, source_target_pairs={{0,32},{1,33},{2,34},{3,35},{4,36},{5,37},{6,38},{7,39},{8,40},{9,... | collective-permute-start | bytes 1572872 | tf_op jit(solution)/shard_map/ppermute | solution.py:35
  86.5 15.6 %collective-permute-start.10 = (bf16[16,16,1024]{2,1,0:T(8,128)(2,1)}, bf16[16,16,1024]{2,1,0:T(8,128)(2,1)S(1)}, u32[]{:S(2)}, u32[]{:S(2)}) collective-permute-start(bf16[16,16,1024]{2,1,0:T(8,128)(2,1)} %collective-permute-done.3.refs_4_), channel_id=1, source_target_pairs={{0,16},{1,17},{2,18},{3,19},{4,20},{5,21},{6,22},{7,23},{8,24},{9,... | collective-permute-start | bytes 1572872 | tf_op jit(solution)/shard_map/ppermute | solution.py:35
  87.8 15.1 %collective-permute-start.9 = (bf16[16,16,1024]{2,1,0:T(8,128)(2,1)S(1)}, bf16[16,16,1024]{2,1,0:T(8,128)(2,1)S(1)}, u32[]{:S(2)}, u32[]{:S(2)}) collective-permute-start(bf16[16,16,1024]{2,1,0:T(8,128)(2,1)S(1)} %collective-permute-done.2.refs_3_), channel_id=1, source_target_pairs={{0,16},{1,17},{2,18},{3,19},{4,20},{5,21},{6,22},{7,23},{8,24},{9,... | collective-permute-start | bytes 1572872 | tf_op jit(solution)/shard_map/ppermute | solution.py:35
  92.4 20.8 %collective-permute-start.12 = (bf16[16,16,1024]{2,1,0:T(8,128)(2,1)}, bf16[16,16,1024]{2,1,0:T(8,128)(2,1)}, u32[]{:S(2)}, u32[]{:S(2)}) collective-permute-start(bf16[16,16,1024]{2,1,0:T(8,128)(2,1)} %collective-permute-done.5.refs_6_), channel_id=1, source_target_pairs={{0,16},{1,17},{2,18},{3,19},{4,20},{5,21},{6,22},{7,23},{8,24},{9,... | collective-permute-start | bytes 1572872 | tf_op jit(solution)/shard_map/ppermute | solution.py:35
  97.6 1.0 copy-start
  98.5 14.8 %collective-permute-start.7 = (bf16[16,16,1024]{2,1,0:T(8,128)(2,1)}, bf16[16,16,1024]{2,1,0:T(8,128)(2,1)}, u32[]{:S(2)}, u32[]{:S(2)}) collective-permute-start(bf16[16,16,1024]{2,1,0:T(8,128)(2,1)} %collective-permute-done.5.refs_6_), channel_id=1, source_target_pairs={{0,32},{1,33},{2,34},{3,35},{4,36},{5,37},{6,38},{7,39},{8,40},{9,... | collective-permute-start | bytes 1572872 | tf_op jit(solution)/shard_map/ppermute | solution.py:35
  99.7 14.2 %collective-permute-start.6 = (bf16[16,16,1024]{2,1,0:T(8,128)(2,1)}, bf16[16,16,1024]{2,1,0:T(8,128)(2,1)}, u32[]{:S(2)}, u32[]{:S(2)}) collective-permute-start(bf16[16,16,1024]{2,1,0:T(8,128)(2,1)} %collective-permute-done.4.refs_5_), channel_id=1, source_target_pairs={{0,32},{1,33},{2,34},{3,35},{4,36},{5,37},{6,38},{7,39},{8,40},{9,... | collective-permute-start | bytes 1572872 | tf_op jit(solution)/shard_map/ppermute | solution.py:35
  102.9 19.7 %collective-permute-start.23 = (bf16[1024,512]{1,0:T(8,128)(2,1)}, bf16[1024,512]{1,0:T(8,128)(2,1)}, u32[]{:S(2)}, u32[]{:S(2)}) collective-permute-start(bf16[1024,512]{1,0:T(8,128)(2,1)} %collective-permute-done.19.refs_18_), channel_id=1, source_target_pairs={{0,1},{1,2},{2,3},{3,0},{4,5},{5,6},{6,7},{7,4},{8,9},{9,10},{10,1... | collective-permute-start | bytes 3145736 | tf_op jit(solution)/shard_map/ppermute | solution.py:35
  102.9 0.8 copy-start.6
  103.8 18.8 %collective-permute-start.24 = (bf16[1024,512]{1,0:T(8,128)(2,1)}, bf16[1024,512]{1,0:T(8,128)(2,1)}, u32[]{:S(2)}, u32[]{:S(2)}) collective-permute-start(bf16[1024,512]{1,0:T(8,128)(2,1)} %collective-permute-done.22.refs_21_), channel_id=1, source_target_pairs={{0,3},{1,0},{2,1},{3,2},{4,7},{5,4},{6,5},{7,6},{8,11},{9,8},{10,9... | collective-permute-start | bytes 3145736 | tf_op jit(solution)/shard_map/ppermute | solution.py:35
  108.4 13.9 %all-to-all-start.3 = ((bf16[16,32,256]{2,1,0:T(8,128)(2,1)}), bf16[16,32,256]{2,1,0:T(8,128)(2,1)S(1)}, u32[]{:S(2)}, u32[]{:S(2)}) async-start(bf16[16,32,256]{2,1,0:T(8,128)(2,1)} %broadcast_in_dim.15), calls=%async_computation.3 | async-start | bytes 524288 | tf_op jit(solution)/shard_map/all_to_all | solution.py:329
  113.3 9.3 %collective-permute-start.11 = (bf16[16,16,1024]{2,1,0:T(8,128)(2,1)}, bf16[16,16,1024]{2,1,0:T(8,128)(2,1)}, u32[]{:S(2)}, u32[]{:S(2)}) collective-permute-start(bf16[16,16,1024]{2,1,0:T(8,128)(2,1)} %collective-permute-done.4.refs_5_), channel_id=1, source_target_pairs={{0,16},{1,17},{2,18},{3,19},{4,20},{5,21},{6,22},{7,23},{8,24},{9,... | collective-permute-start | bytes 1572872 | tf_op jit(solution)/shard_map/ppermute | solution.py:35
  113.4 9.2 %collective-permute-start.14 = (bf16[16,16,1024]{2,1,0:T(8,128)(2,1)}, bf16[16,16,1024]{2,1,0:T(8,128)(2,1)}, u32[]{:S(2)}, u32[]{:S(2)}) collective-permute-start(bf16[16,16,1024]{2,1,0:T(8,128)(2,1)} %collective-permute-done.7.refs_8_), channel_id=1, source_target_pairs={{0,16},{1,17},{2,18},{3,19},{4,20},{5,21},{6,22},{7,23},{8,24},{9,... | collective-permute-start | bytes 1572872 | tf_op jit(solution)/shard_map/ppermute | solution.py:35
  113.9 8.8 %collective-permute-start.13 = (bf16[16,16,1024]{2,1,0:T(8,128)(2,1)}, bf16[16,16,1024]{2,1,0:T(8,128)(2,1)}, u32[]{:S(2)}, u32[]{:S(2)}) collective-permute-start(bf16[16,16,1024]{2,1,0:T(8,128)(2,1)} %collective-permute-done.6.refs_7_), channel_id=1, source_target_pairs={{0,16},{1,17},{2,18},{3,19},{4,20},{5,21},{6,22},{7,23},{8,24},{9,... | collective-permute-start | bytes 1572872 | tf_op jit(solution)/shard_map/ppermute | solution.py:35
  122.6 1.2 copy-start.1
  123.9 1.0 copy-start.3
  124.9 1.0 copy-start.5
  125.9 1.0 copy-start.7
  146.0 26.5 %copy-start.8 = (bf16[1024,1024]{1,0:T(8,128)(2,1)S(1)}, bf16[1024,1024]{1,0:T(8,128)(2,1)}, u32[]{:S(2)}) copy-start(bf16[1024,1024]{1,0:T(8,128)(2,1)} %get-tuple-element.16) | copy-start | bytes 6291460
  173.2 1.3 collective-permute-start.27
  188.5 1.3 collective-permute-start.29
  190.6 11.9 %all-to-all-start.7 = ((f32[16,24,128]{2,1,0:T(8,128)}), f32[16,24,128]{2,1,0:T(8,128)S(1)}, u32[]{:S(2)}, u32[]{:S(2)}) async-start(f32[16,24,128]{2,1,0:T(8,128)} %broadcast_in_dim.20), calls=%async_computation.7 | async-start | bytes 393216 | tf_op jit(solution)/shard_map/all_to_all | solution.py:206
  194.3 1.2 collective-permute-start.28
  (4 other events, 3.0 us)

commit v4 on v3

--- a/solution.py
+++ b/solution.py
@@ -128,8 +128,8 @@
 def tile_kernel(index, *refs):
     columns, rows = refs[:16], refs[16:24]
     prior, spread, first = refs[24:27]
-    out, rounded, image = refs[27:30]
-    total, old, left, stage, old_sem, left_sem, stage_sem, out_sem = refs[30:]
+    out, rounded, second, gram = refs[27:31]
+    total, old, image, left, stage, old_sem, left_sem, stage_sem, out_sem = refs[31:]
 
     def fetch_row(i):
         return pltpu.make_async_copy(rows[i], left.at[i, pl.ds(0, 1024)], left_sem.at[i])
@@ -169,6 +169,9 @@
             return carry
 
         lax.fori_loop(0, 4, step, 0)
+    vectors = image[...]
+    second[...] = dot_t(vectors.astype(BF16), rounded[...], ((1,), (1,)))
+    gram[...] = dot_t(vectors, vectors, ((1,), (1,)))
     for n in range(4):
         at = pl.ds(n * 256, 256)
         pltpu.make_async_copy(old.at[:, at], out.at[:, at], out_sem.at[n]).wait()
@@ -178,15 +181,17 @@
     return pl.pallas_call(
         tile_kernel,
         in_specs=[SMEM] + [ANY] * 25 + [VMEM] * 2,
-        out_specs=[ANY, VMEM, VMEM],
+        out_specs=[ANY, VMEM, VMEM, VMEM],
         out_shape=[
             jax.ShapeDtypeStruct((1024, 1024), F32),
             jax.ShapeDtypeStruct((1024, 1024), BF16),
             jax.ShapeDtypeStruct((K, 1024), F32),
+            jax.ShapeDtypeStruct((K, K), F32),
         ],
         scratch_shapes=[
             pltpu.VMEM((1056, 1024), F32),
             pltpu.VMEM((1024, 1024), F32),
+            pltpu.VMEM((K, 1024), F32),
             pltpu.VMEM((8, 1056, 512), BF16),
             pltpu.VMEM((8, 512, 1024), BF16),
             pltpu.SemaphoreType.DMA,
@@ -346,9 +351,8 @@
     last0 = second_axis(f0, 1)
     last1 = second_axis(g1, -1)
     rows = [h0, h1, f0, f1, g0, g1, last0, last1]
-    grm, rounded, image = tile(index, columns, rows, prior, spread, early[:, :1024])
-    gram1 = dot_t(image, image, ((1,), (1,)))
-    packed = with_gram(dot_t(image.astype(BF16), rounded, ((1,), (1,))), gram1)
+    grm, rounded, second, gram1 = tile(index, columns, rows, prior, spread, early[:, :1024])
+    packed = with_gram(second, gram1)
     packed = bcast_sum(packed, "x").astype(BF16)
     second, gram1 = split_gram(bcast_sum(packed, "y"))
     second, diagonal = solve(gram1, second)

time: 207 us -> 205 us (level)
  matrix products: 6.23 us -> 3.73 us
    dot_general x8 -> x6, matrix products: 6.23 us -> 3.73 us  [dot_t(): return lax.dot_general(a, b, (dims, ((), ())), preferred_element_type=F32)]
where the time goes in v4:
time: 205 us; the launch traced here: 203 us
  waiting for transfers between devices  61.7 us (30%)
  starting transfers between devices  56.4 us (28%)
  blocking collectives  35.9 us (18%)
  Pallas kernels  27.9 us (14%)
  local copies, waits for them, and re-layouts  13.7 us (7%)
  matrix products  3.73 us (2%)
  other arithmetic  2.06 us (1%)
    all_to_all x3, blocking collectives, bcast_sum(): lax.all_to_all(copies, axis, 0, 0, tiled=True).astype(F32).sum(axis=0)  35.9 us
    ppermute x30, starting transfers between devices, send(): return lax.ppermute(array, ALL, pairs)  26.6 us
    ppermute x30, waiting for transfers between devices, send(): return lax.ppermute(array, ALL, pairs)  24.7 us
    pallas_call x1, Pallas kernels, tile(): pl.pallas_call(tile_kernel, in_specs=[SMEM] + [ANY] * 25 + [VMEM] * 2, ou...  18.8 us
    all_to_all x1, waiting for transfers between devices, body(): piece = lax.all_to_all(standard, ROW, 0, 0, tiled=True)  11.6 us
    all_to_all x1, waiting for transfers between devices, body(): own = lax.all_to_all(standard, COL, 0, 0, tiled=True)  11.2 us
    all_to_all x2, starting transfers between devices, bcast_sum(): lax.all_to_all(copies, axis, 0, 0, tiled=True).astype(F32).sum(axis=0)  9.18 us
    unnamed x34, local copies, waits for them, and re-layouts  9.17 us
  transfers between devices with their start and end apart: 35, of which 15 were waited for; matrix products, arithmetic and copies ran while one was open for 4% of the time, Pallas kernels for 0%

profile of v4, /device:TPU:32, one launch (start us, length us, event | category | flops | bytes accessed | tf_op | source)
XLA Modules:
  0.0 202.5 jit_solution(17351942184368251867)
XLA Ops:
  0.7 4.4 %standardize.1 = bf16[16,16,1024]{2,1,0:T(8,128)(2,1)} custom-call(s32[16]{0:T(128)} %index.1, f32[128,128]{1,0:T(8,128)} %bitcast.22, s32[16,16384]{1,0:T(8,128)} %genotypes.1), custom_call_target="tpu_custom_call" | custom-call | tf_op jit(solution)/shard_map/standardize/pallas_call | solution.py:83
  5.1 8.6 %all-to-all-start = ((bf16[16,16,1024]{2,1,0:T(8,128)(2,1)}), bf16[16,16,1024]{2,1,0:T(8,128)(2,1)S(1)}, u32[]{:S(2)}, u32[]{:S(2)}) async-start(bf16[16,16,1024]{2,1,0:T(8,128)(2,1)} %standardize.1), calls=%async_computation | async-start | bytes 1048576 | tf_op jit(solution)/shard_map/all_to_all | solution.py:314
  13.7 2.6 %fusion = f32[20,1024]{1,0:T(8,128)S(1)} fusion(f32[1024,1024]{1,0:T(8,128)} %refs_24_.1, f32[1024,20]{0,1:T(8,128)S(1)} %copy-done.11), kind=kOutput, calls=%fused_computation | convolution fusion | flops 43032576 | bytes 4358144 | tf_op jit(solution)/shard_map/dot_general | solution.py:249
  16.3 11.6 %all-to-all-done.piece = bf16[16,16,1024]{2,1,0:T(8,128)(2,1)S(1)} async-done(((bf16[16,16,1024]{2,1,0:T(8,128)(2,1)}), bf16[16,16,1024]{2,1,0:T(8,128)(2,1)S(1)}, u32[]{:S(2)}, u32[]{:S(2)}) %all-to-all-start) | async-done | bytes 524320 | tf_op jit(solution)/shard_map/all_to_all | solution.py:314
  28.6 2.8 %collective-permute-start.16 = (bf16[1024,256]{1,0:T(8,128)(2,1)S(1)}, bf16[1024,256]{1,0:T(8,128)(2,1)S(1)}, u32[]{:S(2)}, u32[]{:S(2)}) collective-permute-start(bf16[1024,256]{1,0:T(8,128)(2,1)S(1)} %turn.1), channel_id=1, source_target_pairs={{0,12},{1,13},{2,14},{3,15},{4,0},{5,1},{6,2},{7,3},{8,4},{9,5},{1... | collective-permute-start | bytes 1572872 | tf_op jit(solution)/shard_map/ppermute | solution.py:35
  31.5 7.2 %all-to-all-start.1 = ((bf16[16,16,1024]{2,1,0:T(8,128)(2,1)}), bf16[16,16,1024]{2,1,0:T(8,128)(2,1)S(1)}, u32[]{:S(2)}, u32[]{:S(2)}) async-start(bf16[16,16,1024]{2,1,0:T(8,128)(2,1)} %standardize.1), calls=%async_computation.1 | async-start | bytes 1048576 | tf_op jit(solution)/shard_map/all_to_all | solution.py:316
  39.1 11.2 %all-to-all-done.1.refs_0_ = bf16[16,16,1024]{2,1,0:T(8,128)(2,1)S(1)} async-done(((bf16[16,16,1024]{2,1,0:T(8,128)(2,1)}), bf16[16,16,1024]{2,1,0:T(8,128)(2,1)S(1)}, u32[]{:S(2)}, u32[]{:S(2)}) %all-to-all-start.1) | async-done | bytes 524320 | tf_op jit(solution)/shard_map/all_to_all | solution.py:316
  50.4 1.9 collective-permute-start.1
  53.0 5.7 %all-to-all-start.2 = ((bf16[8,20,640]{2,1,0:T(8,128)(2,1)}), bf16[8,20,640]{2,1,0:T(8,128)(2,1)S(1)}, u32[]{:S(2)}, u32[]{:S(2)}) async-start(bf16[8,20,640]{2,1,0:T(8,128)(2,1)} %broadcast_in_dim.14), calls=%async_computation.2 | async-start | bytes 491520 | tf_op jit(solution)/shard_map/all_to_all | solution.py:211
  58.7 1.3 collective-permute-start.18
  61.6 0.9 collective-permute-start.21
  62.7 3.2 %collective-permute-done.18 = bf16[512,256]{1,0:T(8,128)(2,1)S(1)} collective-permute-done((bf16[512,256]{1,0:T(8,128)(2,1)S(1)}, bf16[512,256]{1,0:T(8,128)(2,1)S(1)}, u32[]{:S(2)}, u32[]{:S(2)}) %collective-permute-start.18) | collective-permute-done | bytes 262176 | tf_op jit(solution)/shard_map/ppermute | solution.py:35
  66.7 1.5 collective-permute-start.3
  68.9 1.3 maximum_maximum_fusion.refs_17_
  70.9 2.7 %collective-permute-start.22 = (bf16[1024,512]{1,0:T(8,128)(2,1)S(1)}, bf16[1024,512]{1,0:T(8,128)(2,1)}, u32[]{:S(2)}, u32[]{:S(2)}) collective-permute-start(bf16[1024,512]{1,0:T(8,128)(2,1)S(1)} %maximum_maximum_fusion.refs_17_), channel_id=1, source_target_pairs={{0,3},{1,0},{2,1},{3,2},{4,7},{5,4},{6,5},{7,6},{8,11},{9,8},{10,9... | collective-permute-start | bytes 3145736 | tf_op jit(solution)/shard_map/ppermute | solution.py:35
  73.6 1.2 collective-permute-start.2
  74.7 1.2 collective-permute-done.3.refs_4_
  75.9 0.8 collective-permute-start.20
  76.8 6.1 %collective-permute-done.2.refs_3_ = bf16[16,16,1024]{2,1,0:T(8,128)(2,1)S(1)} collective-permute-done((bf16[16,16,1024]{2,1,0:T(8,128)(2,1)}, bf16[16,16,1024]{2,1,0:T(8,128)(2,1)S(1)}, u32[]{:S(2)}, u32[]{:S(2)}) %collective-permute-start.2) | collective-permute-done | bytes 524320 | tf_op jit(solution)/shard_map/ppermute | solution.py:35
  82.9 1.2 collective-permute-start.5
  84.1 2.4 %collective-permute-start.4 = (bf16[16,16,1024]{2,1,0:T(8,128)(2,1)S(1)}, bf16[16,16,1024]{2,1,0:T(8,128)(2,1)}, u32[]{:S(2)}, u32[]{:S(2)}) collective-permute-start(bf16[16,16,1024]{2,1,0:T(8,128)(2,1)S(1)} %collective-permute-done.2.refs_3_), channel_id=1, source_target_pairs={{0,32},{1,33},{2,34},{3,35},{4,36},{5,37},{6,38},{7,39},{8,40},{9,... | collective-permute-start | bytes 1572872 | tf_op jit(solution)/shard_map/ppermute | solution.py:35
  86.5 1.3 collective-permute-done.22.refs_21_
  88.7 3.8 %collective-permute-done.5.refs_6_ = bf16[16,16,1024]{2,1,0:T(8,128)(2,1)} collective-permute-done((bf16[16,16,1024]{2,1,0:T(8,128)(2,1)}, bf16[16,16,1024]{2,1,0:T(8,128)(2,1)}, u32[]{:S(2)}, u32[]{:S(2)}) %collective-permute-start.5) | collective-permute-done | bytes 524320 | tf_op jit(solution)/shard_map/ppermute | solution.py:35
  92.4 5.1 %collective-permute-done.20.refs_19_ = bf16[1024,512]{1,0:T(8,128)(2,1)S(1)} collective-permute-done((bf16[1024,512]{1,0:T(8,128)(2,1)S(1)}, bf16[1024,512]{1,0:T(8,128)(2,1)S(1)}, u32[]{:S(2)}, u32[]{:S(2)}) %collective-permute-start.20) | collective-permute-done | bytes 1048608 | tf_op jit(solution)/shard_map/ppermute | solution.py:35
  97.6 1.0 copy-done
  98.5 1.2 collective-permute-start.7
  99.7 2.4 %collective-permute-start.6 = (bf16[16,16,1024]{2,1,0:T(8,128)(2,1)}, bf16[16,16,1024]{2,1,0:T(8,128)(2,1)}, u32[]{:S(2)}, u32[]{:S(2)}) collective-permute-start(bf16[16,16,1024]{2,1,0:T(8,128)(2,1)} %collective-permute-done.4.refs_5_), channel_id=1, source_target_pairs={{0,32},{1,33},{2,34},{3,35},{4,36},{5,37},{6,38},{7,39},{8,40},{9,... | collective-permute-start | bytes 1572872 | tf_op jit(solution)/shard_map/ppermute | solution.py:35
  102.1 0.8 copy-done.4
  102.9 0.8 copy-done.6
  103.8 3.2 %collective-permute-start.24 = (bf16[1024,512]{1,0:T(8,128)(2,1)}, bf16[1024,512]{1,0:T(8,128)(2,1)}, u32[]{:S(2)}, u32[]{:S(2)}) collective-permute-start(bf16[1024,512]{1,0:T(8,128)(2,1)} %collective-permute-done.22.refs_21_), channel_id=1, source_target_pairs={{0,3},{1,0},{2,1},{3,2},{4,7},{5,4},{6,5},{7,6},{8,11},{9,8},{10,9... | collective-permute-start | bytes 3145736 | tf_op jit(solution)/shard_map/ppermute | solution.py:35
  108.4 4.8 %all-to-all-start.3 = ((bf16[16,32,256]{2,1,0:T(8,128)(2,1)}), bf16[16,32,256]{2,1,0:T(8,128)(2,1)S(1)}, u32[]{:S(2)}, u32[]{:S(2)}) async-start(bf16[16,32,256]{2,1,0:T(8,128)(2,1)} %broadcast_in_dim.15), calls=%async_computation.3 | async-start | bytes 524288 | tf_op jit(solution)/shard_map/all_to_all | solution.py:334
  114.4 0.9 slice.65.refs_26_
  115.3 7.1 %all-to-all-done.3 = bf16[16,32,256]{2,1,0:T(8,128)(2,1)S(1)} async-done(((bf16[16,32,256]{2,1,0:T(8,128)(2,1)}), bf16[16,32,256]{2,1,0:T(8,128)(2,1)S(1)}, u32[]{:S(2)}, u32[]{:S(2)}) %all-to-all-start.3) | async-done | bytes 262176 | tf_op jit(solution)/shard_map/all_to_all | solution.py:334
  122.6 1.2 copy-done.1
  123.9 1.0 copy-done.3
  124.9 1.0 copy-done.5
  125.9 1.0 copy-done.7
  127.0 18.8 %tile.1 = (f32[1024,1024]{1,0:T(8,128)}, bf16[1024,1024]{1,0:T(8,128)(2,1)}, f32[20,1024]{1,0:T(8,128)S(1)}, f32[20,20]{1,0:T(8,128)S(1)}) custom-call(s32[16]{0:T(128)S(1)} %fusion.15.index, bf16[16,16,1024]{2,1,0:T(8,128)(2,1)S(1)} %all-to-all-done.1.refs_0_, bf16[16,16,1024]{2,1,0:T(8,128)(2,1)} %collective-permute-done.refs_1_, ...), custom_call_target="tpu_custom_call" | custom-call | flops 8589934592 | bytes 27262976 | tf_op jit(solution)/shard_map/tile/pallas_call | solution.py:181
  146.2 11.0 %all_to_all.40 = bf16[4,24,1024]{2,1,0:T(8,128)(2,1)S(1)} all-to-all(bf16[4,24,1024]{2,1,0:T(8,128)(2,1)S(1)} %broadcast_in_dim.17), channel_id=1, replica_groups=mesh['z'=8,'core'=2,'x'=4,'y'=4] {'x'}, dimensions={0} | all-to-all | bytes 393216 | tf_op jit(solution)/shard_map/all_to_all | solution.py:211
  157.2 11.1 %all_to_all.41 = bf16[4,24,1024]{2,1,0:T(8,128)(2,1)S(1)} all-to-all(bf16[4,24,1024]{2,1,0:T(8,128)(2,1)S(1)} %broadcast_in_dim.18), channel_id=1, replica_groups=mesh['z'=8,'core'=2,'x'=4,'y'=4] {'y'}, dimensions={0} | all-to-all | bytes 393216 | tf_op jit(solution)/shard_map/all_to_all | solution.py:211
  168.5 1.6 solve.1
  171.0 1.1 collective-permute-done.27
  172.2 13.8 %all_to_all.42 = bf16[8,24,512]{2,1,0:T(8,128)(2,1)S(1)} all-to-all(bf16[8,24,512]{2,1,0:T(8,128)(2,1)S(1)} %broadcast_in_dim.19), channel_id=1, replica_groups=mesh['z'=8,'core'=2,'x'=4,'y'=4] {'z'}, dimensions={0} | all-to-all | bytes 393216 | tf_op jit(solution)/shard_map/all_to_all | solution.py:211
  186.2 1.2 collective-permute-done.29
  188.2 3.5 %all-to-all-start.7 = ((f32[16,24,128]{2,1,0:T(8,128)}), f32[16,24,128]{2,1,0:T(8,128)S(1)}, u32[]{:S(2)}, u32[]{:S(2)}) async-start(f32[16,24,128]{2,1,0:T(8,128)} %broadcast_in_dim.20), calls=%async_computation.7 | async-start | bytes 393216 | tf_op jit(solution)/shard_map/all_to_all | solution.py:211
  192.1 1.0 collective-permute-done.28
  193.1 7.1 %all-to-all-done.7 = f32[16,24,128]{2,1,0:T(8,128)S(1)} async-done(((f32[16,24,128]{2,1,0:T(8,128)}), f32[16,24,128]{2,1,0:T(8,128)S(1)}, u32[]{:S(2)}, u32[]{:S(2)}) %all-to-all-start.7) | async-done | bytes 196640 | tf_op jit(solution)/shard_map/all_to_all | solution.py:211
  200.2 2.3 %last.1 = (f32[20,1024]{1,0:T(8,128)}, f32[3,20]{1,0:T(4,128)}) custom-call(f32[1,20]{1,0:T(1,128)S(1)} %get-tuple-element.18.first, f32[20,20]{1,0:T(8,128)S(1)} %add.110.gram2, f32[20,20]{1,0:T(8,128)S(1)} %bitcast.18, f32[20,1024]{1,0:T(8,128)S(1)} %maximum_select_fusion.1.wide), custom_call_target="tpu_custom_call" | custom-call | tf_op jit(solution)/shard_map/last/pallas_call | solution.py:291
  (115 shorter events, 12.2 us)
Async XLA Ops:
  0.6 13.1 %copy-start.13 = (s32[16]{0:T(128)S(1)}, s32[16]{0:T(128)}, u32[]{:S(2)}) copy-start(s32[16]{0:T(128)} %constant.99.clone) | copy-start | bytes 196
  0.6 13.0 %copy-start.14 = (s32[16]{0:T(128)S(1)}, s32[16]{0:T(128)}, u32[]{:S(2)}) copy-start(s32[16]{0:T(128)} %constant.98.clone) | copy-start | bytes 196
  0.7 13.1 %copy-start.11 = (f32[1024,20]{0,1:T(8,128)S(1)}, f32[1024,20]{0,1:T(8,128)}, u32[]{:S(2)}) copy-start(f32[1024,20]{0,1:T(8,128)} %param.13) | copy-start | bytes 245764
  5.1 22.8 %all-to-all-start = ((bf16[16,16,1024]{2,1,0:T(8,128)(2,1)}), bf16[16,16,1024]{2,1,0:T(8,128)(2,1)S(1)}, u32[]{:S(2)}, u32[]{:S(2)}) async-start(bf16[16,16,1024]{2,1,0:T(8,128)(2,1)} %standardize.1), calls=%async_computation | async-start | bytes 1048576 | tf_op jit(solution)/shard_map/all_to_all | solution.py:314
  28.6 30.0 %collective-permute-start.16 = (bf16[1024,256]{1,0:T(8,128)(2,1)S(1)}, bf16[1024,256]{1,0:T(8,128)(2,1)S(1)}, u32[]{:S(2)}, u32[]{:S(2)}) collective-permute-start(bf16[1024,256]{1,0:T(8,128)(2,1)S(1)} %turn.1), channel_id=1, source_target_pairs={{0,12},{1,13},{2,14},{3,15},{4,0},{5,1},{6,2},{7,3},{8,4},{9,5},{1... | collective-permute-start | bytes 1572872 | tf_op jit(solution)/shard_map/ppermute | solution.py:35
  31.5 28.5 %collective-permute-start.15 = (bf16[1024,256]{1,0:T(8,128)(2,1)S(1)}, bf16[1024,256]{1,0:T(8,128)(2,1)S(1)}, u32[]{:S(2)}, u32[]{:S(2)}) collective-permute-start(bf16[1024,256]{1,0:T(8,128)(2,1)S(1)} %turn.1), channel_id=1, source_target_pairs={{0,4},{1,5},{2,6},{3,7},{4,8},{5,9},{6,10},{7,11},{8,12},{9,13},{1... | collective-permute-start | bytes 1572872 | tf_op jit(solution)/shard_map/ppermute | solution.py:35
  31.5 18.9 %all-to-all-start.1 = ((bf16[16,16,1024]{2,1,0:T(8,128)(2,1)}), bf16[16,16,1024]{2,1,0:T(8,128)(2,1)S(1)}, u32[]{:S(2)}, u32[]{:S(2)}) async-start(bf16[16,16,1024]{2,1,0:T(8,128)(2,1)} %standardize.1), calls=%async_computation.1 | async-start | bytes 1048576 | tf_op jit(solution)/shard_map/all_to_all | solution.py:316
  39.0 13.2 %collective-permute-start.25 = (f32[20,640]{1,0:T(8,128)S(1)}, f32[20,640]{1,0:T(8,128)S(1)}, u32[]{:S(2)}, u32[]{:S(2)}) collective-permute-start(f32[20,640]{1,0:T(8,128)S(1)} %slice_select_fusion), channel_id=1, source_target_pairs={{0,16},{1,17},{2,18},{3,19},{4,20},{5,21},{6,22},{7,23},{8,24},{9,... | collective-permute-start | bytes 153608 | tf_op jit(solution)/shard_map/ppermute | solution.py:35
  50.4 12.4 %collective-permute-start.1 = (bf16[16,16,1024]{2,1,0:T(8,128)(2,1)S(1)}, bf16[16,16,1024]{2,1,0:T(8,128)(2,1)S(1)}, u32[]{:S(2)}, u32[]{:S(2)}) collective-permute-start(bf16[16,16,1024]{2,1,0:T(8,128)(2,1)S(1)} %all-to-all-done.1.refs_0_), channel_id=1, source_target_pairs={{0,32},{1,33},{2,34},{3,35},{4,36},{5,37},{6,38},{7,39},{8,40},{9,... | collective-permute-start | bytes 1572872 | tf_op jit(solution)/shard_map/ppermute | solution.py:35
  53.0 15.2 %all-to-all-start.2 = ((bf16[8,20,640]{2,1,0:T(8,128)(2,1)}), bf16[8,20,640]{2,1,0:T(8,128)(2,1)S(1)}, u32[]{:S(2)}, u32[]{:S(2)}) async-start(bf16[8,20,640]{2,1,0:T(8,128)(2,1)} %broadcast_in_dim.14), calls=%async_computation.2 | async-start | bytes 491520 | tf_op jit(solution)/shard_map/all_to_all | solution.py:211
  58.7 2.1 %copy-start.9 = (bf16[1024,256]{1,0:T(8,128)(2,1)}, bf16[1024,256]{1,0:T(8,128)(2,1)S(1)}, u32[]{:S(2)}) copy-start(bf16[1024,256]{1,0:T(8,128)(2,1)S(1)} %collective-permute-done.16) | copy-start | bytes 1572868
  58.7 7.3 %collective-permute-start.18 = (bf16[512,256]{1,0:T(8,128)(2,1)S(1)}, bf16[512,256]{1,0:T(8,128)(2,1)S(1)}, u32[]{:S(2)}, u32[]{:S(2)}) collective-permute-start(bf16[512,256]{1,0:T(8,128)(2,1)S(1)} %slice.62), channel_id=1, source_target_pairs={{0,12},{1,13},{2,14},{3,15},{4,0},{5,1},{6,2},{7,3},{8,4},{9,5},{1... | collective-permute-start | bytes 786440 | tf_op jit(solution)/shard_map/ppermute | solution.py:35
  60.0 10.9 %collective-permute-start = (bf16[16,16,1024]{2,1,0:T(8,128)(2,1)S(1)}, bf16[16,16,1024]{2,1,0:T(8,128)(2,1)}, u32[]{:S(2)}, u32[]{:S(2)}) collective-permute-start(bf16[16,16,1024]{2,1,0:T(8,128)(2,1)S(1)} %all-to-all-done.1.refs_0_), channel_id=1, source_target_pairs={{0,16},{1,17},{2,18},{3,19},{4,20},{5,21},{6,22},{7,23},{8,24},{9,... | collective-permute-start | bytes 1572872 | tf_op jit(solution)/shard_map/ppermute | solution.py:35
  60.8 7.9 %collective-permute-start.17 = (bf16[512,256]{1,0:T(8,128)(2,1)}, bf16[512,256]{1,0:T(8,128)(2,1)}, u32[]{:S(2)}, u32[]{:S(2)}) collective-permute-start(bf16[512,256]{1,0:T(8,128)(2,1)} %slice.61), channel_id=1, source_target_pairs={{0,4},{1,5},{2,6},{3,7},{4,8},{5,9},{6,10},{7,11},{8,12},{9,13},{1... | collective-permute-start | bytes 786440 | tf_op jit(solution)/shard_map/ppermute | solution.py:35
  61.6 52.6 %copy-start.15 = (s32[16]{0:T(128)S(1)}, s32[16]{0:T(128)}, u32[]{:S(2)}) copy-start(s32[16]{0:T(128)} %constant.101.clone) | copy-start | bytes 196
  61.6 52.6 %copy-start.16 = (s32[16]{0:T(128)S(1)}, s32[16]{0:T(128)}, u32[]{:S(2)}) copy-start(s32[16]{0:T(128)} %constant.100.clone) | copy-start | bytes 196
  61.6 22.5 %collective-permute-start.21 = (bf16[1024,512]{1,0:T(8,128)(2,1)S(1)}, bf16[1024,512]{1,0:T(8,128)(2,1)}, u32[]{:S(2)}, u32[]{:S(2)}) collective-permute-start(bf16[1024,512]{1,0:T(8,128)(2,1)S(1)} %pad_maximum_fusion.refs_16_), channel_id=1, source_target_pairs={{0,3},{1,0},{2,1},{3,2},{4,7},{5,4},{6,5},{7,6},{8,11},{9,8},{10,9... | collective-permute-start | bytes 3145736 | tf_op jit(solution)/shard_map/ppermute | solution.py:35
  62.7 10.8 %collective-permute-start.8 = (bf16[16,16,1024]{2,1,0:T(8,128)(2,1)S(1)}, bf16[16,16,1024]{2,1,0:T(8,128)(2,1)}, u32[]{:S(2)}, u32[]{:S(2)}) collective-permute-start(bf16[16,16,1024]{2,1,0:T(8,128)(2,1)S(1)} %collective-permute-done.1.refs_2_), channel_id=1, source_target_pairs={{0,16},{1,17},{2,18},{3,19},{4,20},{5,21},{6,22},{7,23},{8,24},{9,... | collective-permute-start | bytes 1572872 | tf_op jit(solution)/shard_map/ppermute | solution.py:35
  66.7 9.3 %collective-permute-start.3 = (bf16[16,16,1024]{2,1,0:T(8,128)(2,1)S(1)}, bf16[16,16,1024]{2,1,0:T(8,128)(2,1)}, u32[]{:S(2)}, u32[]{:S(2)}) collective-permute-start(bf16[16,16,1024]{2,1,0:T(8,128)(2,1)S(1)} %collective-permute-done.1.refs_2_), channel_id=1, source_target_pairs={{0,32},{1,33},{2,34},{3,35},{4,36},{5,37},{6,38},{7,39},{8,40},{9,... | collective-permute-start | bytes 1572872 | tf_op jit(solution)/shard_map/ppermute | solution.py:35
  68.7 1.6 collective-permute-start.26
  70.2 16.3 %collective-permute-start.19 = (bf16[1024,512]{1,0:T(8,128)(2,1)S(1)}, bf16[1024,512]{1,0:T(8,128)(2,1)}, u32[]{:S(2)}, u32[]{:S(2)}) collective-permute-start(bf16[1024,512]{1,0:T(8,128)(2,1)S(1)} %pad_maximum_fusion.refs_16_), channel_id=1, source_target_pairs={{0,1},{1,2},{2,3},{3,0},{4,5},{5,6},{6,7},{7,4},{8,9},{9,10},{10,1... | collective-permute-start | bytes 3145736 | tf_op jit(solution)/shard_map/ppermute | solution.py:35
  70.9 17.0 %collective-permute-start.22 = (bf16[1024,512]{1,0:T(8,128)(2,1)S(1)}, bf16[1024,512]{1,0:T(8,128)(2,1)}, u32[]{:S(2)}, u32[]{:S(2)}) collective-permute-start(bf16[1024,512]{1,0:T(8,128)(2,1)S(1)} %maximum_maximum_fusion.refs_17_), channel_id=1, source_target_pairs={{0,3},{1,0},{2,1},{3,2},{4,7},{5,4},{6,5},{7,6},{8,11},{9,8},{10,9... | collective-permute-start | bytes 3145736 | tf_op jit(solution)/shard_map/ppermute | solution.py:35
  73.6 9.4 %collective-permute-start.2 = (bf16[16,16,1024]{2,1,0:T(8,128)(2,1)}, bf16[16,16,1024]{2,1,0:T(8,128)(2,1)S(1)}, u32[]{:S(2)}, u32[]{:S(2)}) collective-permute-start(bf16[16,16,1024]{2,1,0:T(8,128)(2,1)} %collective-permute-done.refs_1_), channel_id=1, source_target_pairs={{0,32},{1,33},{2,34},{3,35},{4,36},{5,37},{6,38},{7,39},{8,40},{9,... | collective-permute-start | bytes 1572872 | tf_op jit(solution)/shard_map/ppermute | solution.py:35
  75.9 21.6 %collective-permute-start.20 = (bf16[1024,512]{1,0:T(8,128)(2,1)S(1)}, bf16[1024,512]{1,0:T(8,128)(2,1)S(1)}, u32[]{:S(2)}, u32[]{:S(2)}) collective-permute-start(bf16[1024,512]{1,0:T(8,128)(2,1)S(1)} %maximum_maximum_fusion.refs_17_), channel_id=1, source_target_pairs={{0,1},{1,2},{2,3},{3,0},{4,5},{5,6},{6,7},{7,4},{8,9},{9,10},{10,1... | collective-permute-start | bytes 3145736 | tf_op jit(solution)/shard_map/ppermute | solution.py:35
  82.9 9.5 %collective-permute-start.5 = (bf16[16,16,1024]{2,1,0:T(8,128)(2,1)}, bf16[16,16,1024]{2,1,0:T(8,128)(2,1)}, u32[]{:S(2)}, u32[]{:S(2)}) collective-permute-start(bf16[16,16,1024]{2,1,0:T(8,128)(2,1)} %collective-permute-done.3.refs_4_), channel_id=1, source_target_pairs={{0,32},{1,33},{2,34},{3,35},{4,36},{5,37},{6,38},{7,39},{8,40},{9,... | collective-permute-start | bytes 1572872 | tf_op jit(solution)/shard_map/ppermute | solution.py:35
  84.1 15.6 %collective-permute-start.4 = (bf16[16,16,1024]{2,1,0:T(8,128)(2,1)S(1)}, bf16[16,16,1024]{2,1,0:T(8,128)(2,1)}, u32[]{:S(2)}, u32[]{:S(2)}) collective-permute-start(bf16[16,16,1024]{2,1,0:T(8,128)(2,1)S(1)} %collective-permute-done.2.refs_3_), channel_id=1, source_target_pairs={{0,32},{1,33},{2,34},{3,35},{4,36},{5,37},{6,38},{7,39},{8,40},{9,... | collective-permute-start | bytes 1572872 | tf_op jit(solution)/shard_map/ppermute | solution.py:35
  86.5 15.6 %collective-permute-start.10 = (bf16[16,16,1024]{2,1,0:T(8,128)(2,1)}, bf16[16,16,1024]{2,1,0:T(8,128)(2,1)S(1)}, u32[]{:S(2)}, u32[]{:S(2)}) collective-permute-start(bf16[16,16,1024]{2,1,0:T(8,128)(2,1)} %collective-permute-done.3.refs_4_), channel_id=1, source_target_pairs={{0,16},{1,17},{2,18},{3,19},{4,20},{5,21},{6,22},{7,23},{8,24},{9,... | collective-permute-start | bytes 1572872 | tf_op jit(solution)/shard_map/ppermute | solution.py:35
  87.8 15.1 %collective-permute-start.9 = (bf16[16,16,1024]{2,1,0:T(8,128)(2,1)S(1)}, bf16[16,16,1024]{2,1,0:T(8,128)(2,1)S(1)}, u32[]{:S(2)}, u32[]{:S(2)}) collective-permute-start(bf16[16,16,1024]{2,1,0:T(8,128)(2,1)S(1)} %collective-permute-done.2.refs_3_), channel_id=1, source_target_pairs={{0,16},{1,17},{2,18},{3,19},{4,20},{5,21},{6,22},{7,23},{8,24},{9,... | collective-permute-start | bytes 1572872 | tf_op jit(solution)/shard_map/ppermute | solution.py:35
  92.4 20.8 %collective-permute-start.12 = (bf16[16,16,1024]{2,1,0:T(8,128)(2,1)}, bf16[16,16,1024]{2,1,0:T(8,128)(2,1)}, u32[]{:S(2)}, u32[]{:S(2)}) collective-permute-start(bf16[16,16,1024]{2,1,0:T(8,128)(2,1)} %collective-permute-done.5.refs_6_), channel_id=1, source_target_pairs={{0,16},{1,17},{2,18},{3,19},{4,20},{5,21},{6,22},{7,23},{8,24},{9,... | collective-permute-start | bytes 1572872 | tf_op jit(solution)/shard_map/ppermute | solution.py:35
  97.6 1.0 copy-start
  98.5 14.8 %collective-permute-start.7 = (bf16[16,16,1024]{2,1,0:T(8,128)(2,1)}, bf16[16,16,1024]{2,1,0:T(8,128)(2,1)}, u32[]{:S(2)}, u32[]{:S(2)}) collective-permute-start(bf16[16,16,1024]{2,1,0:T(8,128)(2,1)} %collective-permute-done.5.refs_6_), channel_id=1, source_target_pairs={{0,32},{1,33},{2,34},{3,35},{4,36},{5,37},{6,38},{7,39},{8,40},{9,... | collective-permute-start | bytes 1572872 | tf_op jit(solution)/shard_map/ppermute | solution.py:35
  99.7 14.2 %collective-permute-start.6 = (bf16[16,16,1024]{2,1,0:T(8,128)(2,1)}, bf16[16,16,1024]{2,1,0:T(8,128)(2,1)}, u32[]{:S(2)}, u32[]{:S(2)}) collective-permute-start(bf16[16,16,1024]{2,1,0:T(8,128)(2,1)} %collective-permute-done.4.refs_5_), channel_id=1, source_target_pairs={{0,32},{1,33},{2,34},{3,35},{4,36},{5,37},{6,38},{7,39},{8,40},{9,... | collective-permute-start | bytes 1572872 | tf_op jit(solution)/shard_map/ppermute | solution.py:35
  102.9 19.7 %collective-permute-start.23 = (bf16[1024,512]{1,0:T(8,128)(2,1)}, bf16[1024,512]{1,0:T(8,128)(2,1)}, u32[]{:S(2)}, u32[]{:S(2)}) collective-permute-start(bf16[1024,512]{1,0:T(8,128)(2,1)} %collective-permute-done.19.refs_18_), channel_id=1, source_target_pairs={{0,1},{1,2},{2,3},{3,0},{4,5},{5,6},{6,7},{7,4},{8,9},{9,10},{10,1... | collective-permute-start | bytes 3145736 | tf_op jit(solution)/shard_map/ppermute | solution.py:35
  102.9 0.8 copy-start.6
  103.8 18.8 %collective-permute-start.24 = (bf16[1024,512]{1,0:T(8,128)(2,1)}, bf16[1024,512]{1,0:T(8,128)(2,1)}, u32[]{:S(2)}, u32[]{:S(2)}) collective-permute-start(bf16[1024,512]{1,0:T(8,128)(2,1)} %collective-permute-done.22.refs_21_), channel_id=1, source_target_pairs={{0,3},{1,0},{2,1},{3,2},{4,7},{5,4},{6,5},{7,6},{8,11},{9,8},{10,9... | collective-permute-start | bytes 3145736 | tf_op jit(solution)/shard_map/ppermute | solution.py:35
  108.4 13.9 %all-to-all-start.3 = ((bf16[16,32,256]{2,1,0:T(8,128)(2,1)}), bf16[16,32,256]{2,1,0:T(8,128)(2,1)S(1)}, u32[]{:S(2)}, u32[]{:S(2)}) async-start(bf16[16,32,256]{2,1,0:T(8,128)(2,1)} %broadcast_in_dim.15), calls=%async_computation.3 | async-start | bytes 524288 | tf_op jit(solution)/shard_map/all_to_all | solution.py:334
  113.3 9.3 %collective-permute-start.11 = (bf16[16,16,1024]{2,1,0:T(8,128)(2,1)}, bf16[16,16,1024]{2,1,0:T(8,128)(2,1)}, u32[]{:S(2)}, u32[]{:S(2)}) collective-permute-start(bf16[16,16,1024]{2,1,0:T(8,128)(2,1)} %collective-permute-done.4.refs_5_), channel_id=1, source_target_pairs={{0,16},{1,17},{2,18},{3,19},{4,20},{5,21},{6,22},{7,23},{8,24},{9,... | collective-permute-start | bytes 1572872 | tf_op jit(solution)/shard_map/ppermute | solution.py:35
  113.4 9.2 %collective-permute-start.14 = (bf16[16,16,1024]{2,1,0:T(8,128)(2,1)}, bf16[16,16,1024]{2,1,0:T(8,128)(2,1)}, u32[]{:S(2)}, u32[]{:S(2)}) collective-permute-start(bf16[16,16,1024]{2,1,0:T(8,128)(2,1)} %collective-permute-done.7.refs_8_), channel_id=1, source_target_pairs={{0,16},{1,17},{2,18},{3,19},{4,20},{5,21},{6,22},{7,23},{8,24},{9,... | collective-permute-start | bytes 1572872 | tf_op jit(solution)/shard_map/ppermute | solution.py:35
  113.9 8.8 %collective-permute-start.13 = (bf16[16,16,1024]{2,1,0:T(8,128)(2,1)}, bf16[16,16,1024]{2,1,0:T(8,128)(2,1)}, u32[]{:S(2)}, u32[]{:S(2)}) collective-permute-start(bf16[16,16,1024]{2,1,0:T(8,128)(2,1)} %collective-permute-done.6.refs_7_), channel_id=1, source_target_pairs={{0,16},{1,17},{2,18},{3,19},{4,20},{5,21},{6,22},{7,23},{8,24},{9,... | collective-permute-start | bytes 1572872 | tf_op jit(solution)/shard_map/ppermute | solution.py:35
  122.6 1.2 copy-start.1
  123.9 1.0 copy-start.3
  124.9 1.0 copy-start.5
  125.9 1.0 copy-start.7
  145.8 24.4 %copy-start.8 = (bf16[1024,1024]{1,0:T(8,128)(2,1)S(1)}, bf16[1024,1024]{1,0:T(8,128)(2,1)}, u32[]{:S(2)}) copy-start(bf16[1024,1024]{1,0:T(8,128)(2,1)} %get-tuple-element.20) | copy-start | bytes 6291460
  170.8 1.3 collective-permute-start.27
  186.1 1.3 collective-permute-start.29
  188.2 11.9 %all-to-all-start.7 = ((f32[16,24,128]{2,1,0:T(8,128)}), f32[16,24,128]{2,1,0:T(8,128)S(1)}, u32[]{:S(2)}, u32[]{:S(2)}) async-start(f32[16,24,128]{2,1,0:T(8,128)} %broadcast_in_dim.20), calls=%async_computation.7 | async-start | bytes 393216 | tf_op jit(solution)/shard_map/all_to_all | solution.py:211
  191.9 1.2 collective-permute-start.28
  (4 other events, 3.0 us)
